TPU v7x, 64 devices: a 2x2x8 block of a 4x4x8 slice. The times are simulated.
64 devices in a mesh: rep: 8 (over x, y, core), dp: 8 (over z).
Axes of the slice: x: 2, y: 2, z: 8, core: 2. Of those that a mesh axis runs over, the one named last changes fastest.
The devices are a block of a 4x4x8 slice.
Arguments:
- x: bfloat16 [64, 4096, 512], P(('rep', 'dp')), parts along dimension 0
- dy: bfloat16 [64, 4096, 512], P(('rep', 'dp')), parts along dimension 0
- w_gate: bfloat16 [2, 512, 1408], replicated
- w_up: bfloat16 [2, 512, 1408], replicated
- w_down: bfloat16 [2, 1408, 512], replicated
- m_w_gate: float32 [2, 512, 1408], P(None, 'dp')
- m_w_up: float32 [2, 512, 1408], P(None, 'dp')
- m_w_down: float32 [2, 1408, 512], P(None, 'dp')
- v_w_gate: float32 [2, 512, 1408], P(None, 'dp')
- v_w_up: float32 [2, 512, 1408], P(None, 'dp')
- v_w_down: float32 [2, 1408, 512], P(None, 'dp')
Outputs:
- output 1: bfloat16 [16, 512, 1408], P('rep'), parts along dimension 0
- output 2: bfloat16 [16, 512, 1408], P('rep'), parts along dimension 0
- output 3: bfloat16 [16, 1408, 512], P('rep'), parts along dimension 0
- output 4: float32 [16, 512, 1408], P('rep', 'dp'), parts along dimension 0
- output 5: float32 [16, 512, 1408], P('rep', 'dp'), parts along dimension 0
- output 6: float32 [16, 1408, 512], P('rep', 'dp'), parts along dimension 0
- output 7: float32 [16, 512, 1408], P('rep', 'dp'), parts along dimension 0
- output 8: float32 [16, 512, 1408], P('rep', 'dp'), parts along dimension 0
- output 9: float32 [16, 1408, 512], P('rep', 'dp'), parts along dimension 0
There are 8 independent parts. A program takes and returns all parts, laid end to end along the dimension named above; an argument that names none is the same for every part.
All inputs are finite; a program needn't handle non-finite values.
Results may differ from a plain program's by a relative error of at most 0.022.
Values are sent between devices in bfloat16 or wider.
A program may use at most 768 MiB of HBM per device.

v0:
```python
import jax
import jax.numpy as jnp
from jax import lax

NAMES = ("w_gate", "w_up", "w_down")


def matmul(a, w):
    return jnp.dot(a, w, preferred_element_type=jnp.float32).astype(jnp.bfloat16)


def normed(h):
    wide = h.astype(jnp.float32)
    scale = lax.rsqrt(jnp.mean(wide**2, -1, keepdims=True) + 1e-6)
    return (wide * scale).astype(jnp.bfloat16)


def layer(h, w):
    a = normed(h)
    gate = jnp.dot(a, w["w_gate"], preferred_element_type=jnp.float32)
    up = jnp.dot(a, w["w_up"], preferred_element_type=jnp.float32)
    return h + matmul((jax.nn.silu(gate) * up).astype(jnp.bfloat16), w["w_down"])


def adamw(w, m, v, g):
    m = 0.9 * m + 0.1 * g
    v = 0.95 * v + 0.05 * g * g
    step = m * lax.rsqrt(v + 1e-8) + 0.1 * w
    return (w - 0.02 * step).astype(jnp.bfloat16), m, v


def clipped(gradients, sum_of_squares, count):
    factor = jnp.minimum(1.0, 0.5 * lax.rsqrt(sum_of_squares / count + 1e-30))
    return [g * factor for g in gradients]


def stack(weights, h):
    for number in range(weights["w_gate"].shape[0]):
        h = layer(h, {name: w[number] for name, w in weights.items()})
    return h


def solution(mesh):
    groups = mesh.shape["rep"]

    def step(x, dy, *arrays):
        weights, m, v = (arrays[i : i + 3] for i in (0, 3, 6))
        x, dy = (t.reshape(groups, -1, *t.shape[1:]) for t in (x, dy))

        def of_a_group(x, dy):
            _, back = jax.vjp(lambda w: stack(w, x), dict(zip(NAMES, weights, strict=True)))
            by_weights = back(dy)[0]
            gradients = [by_weights[name].astype(jnp.float32) for name in NAMES]
            gradients = clipped(gradients, sum(jnp.sum(g * g) for g in gradients), sum(g.size for g in gradients))
            new = [adamw(w.astype(jnp.float32), m, v, g) for w, m, v, g in zip(weights, m, v, gradients, strict=True)]
            return tuple(one[which] for which in range(3) for one in new)

        return tuple(t.reshape(-1, *t.shape[2:]) for t in jax.vmap(of_a_group)(x, dy))

    return step
```

profile of v0, /device:TPU:22, one launch (start us, length us, event | category | flops | bytes accessed | tf_op | source)
XLA Modules:
  0.0 744.2 jit_solution(14218155638841947876)
XLA Ops:
  10.3 6.4 copy
  16.8 6.6 copy.1
  23.3 11.8 %fusion.168 = bf16[1,1,4096,1408]{3,2,1,0:T(8,128)(2,1)} fusion(bf16[1,4096,512]{2,1,0:T(8,128)(2,1)} %param.17, bf16[2,1408,512]{2,1,0:T(8,128)(2,1)S(1)} %copy-done.27), kind=kOutput, calls=%fused_computation.204 | convolution fusion | flops 5911347200 | bytes 17170432 | tf_op jit(solution)/vmap(transpose(jvp()))/dot_general | solution.py:9
  35.1 11.2 %fusion.210 = f32[4096,1408]{1,0:T(8,128)} fusion(bf16[1,4096,512]{2,1,0:T(8,128)(2,1)S(1)} %copy-done.7, f32[4096]{0:T(1024)S(1)} %add_rsqrt_fusion, bf16[2,512,1408]{2,1,0:T(8,128)(2,1)S(1)} %copy-done.29), kind=kOutput, calls=%fused_computation.235 | convolution fusion | flops 5911871488 | bytes 28721152 | tf_op jit(solution)/vmap(jvp())/dot_general | solution.py:20
  46.3 22.3 %fusion.164 = (bf16[1,1,4096,1408]{3,2,1,0:T(8,128)(2,1)}, f32[4096,1408]{1,0:T(8,128)}) fusion(f32[4096,1408]{1,0:T(8,128)} %fusion.210, bf16[2,512,1408]{2,1,0:T(8,128)(2,1)} %param.15, bf16[1,4096,512]{2,1,0:T(8,128)(2,1)S(1)} %copy-done.7, f32[4096]{0:T(1024)S(1)} %add_rsqrt_fusion), kind=kOutput, calls=%fused_computation.191 | convolution fusion | flops 5946474496 | bytes 63324160 | tf_op jit(solution)/vmap(jvp())/dot_general | solution.py:21
  68.5 15.0 %copy.4 = bf16[1,1,4096,1408]{2,3,1,0:T(8,128)(2,1)} copy(bf16[1,1,4096,1408]{3,2,1,0:T(8,128)(2,1)} %get-tuple-element.263) | data formatting | bytes 23068672
  83.6 12.7 %fusion.176 = (f32[4096]{0:T(1024)S(1)}, bf16[1,1,4096,512]{2,3,1,0:T(8,128)(2,1)S(1)}) fusion(bf16[2,1408,512]{2,1,0:T(8,128)(2,1)S(1)} %copy-done.27, bf16[1,1,4096,1408]{3,2,1,0:T(8,128)(2,1)} %get-tuple-element.263, bf16[1,4096,512]{1,2,0:T(8,128)(2,1)} %copy), kind=kOutput, calls=%fused_computation.215 | convolution fusion | flops 5916061696 | bytes 21381120 | tf_op jit(solution)/vmap(jvp())/dot_general | solution.py:9
  101.4 11.1 %fusion.205 = f32[4096,1408]{1,0:T(8,128)} fusion(bf16[1,1,4096,512]{2,3,1,0:T(8,128)(2,1)S(1)} %fusion.177, bf16[2,512,1408]{2,1,0:T(8,128)(2,1)S(1)} %copy-done.28), kind=kOutput, calls=%fused_computation.231 | convolution fusion | flops 5905580032 | bytes 28704768 | tf_op jit(solution)/vmap(jvp())/dot_general | solution.py:21
  112.5 34.9 %fusion.153 = (bf16[1,1,4096,1408]{3,2,1,0:T(8,128)(2,1)}, bf16[1,1,4096,1408]{3,2,1,0:T(8,128)(2,1)}, f32[4096,1408]{1,0:T(8,128)}) fusion(f32[4096,1408]{1,0:T(8,128)} %fusion.205, bf16[1,1,4096,1408]{3,2,1,0:T(8,128)(2,1)} %fusion.168, bf16[2,512,1408]{2,1,0:T(8,128)(2,1)} %param.12, bf16[1,1,4096,512]{2,3,1,0:T(8,128)(2,1)} %copy-done), kind=kOutput, calls=%fused_computation.175 | convolution fusion | flops 5992087552 | bytes 86376448 | tf_op jit(solution)/vmap(jvp())/dot_general | solution.py:20
  147.4 12.9 %fusion.182 = bf16[4096,512]{0,1:T(8,128)(2,1)} fusion(bf16[1,1,4096,1408]{3,2,1,0:T(8,128)(2,1)} %get-tuple-element.622, bf16[2,512,1408]{2,1,0:T(8,128)(2,1)} %param.15), kind=kOutput, calls=%fused_computation.220 | convolution fusion | flops 5905580032 | bytes 17170432 | tf_op jit(solution)/vmap(transpose(jvp()))/dot_general | solution.py:21
  160.3 10.8 %fusion.178 = (f32[4096]{0:T(1024)S(1)}, bf16[1,1,4096,512]{2,3,1,0:T(8,128)(2,1)}) fusion(bf16[1,1,4096,512]{2,3,1,0:T(8,128)(2,1)S(1)} %copy-done.9, bf16[4096,512]{0,1:T(8,128)(2,1)} %fusion.182, bf16[2,512,1408]{2,1,0:T(8,128)(2,1)} %param.12, bf16[1,1,4096,1408]{3,2,1,0:T(8,128)(2,1)S(1)} %copy-done.1), kind=kOutput, calls=%fused_computation.217 | convolution fusion | flops 5916061696 | bytes 25575424 | tf_op jit(solution)/vmap(transpose(jvp()))/dot_general | solution.py:20
  171.2 6.1 fusion.200
  177.3 6.5 copy.5
  183.8 50.3 %while.17 = (bf16[1,1,4096,1408]{2,3,1,0:T(8,128)(2,1)}, bf16[1,1,4096,512]{3,2,1,0:T(8,128)(2,1)}, f32[1,176,512]{2,1,0:T(8,128)S(1)}, f32[1,176,512]{2,1,0:T(8...) while((bf16[1,1,4096,1408]{2,3,1,0:T(8,128)(2,1)}, ...), condition=%wide.windowed_dot_general_cond_rs.5.clone, body=%wide.windowed_dot_general_body_rs.5.clone.sunk | while | flops 2964865024 | bytes 107348640 | solution.py:9
  186.1 5.3 collective-permute-start.21
  204.8 6.0 collective-permute-done.22
  218.7 4.9 fusion.361
  234.1 19.7 %fusion.163 = bf16[1,1,4096,1408]{3,2,1,0:T(8,128)(2,1)} fusion(f32[4096,1408]{1,0:T(8,128)} %fusion.205, f32[4096,1408]{1,0:T(8,128)} %get-tuple-element.267), kind=kLoop, calls=%fused_computation.189 | loop fusion | flops 34603008 | bytes 57671680 | tf_op jit(solution)/vmap(jvp())/convert_element_type | solution.py:22
  253.8 15.1 %copy.2 = bf16[1,1,4096,1408]{2,3,1,0:T(8,128)(2,1)} copy(bf16[1,1,4096,1408]{3,2,1,0:T(8,128)(2,1)} %fusion.163) | data formatting | bytes 23068672
  268.9 6.5 copy.3
  275.4 44.0 %while.16 = (bf16[1,1,4096,1408]{2,3,1,0:T(8,128)(2,1)}, bf16[1,1,4096,512]{3,2,1,0:T(8,128)(2,1)}, f32[1,176,512]{2,1,0:T(8,128)S(1)}, f32[1,176,512]{2,1,0:T(8...) while((bf16[1,1,4096,1408]{2,3,1,0:T(8,128)(2,1)}, ...), condition=%wide.windowed_dot_general_cond_rs.4.clone, body=%wide.windowed_dot_general_body_rs.4.clone.sunk | while | flops 2964865024 | bytes 107348640 | solution.py:9
  313.1 5.4 collective-permute-done.18
  319.4 5.4 multiply_convert_fusion
  324.8 28.8 %convert_multiply_fusion = (bf16[1,1,4096,1408]{3,2,1,0:T(8,128)(2,1)}, bf16[1,1,4096,1408]{3,2,1,0:T(8,128)(2,1)}) fusion(f32[4096,1408]{1,0:T(8,128)} %fusion.210, f32[4096,1408]{1,0:T(8,128)} %get-tuple-element.264, bf16[2,1408,512]{2,1,0:T(8,128)(2,1)} %param.16, bf16[1,1,4096,512]{2,3,1,0:T(8,128)(2,1)} %fusion.200), kind=kOutput, calls=%fused_computation.170 | convolution fusion | flops 5997854720 | bytes 74842112 | tf_op jit(solution)/vmap(transpose(jvp()))/dot_general | solution.py:9
  353.6 51.6 %while.15 = (bf16[1,1,4096,512]{2,3,1,0:T(8,128)(2,1)}, bf16[1,1,4096,1408]{3,2,1,0:T(8,128)(2,1)}, f32[1,64,1408]{2,1,0:T(8,128)S(1)}, f32[1,64,1408]{2,1,0:T(8...) while((bf16[1,1,4096,512]{2,3,1,0:T(8,128)(2,1)}, ...), condition=%wide.windowed_dot_general_cond_rs.3.clone, body=%wide.windowed_dot_general_body_rs.3.clone.sunk | while | flops 2957524992 | bytes 44434020 | solution.py:21
  359.0 6.4 fusion.345
  369.5 6.4 fusion.347
  384.6 6.4 fusion.345
  395.3 6.4 fusion.347
  405.9 58.4 %while.14 = (bf16[1,1,4096,512]{2,3,1,0:T(8,128)(2,1)}, bf16[1,1,4096,1408]{3,2,1,0:T(8,128)(2,1)}, f32[1,64,1408]{2,1,0:T(8,128)S(1)}, f32[1,64,1408]{2,1,0:T(8...) while((bf16[1,1,4096,512]{2,3,1,0:T(8,128)(2,1)}, ...), condition=%wide.windowed_dot_general_cond_rs.2.clone, body=%wide.windowed_dot_general_body_rs.2.clone.sunk | while | flops 2957524992 | bytes 45875840 | solution.py:21
  411.5 6.4 fusion.337
  426.6 6.4 fusion.339
  442.5 6.4 fusion.337
  454.7 6.4 fusion.339
  465.1 48.8 %while.13 = (bf16[1,1,4096,512]{2,3,1,0:T(8,128)(2,1)}, bf16[1,1,4096,1408]{3,2,1,0:T(8,128)(2,1)}, f32[1,64,1408]{2,1,0:T(8,128)S(1)}, f32[1,64,1408]{2,1,0:T(8...) while((bf16[1,1,4096,512]{2,3,1,0:T(8,128)(2,1)}, ...), condition=%wide.windowed_dot_general_cond_rs.1.clone, body=%wide.windowed_dot_general_body_rs.1.clone.sunk | while | flops 2957524992 | bytes 44434020 | solution.py:20
  470.4 6.4 fusion.329
  481.9 6.4 fusion.331
  494.9 6.4 fusion.329
  506.4 6.4 fusion.331
  514.6 56.0 %while.12 = (bf16[1,1,4096,512]{2,3,1,0:T(8,128)(2,1)}, bf16[1,1,4096,1408]{3,2,1,0:T(8,128)(2,1)}, f32[1,64,1408]{2,1,0:T(8,128)S(1)}, f32[1,64,1408]{2,1,0:T(8...) while((bf16[1,1,4096,512]{2,3,1,0:T(8,128)(2,1)}, ...), condition=%wide.windowed_dot_general_cond_rs.clone, body=%wide.windowed_dot_general_body_rs.clone.sunk | while | flops 2957524992 | bytes 45875840 | solution.py:20
  520.9 6.4 fusion.321
  533.0 6.4 fusion.323
  547.4 6.4 fusion.321
  559.5 6.4 fusion.323
  590.1 15.3 %all-reduce.10 = f32[1]{0:T(128)} all-reduce(f32[1]{0:T(128)} %bitcast.39), channel_id=13, replica_groups=mesh['rep'=8,'dp'=8] {'dp'}, use_global_device_ids=true, to_apply=%region_3.4.clone | all-reduce | flops 1 | bytes 8 | tf_op jit(solution)/vmap()/reduce_sum | solution.py:54
  615.2 33.7 %all-gather.14.cloned.1.call-done = bf16[1,2,1408,512]{3,2,1,0:T(8,128)(2,1)} async-done(((bf16[1,2,176,512]{3,2,1,0:T(8,128)(2,1)}), bf16[1,2,1408,512]{3,2,1,0:T(8,128)(2,1)}) %all-gather.14.cloned.1.call-update) | async-done | bytes 2883600 | tf_op jit(solution)/reshape | solution.py:58
  648.9 40.7 %all-gather.12.cloned.1.call-done = bf16[1,2,512,1408]{3,2,1,0:T(8,128)(2,1)} async-done(((bf16[1,2,64,1408]{3,2,1,0:T(8,128)(2,1)}), bf16[1,2,512,1408]{3,2,1,0:T(8,128)(2,1)}) %all-gather.12.cloned.1.call-update) | async-done | bytes 2883600 | tf_op jit(solution)/reshape | solution.py:58
  689.6 40.7 %all-gather.10.cloned.1.call-done = bf16[1,2,512,1408]{3,2,1,0:T(8,128)(2,1)} async-done(((bf16[1,2,64,1408]{3,2,1,0:T(8,128)(2,1)}), bf16[1,2,512,1408]{3,2,1,0:T(8,128)(2,1)}) %all-gather.10.cloned.1.call-update) | async-done | bytes 2883600 | tf_op jit(solution)/reshape | solution.py:58
  (286 shorter events, 203.3 us)
Async XLA Ops:
  7.2 641.7 %all-gather.14.cloned.1.call-start = ((), (), s32[]{:S(2)}) async-start(), calls=%async_computation.2 | async-start | bytes 3244032 | tf_op jit(solution)/reshape | solution.py:58
  183.9 15.9 %collective-permute-start.20 = (f32[1,176,512]{2,1,0:T(8,128)S(1)}, f32[1,176,512]{2,1,0:T(8,128)S(1)}, u32[]{:S(2)}, u32[]{:S(2)}) collective-permute-start(f32[1,176,512]{2,1,0:T(8,128)S(1)} %broadcast_select_fusion.34), channel_id=35, source_target_pairs={{0,1},{1,2},{2,3},{3,4},{4,5},{5,6},{6,7},{7,0},{8,9},{9,10},{10,1... | collective-permute-start | bytes 1081352 | tf_op jit(solution)/vmap(transpose(jvp()))/dot_general | solution.py:9
  186.1 13.6 %collective-permute-start.21 = (f32[1,176,512]{2,1,0:T(8,128)S(1)}, f32[1,176,512]{2,1,0:T(8,128)S(1)}, u32[]{:S(2)}, u32[]{:S(2)}) collective-permute-start(f32[1,176,512]{2,1,0:T(8,128)S(1)} %broadcast_select_fusion.35), channel_id=34, source_target_pairs={{0,7},{1,0},{2,1},{3,2},{4,3},{5,4},{6,5},{7,6},{8,15},{9,8},{10,9... | collective-permute-start | bytes 1081352 | tf_op jit(solution)/vmap(transpose(jvp()))/dot_general | solution.py:9
  199.9 11.0 %collective-permute-start.22 = (f32[1,176,512]{2,1,0:T(8,128)S(1)}, f32[1,176,512]{2,1,0:T(8,128)S(1)}, u32[]{:S(2)}, u32[]{:S(2)}) collective-permute-start(f32[1,176,512]{2,1,0:T(8,128)S(1)} %get-tuple-element.500), channel_id=37, source_target_pairs={{0,1},{1,2},{2,3},{3,4},{4,5},{5,6},{6,7},{7,0},{8,9},{9,10},{10,1... | collective-permute-start | bytes 1081352 | tf_op jit(solution)/vmap(transpose(jvp()))/dot_general | solution.py:9
  200.0 10.8 %collective-permute-start.23 = (f32[1,176,512]{2,1,0:T(8,128)S(1)}, f32[1,176,512]{2,1,0:T(8,128)S(1)}, u32[]{:S(2)}, u32[]{:S(2)}) collective-permute-start(f32[1,176,512]{2,1,0:T(8,128)S(1)} %get-tuple-element.501), channel_id=36, source_target_pairs={{0,7},{1,0},{2,1},{3,2},{4,3},{5,4},{6,5},{7,6},{8,15},{9,8},{10,9... | collective-permute-start | bytes 1081352 | tf_op jit(solution)/vmap(transpose(jvp()))/dot_general | solution.py:9
  212.7 10.9 %collective-permute-start.20 = (f32[1,176,512]{2,1,0:T(8,128)S(1)}, f32[1,176,512]{2,1,0:T(8,128)S(1)}, u32[]{:S(2)}, u32[]{:S(2)}) collective-permute-start(f32[1,176,512]{2,1,0:T(8,128)S(1)} %broadcast_select_fusion.34), channel_id=35, source_target_pairs={{0,1},{1,2},{2,3},{3,4},{4,5},{5,6},{6,7},{7,0},{8,9},{9,10},{10,1... | collective-permute-start | bytes 1081352 | tf_op jit(solution)/vmap(transpose(jvp()))/dot_general | solution.py:9
  234.1 338.0 %collective-permute-start.29 = (f32[1,176,512]{2,1,0:T(8,128)}, f32[1,176,512]{2,1,0:T(8,128)}, u32[]{:S(2)}, u32[]{:S(2)}) collective-permute-start(f32[1,176,512]{2,1,0:T(8,128)} %get-tuple-element.47), channel_id=38, source_target_pairs={{0,1},{1,2},{2,3},{3,4},{4,5},{5,6},{6,7},{7,0},{8,9},{9,10},{10,1... | collective-permute-start | bytes 1081352 | tf_op jit(solution)/vmap(transpose(jvp()))/dot_general | solution.py:9
  275.4 10.9 %collective-permute-start.16 = (f32[1,176,512]{2,1,0:T(8,128)S(1)}, f32[1,176,512]{2,1,0:T(8,128)S(1)}, u32[]{:S(2)}, u32[]{:S(2)}) collective-permute-start(f32[1,176,512]{2,1,0:T(8,128)S(1)} %broadcast_select_fusion.32), channel_id=29, source_target_pairs={{0,1},{1,2},{2,3},{3,4},{4,5},{5,6},{6,7},{7,0},{8,9},{9,10},{10,1... | collective-permute-start | bytes 1081352 | tf_op jit(solution)/vmap(transpose(jvp()))/dot_general | solution.py:9
  297.1 10.9 %collective-permute-start.16 = (f32[1,176,512]{2,1,0:T(8,128)S(1)}, f32[1,176,512]{2,1,0:T(8,128)S(1)}, u32[]{:S(2)}, u32[]{:S(2)}) collective-permute-start(f32[1,176,512]{2,1,0:T(8,128)S(1)} %broadcast_select_fusion.32), channel_id=29, source_target_pairs={{0,1},{1,2},{2,3},{3,4},{4,5},{5,6},{6,7},{7,0},{8,9},{9,10},{10,1... | collective-permute-start | bytes 1081352 | tf_op jit(solution)/vmap(transpose(jvp()))/dot_general | solution.py:9
  308.1 10.4 %collective-permute-start.18 = (f32[1,176,512]{2,1,0:T(8,128)S(1)}, f32[1,176,512]{2,1,0:T(8,128)S(1)}, u32[]{:S(2)}, u32[]{:S(2)}) collective-permute-start(f32[1,176,512]{2,1,0:T(8,128)S(1)} %get-tuple-element.491), channel_id=31, source_target_pairs={{0,1},{1,2},{2,3},{3,4},{4,5},{5,6},{6,7},{7,0},{8,9},{9,10},{10,1... | collective-permute-start | bytes 1081352 | tf_op jit(solution)/vmap(transpose(jvp()))/dot_general | solution.py:9
  319.4 254.9 %collective-permute-start.28 = (f32[1,176,512]{2,1,0:T(8,128)}, f32[1,176,512]{2,1,0:T(8,128)}, u32[]{:S(2)}, u32[]{:S(2)}) collective-permute-start(f32[1,176,512]{2,1,0:T(8,128)} %get-tuple-element.45), channel_id=32, source_target_pairs={{0,1},{1,2},{2,3},{3,4},{4,5},{5,6},{6,7},{7,0},{8,9},{9,10},{10,1... | collective-permute-start | bytes 1081352 | tf_op jit(solution)/vmap(transpose(jvp()))/dot_general | solution.py:9
  353.6 12.4 %collective-permute-start.12 = (f32[1,64,1408]{2,1,0:T(8,128)S(1)}, f32[1,64,1408]{2,1,0:T(8,128)S(1)}, u32[]{:S(2)}, u32[]{:S(2)}) collective-permute-start(f32[1,64,1408]{2,1,0:T(8,128)S(1)} %broadcast_select_fusion.30), channel_id=22, source_target_pairs={{0,1},{1,2},{2,3},{3,4},{4,5},{5,6},{6,7},{7,0},{8,9},{9,10},{10,1... | collective-permute-start | bytes 1081352 | tf_op jit(solution)/vmap(transpose(jvp()))/dot_general | solution.py:21
  355.1 11.0 %collective-permute-start.13 = (f32[1,64,1408]{2,1,0:T(8,128)S(1)}, f32[1,64,1408]{2,1,0:T(8,128)S(1)}, u32[]{:S(2)}, u32[]{:S(2)}) collective-permute-start(f32[1,64,1408]{2,1,0:T(8,128)S(1)} %broadcast_select_fusion.31), channel_id=21, source_target_pairs={{0,7},{1,0},{2,1},{3,2},{4,3},{5,4},{6,5},{7,6},{8,15},{9,8},{10,9... | collective-permute-start | bytes 1081352 | tf_op jit(solution)/vmap(transpose(jvp()))/dot_general | solution.py:21
  366.2 10.9 %collective-permute-start.14 = (f32[1,64,1408]{2,1,0:T(8,128)S(1)}, f32[1,64,1408]{2,1,0:T(8,128)S(1)}, u32[]{:S(2)}, u32[]{:S(2)}) collective-permute-start(f32[1,64,1408]{2,1,0:T(8,128)S(1)} %get-tuple-element.482), channel_id=24, source_target_pairs={{0,1},{1,2},{2,3},{3,4},{4,5},{5,6},{6,7},{7,0},{8,9},{9,10},{10,1... | collective-permute-start | bytes 1081352 | tf_op jit(solution)/vmap(transpose(jvp()))/dot_general | solution.py:21
  366.4 11.0 %collective-permute-start.15 = (f32[1,64,1408]{2,1,0:T(8,128)S(1)}, f32[1,64,1408]{2,1,0:T(8,128)S(1)}, u32[]{:S(2)}, u32[]{:S(2)}) collective-permute-start(f32[1,64,1408]{2,1,0:T(8,128)S(1)} %get-tuple-element.483), channel_id=23, source_target_pairs={{0,7},{1,0},{2,1},{3,2},{4,3},{5,4},{6,5},{7,6},{8,15},{9,8},{10,9... | collective-permute-start | bytes 1081352 | tf_op jit(solution)/vmap(transpose(jvp()))/dot_general | solution.py:21
  379.2 12.4 %collective-permute-start.12 = (f32[1,64,1408]{2,1,0:T(8,128)S(1)}, f32[1,64,1408]{2,1,0:T(8,128)S(1)}, u32[]{:S(2)}, u32[]{:S(2)}) collective-permute-start(f32[1,64,1408]{2,1,0:T(8,128)S(1)} %broadcast_select_fusion.30), channel_id=22, source_target_pairs={{0,1},{1,2},{2,3},{3,4},{4,5},{5,6},{6,7},{7,0},{8,9},{9,10},{10,1... | collective-permute-start | bytes 1081352 | tf_op jit(solution)/vmap(transpose(jvp()))/dot_general | solution.py:21
  381.7 10.0 %collective-permute-start.13 = (f32[1,64,1408]{2,1,0:T(8,128)S(1)}, f32[1,64,1408]{2,1,0:T(8,128)S(1)}, u32[]{:S(2)}, u32[]{:S(2)}) collective-permute-start(f32[1,64,1408]{2,1,0:T(8,128)S(1)} %broadcast_select_fusion.31), channel_id=21, source_target_pairs={{0,7},{1,0},{2,1},{3,2},{4,3},{5,4},{6,5},{7,6},{8,15},{9,8},{10,9... | collective-permute-start | bytes 1081352 | tf_op jit(solution)/vmap(transpose(jvp()))/dot_general | solution.py:21
  391.8 12.6 %collective-permute-start.14 = (f32[1,64,1408]{2,1,0:T(8,128)S(1)}, f32[1,64,1408]{2,1,0:T(8,128)S(1)}, u32[]{:S(2)}, u32[]{:S(2)}) collective-permute-start(f32[1,64,1408]{2,1,0:T(8,128)S(1)} %get-tuple-element.482), channel_id=24, source_target_pairs={{0,1},{1,2},{2,3},{3,4},{4,5},{5,6},{6,7},{7,0},{8,9},{9,10},{10,1... | collective-permute-start | bytes 1081352 | tf_op jit(solution)/vmap(transpose(jvp()))/dot_general | solution.py:21
  393.0 11.4 %collective-permute-start.15 = (f32[1,64,1408]{2,1,0:T(8,128)S(1)}, f32[1,64,1408]{2,1,0:T(8,128)S(1)}, u32[]{:S(2)}, u32[]{:S(2)}) collective-permute-start(f32[1,64,1408]{2,1,0:T(8,128)S(1)} %get-tuple-element.483), channel_id=23, source_target_pairs={{0,7},{1,0},{2,1},{3,2},{4,3},{5,4},{6,5},{7,6},{8,15},{9,8},{10,9... | collective-permute-start | bytes 1081352 | tf_op jit(solution)/vmap(transpose(jvp()))/dot_general | solution.py:21
  405.2 171.0 %collective-permute-start.27 = (f32[1,64,1408]{2,1,0:T(8,128)}, f32[1,64,1408]{2,1,0:T(8,128)}, u32[]{:S(2)}, u32[]{:S(2)}) collective-permute-start(f32[1,64,1408]{2,1,0:T(8,128)} %get-tuple-element.43), channel_id=25, source_target_pairs={{0,1},{1,2},{2,3},{3,4},{4,5},{5,6},{6,7},{7,0},{8,9},{9,10},{10,1... | collective-permute-start | bytes 1081352 | tf_op jit(solution)/vmap(transpose(jvp()))/dot_general | solution.py:21
  406.2 15.4 %collective-permute-start.8 = (f32[1,64,1408]{2,1,0:T(8,128)S(1)}, f32[1,64,1408]{2,1,0:T(8,128)}, u32[]{:S(2)}, u32[]{:S(2)}) collective-permute-start(f32[1,64,1408]{2,1,0:T(8,128)S(1)} %broadcast_select_fusion.28), channel_id=16, source_target_pairs={{0,1},{1,2},{2,3},{3,4},{4,5},{5,6},{6,7},{7,0},{8,9},{9,10},{10,1... | collective-permute-start | bytes 1081352 | tf_op jit(solution)/vmap(transpose(jvp()))/dot_general | solution.py:21
  409.3 12.2 %collective-permute-start.9 = (f32[1,64,1408]{2,1,0:T(8,128)S(1)}, f32[1,64,1408]{2,1,0:T(8,128)S(1)}, u32[]{:S(2)}, u32[]{:S(2)}) collective-permute-start(f32[1,64,1408]{2,1,0:T(8,128)S(1)} %broadcast_select_fusion.29), channel_id=15, source_target_pairs={{0,7},{1,0},{2,1},{3,2},{4,3},{5,4},{6,5},{7,6},{8,15},{9,8},{10,9... | collective-permute-start | bytes 1081352 | tf_op jit(solution)/vmap(transpose(jvp()))/dot_general | solution.py:21
  423.3 11.9 %collective-permute-start.10 = (f32[1,64,1408]{2,1,0:T(8,128)}, f32[1,64,1408]{2,1,0:T(8,128)S(1)}, u32[]{:S(2)}, u32[]{:S(2)}) collective-permute-start(f32[1,64,1408]{2,1,0:T(8,128)} %get-tuple-element.473), channel_id=18, source_target_pairs={{0,1},{1,2},{2,3},{3,4},{4,5},{5,6},{6,7},{7,0},{8,9},{9,10},{10,1... | collective-permute-start | bytes 1081352 | tf_op jit(solution)/vmap(transpose(jvp()))/dot_general | solution.py:21
  423.4 12.6 %collective-permute-start.11 = (f32[1,64,1408]{2,1,0:T(8,128)S(1)}, f32[1,64,1408]{2,1,0:T(8,128)}, u32[]{:S(2)}, u32[]{:S(2)}) collective-permute-start(f32[1,64,1408]{2,1,0:T(8,128)S(1)} %get-tuple-element.474), channel_id=17, source_target_pairs={{0,7},{1,0},{2,1},{3,2},{4,3},{5,4},{6,5},{7,6},{8,15},{9,8},{10,9... | collective-permute-start | bytes 1081352 | tf_op jit(solution)/vmap(transpose(jvp()))/dot_general | solution.py:21
  437.2 12.4 %collective-permute-start.8 = (f32[1,64,1408]{2,1,0:T(8,128)S(1)}, f32[1,64,1408]{2,1,0:T(8,128)}, u32[]{:S(2)}, u32[]{:S(2)}) collective-permute-start(f32[1,64,1408]{2,1,0:T(8,128)S(1)} %broadcast_select_fusion.28), channel_id=16, source_target_pairs={{0,1},{1,2},{2,3},{3,4},{4,5},{5,6},{6,7},{7,0},{8,9},{9,10},{10,1... | collective-permute-start | bytes 1081352 | tf_op jit(solution)/vmap(transpose(jvp()))/dot_general | solution.py:21
  437.3 12.3 %collective-permute-start.9 = (f32[1,64,1408]{2,1,0:T(8,128)S(1)}, f32[1,64,1408]{2,1,0:T(8,128)S(1)}, u32[]{:S(2)}, u32[]{:S(2)}) collective-permute-start(f32[1,64,1408]{2,1,0:T(8,128)S(1)} %broadcast_select_fusion.29), channel_id=15, source_target_pairs={{0,7},{1,0},{2,1},{3,2},{4,3},{5,4},{6,5},{7,6},{8,15},{9,8},{10,9... | collective-permute-start | bytes 1081352 | tf_op jit(solution)/vmap(transpose(jvp()))/dot_general | solution.py:21
  451.4 11.0 %collective-permute-start.10 = (f32[1,64,1408]{2,1,0:T(8,128)}, f32[1,64,1408]{2,1,0:T(8,128)S(1)}, u32[]{:S(2)}, u32[]{:S(2)}) collective-permute-start(f32[1,64,1408]{2,1,0:T(8,128)} %get-tuple-element.473), channel_id=18, source_target_pairs={{0,1},{1,2},{2,3},{3,4},{4,5},{5,6},{6,7},{7,0},{8,9},{9,10},{10,1... | collective-permute-start | bytes 1081352 | tf_op jit(solution)/vmap(transpose(jvp()))/dot_general | solution.py:21
  451.4 11.7 %collective-permute-start.11 = (f32[1,64,1408]{2,1,0:T(8,128)S(1)}, f32[1,64,1408]{2,1,0:T(8,128)}, u32[]{:S(2)}, u32[]{:S(2)}) collective-permute-start(f32[1,64,1408]{2,1,0:T(8,128)S(1)} %get-tuple-element.474), channel_id=17, source_target_pairs={{0,7},{1,0},{2,1},{3,2},{4,3},{5,4},{6,5},{7,6},{8,15},{9,8},{10,9... | collective-permute-start | bytes 1081352 | tf_op jit(solution)/vmap(transpose(jvp()))/dot_general | solution.py:21
  465.1 12.4 %collective-permute-start.4 = (f32[1,64,1408]{2,1,0:T(8,128)S(1)}, f32[1,64,1408]{2,1,0:T(8,128)}, u32[]{:S(2)}, u32[]{:S(2)}) collective-permute-start(f32[1,64,1408]{2,1,0:T(8,128)S(1)} %broadcast_select_fusion.26), channel_id=9, source_target_pairs={{0,1},{1,2},{2,3},{3,4},{4,5},{5,6},{6,7},{7,0},{8,9},{9,10},{10,1... | collective-permute-start | bytes 1081352 | tf_op jit(solution)/vmap(transpose(jvp()))/dot_general | solution.py:20
  465.2 12.3 %collective-permute-start.5 = (f32[1,64,1408]{2,1,0:T(8,128)S(1)}, f32[1,64,1408]{2,1,0:T(8,128)S(1)}, u32[]{:S(2)}, u32[]{:S(2)}) collective-permute-start(f32[1,64,1408]{2,1,0:T(8,128)S(1)} %broadcast_select_fusion.27), channel_id=8, source_target_pairs={{0,7},{1,0},{2,1},{3,2},{4,3},{5,4},{6,5},{7,6},{8,15},{9,8},{10,9... | collective-permute-start | bytes 1081352 | tf_op jit(solution)/vmap(transpose(jvp()))/dot_general | solution.py:20
  478.6 9.8 %collective-permute-start.6 = (f32[1,64,1408]{2,1,0:T(8,128)S(1)}, f32[1,64,1408]{2,1,0:T(8,128)S(1)}, u32[]{:S(2)}, u32[]{:S(2)}) collective-permute-start(f32[1,64,1408]{2,1,0:T(8,128)S(1)} %get-tuple-element.464), channel_id=11, source_target_pairs={{0,1},{1,2},{2,3},{3,4},{4,5},{5,6},{6,7},{7,0},{8,9},{9,10},{10,1... | collective-permute-start | bytes 1081352 | tf_op jit(solution)/vmap(transpose(jvp()))/dot_general | solution.py:20
  478.7 9.7 %collective-permute-start.7 = (f32[1,64,1408]{2,1,0:T(8,128)S(1)}, f32[1,64,1408]{2,1,0:T(8,128)}, u32[]{:S(2)}, u32[]{:S(2)}) collective-permute-start(f32[1,64,1408]{2,1,0:T(8,128)S(1)} %get-tuple-element.465), channel_id=10, source_target_pairs={{0,7},{1,0},{2,1},{3,2},{4,3},{5,4},{6,5},{7,6},{8,15},{9,8},{10,9... | collective-permute-start | bytes 1081352 | tf_op jit(solution)/vmap(transpose(jvp()))/dot_general | solution.py:20
  489.5 12.4 %collective-permute-start.4 = (f32[1,64,1408]{2,1,0:T(8,128)S(1)}, f32[1,64,1408]{2,1,0:T(8,128)}, u32[]{:S(2)}, u32[]{:S(2)}) collective-permute-start(f32[1,64,1408]{2,1,0:T(8,128)S(1)} %broadcast_select_fusion.26), channel_id=9, source_target_pairs={{0,1},{1,2},{2,3},{3,4},{4,5},{5,6},{6,7},{7,0},{8,9},{9,10},{10,1... | collective-permute-start | bytes 1081352 | tf_op jit(solution)/vmap(transpose(jvp()))/dot_general | solution.py:20
  489.7 12.3 %collective-permute-start.5 = (f32[1,64,1408]{2,1,0:T(8,128)S(1)}, f32[1,64,1408]{2,1,0:T(8,128)S(1)}, u32[]{:S(2)}, u32[]{:S(2)}) collective-permute-start(f32[1,64,1408]{2,1,0:T(8,128)S(1)} %broadcast_select_fusion.27), channel_id=8, source_target_pairs={{0,7},{1,0},{2,1},{3,2},{4,3},{5,4},{6,5},{7,6},{8,15},{9,8},{10,9... | collective-permute-start | bytes 1081352 | tf_op jit(solution)/vmap(transpose(jvp()))/dot_general | solution.py:20
  503.0 9.8 %collective-permute-start.6 = (f32[1,64,1408]{2,1,0:T(8,128)S(1)}, f32[1,64,1408]{2,1,0:T(8,128)S(1)}, u32[]{:S(2)}, u32[]{:S(2)}) collective-permute-start(f32[1,64,1408]{2,1,0:T(8,128)S(1)} %get-tuple-element.464), channel_id=11, source_target_pairs={{0,1},{1,2},{2,3},{3,4},{4,5},{5,6},{6,7},{7,0},{8,9},{9,10},{10,1... | collective-permute-start | bytes 1081352 | tf_op jit(solution)/vmap(transpose(jvp()))/dot_general | solution.py:20
  503.2 9.7 %collective-permute-start.7 = (f32[1,64,1408]{2,1,0:T(8,128)S(1)}, f32[1,64,1408]{2,1,0:T(8,128)}, u32[]{:S(2)}, u32[]{:S(2)}) collective-permute-start(f32[1,64,1408]{2,1,0:T(8,128)S(1)} %get-tuple-element.465), channel_id=10, source_target_pairs={{0,7},{1,0},{2,1},{3,2},{4,3},{5,4},{6,5},{7,6},{8,15},{9,8},{10,9... | collective-permute-start | bytes 1081352 | tf_op jit(solution)/vmap(transpose(jvp()))/dot_general | solution.py:20
  515.6 12.3 %collective-permute-start = (f32[1,64,1408]{2,1,0:T(8,128)}, f32[1,64,1408]{2,1,0:T(8,128)}, u32[]{:S(2)}, u32[]{:S(2)}) collective-permute-start(f32[1,64,1408]{2,1,0:T(8,128)} %broadcast_select_fusion.24), channel_id=3, source_target_pairs={{0,1},{1,2},{2,3},{3,4},{4,5},{5,6},{6,7},{7,0},{8,9},{9,10},{10,1... | collective-permute-start | bytes 1081352 | tf_op jit(solution)/vmap(transpose(jvp()))/dot_general | solution.py:20
  515.7 12.3 %collective-permute-start.1 = (f32[1,64,1408]{2,1,0:T(8,128)S(1)}, f32[1,64,1408]{2,1,0:T(8,128)S(1)}, u32[]{:S(2)}, u32[]{:S(2)}) collective-permute-start(f32[1,64,1408]{2,1,0:T(8,128)S(1)} %broadcast_select_fusion.25), channel_id=2, source_target_pairs={{0,7},{1,0},{2,1},{3,2},{4,3},{5,4},{6,5},{7,6},{8,15},{9,8},{10,9... | collective-permute-start | bytes 1081352 | tf_op jit(solution)/vmap(transpose(jvp()))/dot_general | solution.py:20
  529.8 9.7 %collective-permute-start.2 = (f32[1,64,1408]{2,1,0:T(8,128)}, f32[1,64,1408]{2,1,0:T(8,128)S(1)}, u32[]{:S(2)}, u32[]{:S(2)}) collective-permute-start(f32[1,64,1408]{2,1,0:T(8,128)} %get-tuple-element.455), channel_id=5, source_target_pairs={{0,1},{1,2},{2,3},{3,4},{4,5},{5,6},{6,7},{7,0},{8,9},{9,10},{10,1... | collective-permute-start | bytes 1081352 | tf_op jit(solution)/vmap(transpose(jvp()))/dot_general | solution.py:20
  529.8 10.4 %collective-permute-start.3 = (f32[1,64,1408]{2,1,0:T(8,128)S(1)}, f32[1,64,1408]{2,1,0:T(8,128)}, u32[]{:S(2)}, u32[]{:S(2)}) collective-permute-start(f32[1,64,1408]{2,1,0:T(8,128)S(1)} %get-tuple-element.456), channel_id=4, source_target_pairs={{0,7},{1,0},{2,1},{3,2},{4,3},{5,4},{6,5},{7,6},{8,15},{9,8},{10,9... | collective-permute-start | bytes 1081352 | tf_op jit(solution)/vmap(transpose(jvp()))/dot_general | solution.py:20
  542.2 12.3 %collective-permute-start = (f32[1,64,1408]{2,1,0:T(8,128)}, f32[1,64,1408]{2,1,0:T(8,128)}, u32[]{:S(2)}, u32[]{:S(2)}) collective-permute-start(f32[1,64,1408]{2,1,0:T(8,128)} %broadcast_select_fusion.24), channel_id=3, source_target_pairs={{0,1},{1,2},{2,3},{3,4},{4,5},{5,6},{6,7},{7,0},{8,9},{9,10},{10,1... | collective-permute-start | bytes 1081352 | tf_op jit(solution)/vmap(transpose(jvp()))/dot_general | solution.py:20
  542.2 12.3 %collective-permute-start.1 = (f32[1,64,1408]{2,1,0:T(8,128)S(1)}, f32[1,64,1408]{2,1,0:T(8,128)S(1)}, u32[]{:S(2)}, u32[]{:S(2)}) collective-permute-start(f32[1,64,1408]{2,1,0:T(8,128)S(1)} %broadcast_select_fusion.25), channel_id=2, source_target_pairs={{0,7},{1,0},{2,1},{3,2},{4,3},{5,4},{6,5},{7,6},{8,15},{9,8},{10,9... | collective-permute-start | bytes 1081352 | tf_op jit(solution)/vmap(transpose(jvp()))/dot_general | solution.py:20
  556.3 12.5 %collective-permute-start.2 = (f32[1,64,1408]{2,1,0:T(8,128)}, f32[1,64,1408]{2,1,0:T(8,128)S(1)}, u32[]{:S(2)}, u32[]{:S(2)}) collective-permute-start(f32[1,64,1408]{2,1,0:T(8,128)} %get-tuple-element.455), channel_id=5, source_target_pairs={{0,1},{1,2},{2,3},{3,4},{4,5},{5,6},{6,7},{7,0},{8,9},{9,10},{10,1... | collective-permute-start | bytes 1081352 | tf_op jit(solution)/vmap(transpose(jvp()))/dot_general | solution.py:20
  556.3 13.2 %collective-permute-start.3 = (f32[1,64,1408]{2,1,0:T(8,128)S(1)}, f32[1,64,1408]{2,1,0:T(8,128)}, u32[]{:S(2)}, u32[]{:S(2)}) collective-permute-start(f32[1,64,1408]{2,1,0:T(8,128)S(1)} %get-tuple-element.456), channel_id=4, source_target_pairs={{0,7},{1,0},{2,1},{3,2},{4,3},{5,4},{6,5},{7,6},{8,15},{9,8},{10,9... | collective-permute-start | bytes 1081352 | tf_op jit(solution)/vmap(transpose(jvp()))/dot_general | solution.py:20
  572.0 11.4 %collective-permute-start.25 = (f32[1,64,1408]{2,1,0:T(8,128)}, f32[1,64,1408]{2,1,0:T(8,128)S(1)}, u32[]{:S(2)}, u32[]{:S(2)}) collective-permute-start(f32[1,64,1408]{2,1,0:T(8,128)} %copy-done.17), channel_id=12, source_target_pairs={{0,1},{1,2},{2,3},{3,4},{4,5},{5,6},{6,7},{7,0},{8,9},{9,10},{10,1... | collective-permute-start | bytes 1081352 | tf_op jit(solution)/vmap(transpose(jvp()))/dot_general | solution.py:20
  572.2 15.1 %collective-permute-start.24 = (f32[1,64,1408]{2,1,0:T(8,128)S(1)}, f32[1,64,1408]{2,1,0:T(8,128)S(1)}, u32[]{:S(2)}, u32[]{:S(2)}) collective-permute-start(f32[1,64,1408]{2,1,0:T(8,128)S(1)} %get-tuple-element.37), channel_id=6, source_target_pairs={{0,1},{1,2},{2,3},{3,4},{4,5},{5,6},{6,7},{7,0},{8,9},{9,10},{10,1... | collective-permute-start | bytes 1081352 | tf_op jit(solution)/vmap(transpose(jvp()))/dot_general | solution.py:20
  609.2 80.4 %all-gather.12.cloned.1.call-start = ((), (), s32[]{:S(2)}) async-start(), calls=%async_computation.1 | async-start | bytes 3244032 | tf_op jit(solution)/reshape | solution.py:58
  612.0 118.3 %all-gather.10.cloned.1.call-start = ((), (), s32[]{:S(2)}) async-start(), calls=%async_computation | async-start | bytes 3244032 | tf_op jit(solution)/reshape | solution.py:58
  (46 other events, 655.0 us)
Sparse Core Ops, SparseCore 0:
  609.4 39.4 all-gather.13
  651.0 38.4 all-gather.11
  691.8 38.4 all-gather.9
where the time goes:
time: 755 us; the launch traced here: 744 us
  matrix products  285 us (38%)
  waiting for transfers between devices  159 us (21%)
  starting transfers between devices  86.9 us (12%)
  local copies, waits for them, and re-layouts  79.3 us (11%)
  other arithmetic  76.3 us (10%)
  loops' own time  24.7 us (3%)
  between operations  17.8 us (2%)
  blocking collectives  15.3 us (2%)
    reshape x3, waiting for transfers between devices, step(): t.reshape(-1, *t.shape[2:])  115 us
    dot_general x11, matrix products, layer(): gate = jnp.dot(a, w['w_gate'], preferred_element_type=jnp.float32)  108 us
    dot_general x11, matrix products, layer(): up = jnp.dot(a, w['w_up'], preferred_element_type=jnp.float32)  97.7 us
    dot_general x11, matrix products, matmul(): jnp.dot(a, w, preferred_element_type=jnp.float32).astype(jnp.bfloat16)  79.2 us
    unnamed x59, local copies, waits for them, and re-layouts  68.7 us
    dot_general x18, starting transfers between devices, matmul(): jnp.dot(a, w, preferred_element_type=jnp.float32).astype(jnp.bfloat16)  31.2 us
    dot_general x18, starting transfers between devices, layer(): gate = jnp.dot(a, w['w_gate'], preferred_element_type=jnp.float32)  27.8 us
    dot_general x18, starting transfers between devices, layer(): up = jnp.dot(a, w['w_up'], preferred_element_type=jnp.float32)  27.8 us
  transfers between devices with their start and end apart: 57, of which 18 were waited for; matrix products, arithmetic and copies ran while one was open for 33% of the time, Pallas kernels for 0%

commit v1 on v0

v1 whole, which is shorter than its diff:
```python
import jax
import jax.numpy as jnp
from jax import lax
from jax.sharding import PartitionSpec as P


def normed(h):
    wide = h.astype(jnp.float32)
    scale = lax.rsqrt(jnp.mean(wide**2, -1, keepdims=True) + 1e-6)
    return (wide * scale).astype(jnp.bfloat16)


def mid(gate, up):
    return (jax.nn.silu(gate) * up).astype(jnp.bfloat16)


def dot(a, b, dims):
    return lax.dot_general(a, b, (dims, ((), ())), preferred_element_type=jnp.float32)


def weight_grad(a, d):
    return dot(a, d, ((0,), (0,))).astype(jnp.bfloat16)


def adamw(w, m, v, g):
    m = 0.9 * m + 0.1 * g
    v = 0.95 * v + 0.05 * g * g
    step = m * lax.rsqrt(v + 1e-8) + 0.1 * w
    return (w - 0.02 * step).astype(jnp.bfloat16), m, v


def solution(mesh):
    n = mesh.shape["dp"]

    def scatter(g):
        return lax.psum_scatter(g, "dp", scatter_dimension=0, tiled=True)

    def step(x, dy, wg, wu, wd, mg, mu, md, vg, vu, vd):
        x, dy = x[0], dy[0]
        layers = wg.shape[0]
        saved = []
        h = x
        for i in range(layers):
            a, norm_back = jax.vjp(normed, h)
            gate, up = dot(a, wg[i], ((1,), (0,))), dot(a, wu[i], ((1,), (0,)))
            s, mid_back = jax.vjp(mid, gate, up)
            saved.append((a, norm_back, s, mid_back))
            if i < layers - 1:
                h = h + dot(s, wd[i], ((1,), (0,))).astype(jnp.bfloat16)
        shards = [None] * layers
        dh = dy
        for i in reversed(range(layers)):
            a, norm_back, s, mid_back = saved[i]
            down = scatter(weight_grad(s, dh))
            ds = dot(dh, wd[i], ((1,), (1,))).astype(jnp.bfloat16)
            dgate, dup = (t.astype(jnp.bfloat16) for t in mid_back(ds))
            gate_shard = scatter(weight_grad(a, dgate))
            up_shard = scatter(weight_grad(a, dup))
            shards[i] = (gate_shard, up_shard, down)
            if i > 0:
                da = dot(dgate, wg[i], ((1,), (1,))).astype(jnp.bfloat16) + dot(dup, wu[i], ((1,), (1,))).astype(jnp.bfloat16)
                dh = dh + norm_back(da)[0]
        grads = [[s.astype(jnp.float32) for s in layer] for layer in shards]
        total = lax.psum(sum(jnp.sum(g * g) for layer in grads for g in layer), "dp")
        count = sum(w.size for w in (wg, wu, wd))
        factor = jnp.minimum(1.0, 0.5 * lax.rsqrt(total / count + 1e-30))
        me = lax.axis_index("dp")
        new_w, new_m, new_v = [], [], []
        for k, (w, m, v) in enumerate(((wg, mg, vg), (wu, mu, vu), (wd, md, vd))):
            rows = w.shape[1] // n
            out = []
            for i in range(layers):
                mine = lax.dynamic_slice_in_dim(w[i], me * rows, rows, 0).astype(jnp.float32)
                nw, nm, nv = adamw(mine, m[i], v[i], grads[i][k] * factor)
                out.append((lax.all_gather(nw, "dp", axis=0, tiled=True), nm, nv))
            for lst, vals in zip((new_w, new_m, new_v), zip(*out)):
                lst.append(jnp.stack(vals))
        return (*new_w, *new_m, *new_v)

    seq, whole, rows = P(("rep", "dp"), None, None), P(None, None, None), P(None, "dp", None)
    return jax.shard_map(
        step,
        mesh=mesh,
        in_specs=(seq, seq) + (whole,) * 3 + (rows,) * 6,
        out_specs=(P("rep", None, None),) * 3 + (P("rep", "dp", None),) * 6,
        check_vma=False,
    )
```

time: 755 us -> 674 us (0.89)
  waiting for transfers between devices: 159 us -> 332 us
  starting transfers between devices: 86.9 us -> 0.77 us
  local copies, waits for them, and re-layouts: 79.3 us -> 21.2 us
  matrix products: 285 us -> 238 us
  other arithmetic: 76.3 us -> 37.5 us
  loops' own time: 24.7 us -> 0 us
    all_gather x0 -> x6, waiting for transfers between devices: none -> 196 us  [step(): out.append((lax.all_gather(nw, 'dp', axis=0, tiled=True), nm, nv))]
    reduce_scatter x0 -> x6, waiting for transfers between devices: none -> 134 us  [scatter(): return lax.psum_scatter(g, 'dp', scatter_dimension=0, tiled=True)]
    reshape x3 -> x0, waiting for transfers between devices: 115 us -> none  [step(): t.reshape(-1, *t.shape[2:])]
    dot_general x54 -> x0, starting transfers between devices: 86.8 us -> none  [the longest x18 31.2 us: matmul(): jnp.dot(a, w, preferred_element_type=jnp.float32).astype(jnp.bfloat16)]
    unnamed x59 -> x60, local copies, waits for them, and re-layouts: 68.7 us -> 19 us
    dot_general x33 -> x15, matrix products: 285 us -> 238 us  [dot(): lax.dot_general(a, b, (dims, ((), ())), preferred_element_type=jnp.float32)]
    dot_general x54 -> x0, waiting for transfers between devices: 43.3 us -> none  [the longest x18 20.6 us: matmul(): jnp.dot(a, w, preferred_element_type=jnp.float32).astype(jnp.bfloat16)]
    dot_general x48 -> x0, other arithmetic: 26.8 us -> none  [the longest x8 10.1 us: layer(): gate = jnp.dot(a, w['w_gate'], preferred_element_type=jnp.float32)]
  transfers between devices with their start and end apart: 57 -> 12, of which waited for: 18 -> 10; matrix products, arithmetic and copies ran while one was open for 33% -> 16% of each run, Pallas kernels for 0% -> 0%
where the time goes in v1:
time: 674 us; the launch traced here: 665 us
  waiting for transfers between devices  332 us (49%)
  matrix products  238 us (35%)
  other arithmetic  37.5 us (6%)
  local copies, waits for them, and re-layouts  21.2 us (3%)
  between operations  19.6 us (3%)
  blocking collectives  16.1 us (2%)
    dot_general x15, matrix products, dot(): lax.dot_general(a, b, (dims, ((), ())), preferred_element_type=jnp.float32)  238 us
    all_gather x6, waiting for transfers between devices, step(): out.append((lax.all_gather(nw, 'dp', axis=0, tiled=True), nm, nv))  196 us
    reduce_scatter x6, waiting for transfers between devices, scatter(): return lax.psum_scatter(g, 'dp', scatter_dimension=0, tiled=True)  134 us
    unnamed x60, local copies, waits for them, and re-layouts  19 us
    psum x1, blocking collectives, step(): lax.psum(sum((jnp.sum(g * g) for layer in grads for g in layer)), 'dp')  16.1 us
    another operation x6, other arithmetic, step(): lst.append(jnp.stack(vals))  14.6 us
  transfers between devices with their start and end apart: 12, of which 10 were waited for; matrix products, arithmetic and copies ran while one was open for 16% of the time, Pallas kernels for 0%

profile of v1, /device:TPU:22, one launch (start us, length us, event | category | flops | bytes accessed | tf_op | source)
XLA Modules:
  0.0 665.3 jit_solution(2200569997400336475)
XLA Ops:
  7.3 6.4 copy.20
  13.7 3.1 fusion.15
  16.8 6.4 copy.21
  23.2 11.6 %convolution_convert_fusion.1 = bf16[4096,1408]{1,0:T(8,128)(2,1)} fusion(bf16[1,4096,512]{2,1,0:T(8,128)(2,1)} %param.12, bf16[2,1408,512]{2,1,0:T(8,128)(2,1)} %param.15), kind=kOutput, calls=%fused_computation.21 | convolution fusion | flops 5911347200 | bytes 17170432 | tf_op jit(solution)/shard_map/dot_general | solution.py:18
  34.8 11.2 %fusion.53 = f32[4096,1408]{1,0:T(8,128)} fusion(bf16[1,4096,512]{2,1,0:T(8,128)(2,1)S(1)} %copy-done.2, f32[4096]{0:T(1024)S(1)} %add_rsqrt_fusion, bf16[2,512,1408]{2,1,0:T(8,128)(2,1)S(1)} %copy-done.10), kind=kOutput, calls=%fused_computation.61 | convolution fusion | flops 5911871488 | bytes 28721152 | tf_op jit(solution)/shard_map/dot_general | solution.py:18
  46.0 22.5 %multiply_convert_fusion.1 = (bf16[4096,1408]{1,0:T(8,128)(2,1)}, f32[4096,1408]{1,0:T(8,128)}) fusion(f32[4096,1408]{1,0:T(8,128)} %fusion.53, bf16[2,512,1408]{2,1,0:T(8,128)(2,1)} %param.14, bf16[1,4096,512]{2,1,0:T(8,128)(2,1)S(1)} %copy-done.2, f32[4096]{0:T(1024)S(1)} %add_rsqrt_fusion), kind=kOutput, calls=%fused_computation.17 | convolution fusion | flops 5946474496 | bytes 63324160 | tf_op jit(solution)/shard_map/dot_general | solution.py:18
  68.5 11.1 %fusion.19 = (f32[4096]{0:T(1024)S(1)}, bf16[4096,512]{0,1:T(8,128)(2,1)S(1)}) fusion(bf16[4096,1408]{1,0:T(8,128)(2,1)} %get-tuple-element.35, bf16[2,1408,512]{2,1,0:T(8,128)(2,1)} %param.15, bf16[1,4096,512]{1,2,0:T(8,128)(2,1)S(1)} %copy-done), kind=kOutput, calls=%fused_computation.36 | convolution fusion | flops 5916061696 | bytes 21381120 | tf_op jit(solution)/shard_map/dot_general | solution.py:18
  79.6 2.0 copy-done.3
  81.6 11.2 %fusion.49 = f32[4096,1408]{1,0:T(8,128)} fusion(bf16[4096,512]{0,1:T(8,128)(2,1)S(1)} %get-tuple-element.38, f32[4096]{0:T(1024)S(1)} %fusion.118, bf16[2,512,1408]{2,1,0:T(8,128)(2,1)S(1)} %copy-done.8), kind=kOutput, calls=%fused_computation.59 | convolution fusion | flops 5911871488 | bytes 28721152 | tf_op jit(solution)/shard_map/dot_general | solution.py:18
  92.7 35.1 %fusion.4 = (bf16[4096,1408]{1,0:T(8,128)(2,1)}, bf16[4096,1408]{1,0:T(8,128)(2,1)}, f32[4096,1408]{1,0:T(8,128)}) fusion(f32[4096,1408]{1,0:T(8,128)} %fusion.49, bf16[4096,1408]{1,0:T(8,128)(2,1)} %convolution_convert_fusion.1, bf16[2,512,1408]{2,1,0:T(8,128)(2,1)} %param.13, bf16[4096,512]{0,1:T(8,128)(2,1)} %copy-done.3, f32[4096]{0:T(1024)S(1)} %fusion.118), kind=kOutput, calls=%fused_computation.10 | convolution fusion | flops 5998379008 | bytes 86392832 | tf_op jit(solution)/shard_map/dot_general | solution.py:18
  127.9 12.7 %convolution_convert_fusion.2 = bf16[4096,512]{0,1:T(8,128)(2,1)} fusion(bf16[4096,1408]{1,0:T(8,128)(2,1)} %get-tuple-element.10, bf16[2,512,1408]{2,1,0:T(8,128)(2,1)S(1)} %copy-done.8), kind=kOutput, calls=%fused_computation.40 | convolution fusion | flops 5907677184 | bytes 17170432 | tf_op jit(solution)/shard_map/dot_general | solution.py:18
  140.6 12.7 %fusion.21 = (f32[4096]{0:T(1024)S(1)}, bf16[4096,512]{0,1:T(8,128)(2,1)S(1)}) fusion(bf16[4096,512]{0,1:T(8,128)(2,1)S(1)} %copy-done.4, bf16[4096,512]{0,1:T(8,128)(2,1)} %convolution_convert_fusion.2, bf16[4096,1408]{1,0:T(8,128)(2,1)} %get-tuple-element.9, bf16[2,512,1408]{2,1,0:T(8,128)(2,1)S(1)} %copy-done.11), kind=kOutput, calls=%fused_computation.38 | convolution fusion | flops 5918158848 | bytes 25575424 | tf_op jit(solution)/shard_map/dot_general | solution.py:18
  153.3 3.3 fusion.25
  156.7 1.9 copy-done.5
  158.6 9.5 %convolution_convert_fusion = bf16[4096,1408]{1,0:T(8,128)(2,1)} fusion(bf16[4096,512]{0,1:T(8,128)(2,1)S(1)} %fusion.25, bf16[2,1408,512]{2,1,0:T(8,128)(2,1)S(1)} %copy-done.6), kind=kOutput, calls=%fused_computation.20 | convolution fusion | flops 5911347200 | bytes 17170432 | tf_op jit(solution)/shard_map/dot_general | solution.py:18
  168.1 17.2 %fusion.37 = bf16[512,1408]{1,0:T(8,128)(2,1)} fusion(bf16[4096,1408]{1,0:T(8,128)(2,1)} %convolution_convert_fusion, f32[4096,1408]{1,0:T(8,128)} %fusion.53, bf16[1,4096,512]{1,2,0:T(8,128)(2,1)} %copy.20, f32[4096]{0:T(1024)S(1)} %add_rsqrt_fusion), kind=kOutput, calls=%fused_computation.50 | convolution fusion | flops 5952962560 | bytes 40255488 | tf_op jit(solution)/shard_map/dot_general | solution.py:18
  185.4 24.5 %fusion.32 = bf16[512,1408]{1,0:T(8,128)(2,1)} fusion(f32[4096,1408]{1,0:T(8,128)} %fusion.53, f32[4096,1408]{1,0:T(8,128)} %get-tuple-element.36, bf16[4096,1408]{1,0:T(8,128)(2,1)} %convolution_convert_fusion, bf16[1,4096,512]{1,2,0:T(8,128)(2,1)} %copy.20, f32[4096]{0:T(1024)S(1)} %add_rsqrt_fusion), kind=kOutput, calls=%fused_computation.49 | convolution fusion | flops 5981798400 | bytes 63324160 | tf_op jit(solution)/shard_map/dot_general | solution.py:18
  210.0 12.2 %convolution_convert_fusion.7 = bf16[1408,512]{1,0:T(8,128)(2,1)} fusion(bf16[4096,1408]{1,0:T(8,128)(2,1)} %get-tuple-element.35, bf16[4096,512]{0,1:T(8,128)(2,1)} %copy-done.5), kind=kOutput, calls=%fused_computation.54 | convolution fusion | flops 5906300928 | bytes 17170432 | tf_op jit(solution)/shard_map/dot_general | solution.py:18
  222.4 12.6 %convolution_convert_fusion.6 = bf16[512,1408]{1,0:T(8,128)(2,1)} fusion(bf16[4096,1408]{1,0:T(8,128)(2,1)} %get-tuple-element.9, bf16[4096,512]{0,1:T(8,128)(2,1)} %copy-done.3, f32[4096]{0:T(1024)S(1)} %fusion.118), kind=kOutput, calls=%fused_computation.53 | convolution fusion | flops 5912592384 | bytes 17186816 | tf_op jit(solution)/shard_map/dot_general | solution.py:18
  235.2 12.9 %convolution_convert_fusion.5 = bf16[512,1408]{1,0:T(8,128)(2,1)} fusion(bf16[4096,1408]{1,0:T(8,128)(2,1)} %get-tuple-element.10, bf16[4096,512]{0,1:T(8,128)(2,1)} %copy-done.3, f32[4096]{0:T(1024)S(1)} %fusion.118), kind=kOutput, calls=%fused_computation.52 | convolution fusion | flops 5912592384 | bytes 17186816 | tf_op jit(solution)/shard_map/dot_general | solution.py:18
  248.2 20.7 %fusion.42 = bf16[1408,512]{1,0:T(8,128)(2,1)} fusion(bf16[1,4096,512]{2,1,0:T(8,128)(2,1)} %param.12, f32[4096,1408]{1,0:T(8,128)} %fusion.49, f32[4096,1408]{1,0:T(8,128)} %get-tuple-element.39), kind=kOutput, calls=%fused_computation.51 | convolution fusion | flops 5940903936 | bytes 51773440 | tf_op jit(solution)/shard_map/dot_general | solution.py:18
  269.0 1.8 fusion.131
  270.8 1.8 fusion.77
  272.6 1.6 fusion.76
  275.5 27.5 %reduce-scatter.11.cloned.1.call-done = bf16[176,512]{1,0:T(8,128)(2,1)} async-done(((bf16[1408,512]{1,0:T(8,128)(2,1)}), bf16[176,512]{1,0:T(8,128)(2,1)}) %reduce-scatter.11.cloned.1.call-update) | async-done | bytes 180240 | tf_op jit(solution)/shard_map/reduce_scatter | solution.py:36
  303.0 1.6 fusion.78
  305.2 35.5 %reduce-scatter.13.cloned.1.call-done = bf16[64,1408]{1,0:T(8,128)(2,1)} async-done(((bf16[512,1408]{1,0:T(8,128)(2,1)}), bf16[64,1408]{1,0:T(8,128)(2,1)}) %reduce-scatter.13.cloned.1.call-update) | async-done | bytes 180240 | tf_op jit(solution)/shard_map/reduce_scatter | solution.py:36
  340.7 1.6 fusion.79
  343.0 35.4 %reduce-scatter.15.cloned.1.call-done = bf16[64,1408]{1,0:T(8,128)(2,1)} async-done(((bf16[512,1408]{1,0:T(8,128)(2,1)}), bf16[64,1408]{1,0:T(8,128)(2,1)}) %reduce-scatter.15.cloned.1.call-update) | async-done | bytes 180240 | tf_op jit(solution)/shard_map/reduce_scatter | solution.py:36
  378.4 1.6 fusion.80
  380.7 35.5 %reduce-scatter.17.cloned.1.call-done = bf16[176,512]{1,0:T(8,128)(2,1)} async-done(((bf16[1408,512]{1,0:T(8,128)(2,1)}), bf16[176,512]{1,0:T(8,128)(2,1)}) %reduce-scatter.17.cloned.1.call-update) | async-done | bytes 180240 | tf_op jit(solution)/shard_map/reduce_scatter | solution.py:36
  416.1 1.6 fusion.81
  418.4 16.1 %psum.7 = f32[]{:T(128)} all-reduce(f32[]{:T(128)S(6)} %add.160), channel_id=1, replica_groups=mesh['rep'=8,'dp'=8] {'dp'}, use_global_device_ids=true, to_apply=%region_15.16 | all-reduce | flops 1 | bytes 8 | tf_op jit(solution)/shard_map/psum | solution.py:64
  435.2 2.9 fusion.96
  440.4 2.5 fusion.90
  445.1 1.3 fusion.84
  447.2 1.2 pad_maximum_fusion.5
  448.4 1.2 pad_maximum_fusion.4
  449.6 1.2 pad_maximum_fusion.3
  450.8 23.1 %all-gather.15.cloned.1.call-done = bf16[1408,512]{1,0:T(8,128)(2,1)} async-done(((bf16[176,512]{1,0:T(8,128)(2,1)}), bf16[1408,512]{1,0:T(8,128)(2,1)}) %all-gather.15.cloned.1.call-update) | async-done | bytes 1441808 | tf_op jit(solution)/shard_map/all_gather | solution.py:75
  474.0 36.1 %all-gather.17.cloned.1.call-done = bf16[1408,512]{1,0:T(8,128)(2,1)} async-done(((bf16[176,512]{1,0:T(8,128)(2,1)}), bf16[1408,512]{1,0:T(8,128)(2,1)}) %all-gather.17.cloned.1.call-update) | async-done | bytes 1441808 | tf_op jit(solution)/shard_map/all_gather | solution.py:75
  510.1 3.6 pad_maximum_fusion.2
  513.7 32.5 %all-gather.11.cloned.1.call-done = bf16[512,1408]{1,0:T(8,128)(2,1)} async-done(((bf16[64,1408]{1,0:T(8,128)(2,1)}), bf16[512,1408]{1,0:T(8,128)(2,1)}) %all-gather.11.cloned.1.call-update) | async-done | bytes 1441808 | tf_op jit(solution)/shard_map/all_gather | solution.py:75
  546.2 36.0 %all-gather.13.cloned.1.call-done = bf16[512,1408]{1,0:T(8,128)(2,1)} async-done(((bf16[64,1408]{1,0:T(8,128)(2,1)}), bf16[512,1408]{1,0:T(8,128)(2,1)}) %all-gather.13.cloned.1.call-update) | async-done | bytes 1441808 | tf_op jit(solution)/shard_map/all_gather | solution.py:75
  582.2 3.7 pad_maximum_fusion.1
  585.9 32.5 %all-gather.7.cloned.1.call-done = bf16[512,1408]{1,0:T(8,128)(2,1)} async-done(((bf16[64,1408]{1,0:T(8,128)(2,1)}), bf16[512,1408]{1,0:T(8,128)(2,1)}) %all-gather.7.cloned.1.call-update) | async-done | bytes 1441808 | tf_op jit(solution)/shard_map/all_gather | solution.py:75
  618.4 36.0 %all-gather.9.cloned.1.call-done = bf16[512,1408]{1,0:T(8,128)(2,1)} async-done(((bf16[64,1408]{1,0:T(8,128)(2,1)}), bf16[512,1408]{1,0:T(8,128)(2,1)}) %all-gather.9.cloned.1.call-update) | async-done | bytes 1441808 | tf_op jit(solution)/shard_map/all_gather | solution.py:75
  654.3 3.7 pad_maximum_fusion
  (87 shorter events, 5.9 us)
Async XLA Ops:
  7.2 263.6 %reduce-scatter.9.cloned.1.call-start = ((), (), s32[]{:S(2)}) async-start(), calls=%async_computation.7 | async-start | bytes 1622016 | tf_op jit(solution)/shard_map/reduce_scatter | solution.py:36
  23.2 11.6 %copy-start.2 = (bf16[1,4096,512]{2,1,0:T(8,128)(2,1)S(1)}, bf16[1,4096,512]{2,1,0:T(8,128)(2,1)}, u32[]{:S(2)}) copy-start(bf16[1,4096,512]{2,1,0:T(8,128)(2,1)} %param.11) | copy-start | bytes 12582916
  23.2 11.6 %copy-start.10 = (bf16[2,512,1408]{2,1,0:T(8,128)(2,1)S(1)}, bf16[2,512,1408]{2,1,0:T(8,128)(2,1)}, u32[]{:S(2)}) copy-start(bf16[2,512,1408]{2,1,0:T(8,128)(2,1)} %param.13) | copy-start | bytes 8650756
  46.0 22.5 %copy-start = (bf16[1,4096,512]{1,2,0:T(8,128)(2,1)S(1)}, bf16[1,4096,512]{1,2,0:T(8,128)(2,1)}, u32[]{:S(2)}) copy-start(bf16[1,4096,512]{1,2,0:T(8,128)(2,1)} %copy.20) | copy-start | bytes 12582916
  68.5 13.1 %copy-start.8 = (bf16[2,512,1408]{2,1,0:T(8,128)(2,1)S(1)}, bf16[2,512,1408]{2,1,0:T(8,128)(2,1)}, u32[]{:S(2)}) copy-start(bf16[2,512,1408]{2,1,0:T(8,128)(2,1)} %param.14) | copy-start | bytes 8650756
  79.5 2.0 copy-start.3
  127.9 12.7 %copy-start.4 = (bf16[4096,512]{0,1:T(8,128)(2,1)S(1)}, bf16[4096,512]{0,1:T(8,128)(2,1)}, u32[]{:S(2)}) copy-start(bf16[4096,512]{0,1:T(8,128)(2,1)} %copy-done.3) | copy-start | bytes 12582916
  127.9 12.7 %copy-start.11 = (bf16[2,512,1408]{2,1,0:T(8,128)(2,1)S(1)}, bf16[2,512,1408]{2,1,0:T(8,128)(2,1)}, u32[]{:S(2)}) copy-start(bf16[2,512,1408]{2,1,0:T(8,128)(2,1)} %param.13) | copy-start | bytes 8650756
  140.5 12.8 %copy-start.1 = (bf16[1,4096,512]{1,2,0:T(8,128)(2,1)S(1)}, bf16[1,4096,512]{1,2,0:T(8,128)(2,1)}, u32[]{:S(2)}) copy-start(bf16[1,4096,512]{1,2,0:T(8,128)(2,1)} %copy.21) | copy-start | bytes 12582916
  153.3 5.3 copy-start.6
  156.7 1.9 copy-start.5
  185.3 87.3 %reduce-scatter.7.cloned.1.call-start = ((), (), s32[]{:S(2)}) async-start(), calls=%async_computation.6 | async-start | bytes 1622016 | tf_op jit(solution)/shard_map/reduce_scatter | solution.py:36
  210.0 93.0 %reduce-scatter.11.cloned.1.call-start = ((), (), s32[]{:S(2)}) async-start(), calls=%async_computation.8 | async-start | bytes 1622016 | tf_op jit(solution)/shard_map/reduce_scatter | solution.py:36
  222.3 118.4 %reduce-scatter.13.cloned.1.call-start = ((), (), s32[]{:S(2)}) async-start(), calls=%async_computation.9 | async-start | bytes 1622016 | tf_op jit(solution)/shard_map/reduce_scatter | solution.py:36
  235.1 143.3 %reduce-scatter.15.cloned.1.call-start = ((), (), s32[]{:S(2)}) async-start(), calls=%async_computation.10 | async-start | bytes 1622016 | tf_op jit(solution)/shard_map/reduce_scatter | solution.py:36
  248.1 168.0 %reduce-scatter.17.cloned.1.call-start = ((), (), s32[]{:S(2)}) async-start(), calls=%async_computation.11 | async-start | bytes 1622016 | tf_op jit(solution)/shard_map/reduce_scatter | solution.py:36
  248.2 20.8 %copy-start.7 = (bf16[2,1408,512]{2,1,0:T(8,128)(2,1)S(1)}, bf16[2,1408,512]{2,1,0:T(8,128)(2,1)}, u32[]{:S(2)}) copy-start(bf16[2,1408,512]{2,1,0:T(8,128)(2,1)} %param.15) | copy-start | bytes 8650756
  269.0 205.0 %all-gather.15.cloned.1.call-start = ((), (), s32[]{:S(2)}) async-start(), calls=%async_computation.16 | async-start | bytes 1622016 | tf_op jit(solution)/shard_map/all_gather | solution.py:75
  270.8 168.3 %copy-start.9 = (bf16[2,512,1408]{2,1,0:T(8,128)(2,1)S(1)}, bf16[2,512,1408]{2,1,0:T(8,128)(2,1)}, u32[]{:S(2)}) copy-start(bf16[2,512,1408]{2,1,0:T(8,128)(2,1)} %param.14) | copy-start | bytes 8650756
  438.2 71.9 %all-gather.17.cloned.1.call-start = ((), (), s32[]{:S(2)}) async-start(), calls=%async_computation.17 | async-start | bytes 1622016 | tf_op jit(solution)/shard_map/all_gather | solution.py:75
  439.0 107.2 %all-gather.11.cloned.1.call-start = ((), (), s32[]{:S(2)}) async-start(), calls=%async_computation.14 | async-start | bytes 1622016 | tf_op jit(solution)/shard_map/all_gather | solution.py:75
  439.1 1.1 copy-start.25
  439.1 1.3 copy-start.26
  439.3 4.3 copy-start.12
  440.4 3.6 copy-start.23
  443.0 139.3 %all-gather.13.cloned.1.call-start = ((), (), s32[]{:S(2)}) async-start(), calls=%async_computation.15 | async-start | bytes 1622016 | tf_op jit(solution)/shard_map/all_gather | solution.py:75
  443.6 174.7 %all-gather.7.cloned.1.call-start = ((), (), s32[]{:S(2)}) async-start(), calls=%async_computation.12 | async-start | bytes 1622016 | tf_op jit(solution)/shard_map/all_gather | solution.py:75
  443.7 0.9 copy-start.24
  443.7 1.2 copy-start.27
  443.7 1.4 copy-start.28
  443.9 3.2 copy-start.13
  444.0 3.2 copy-start.14
  444.0 3.2 copy-start.15
  444.0 4.4 copy-start.16
  444.0 4.4 copy-start.17
  444.0 4.4 copy-start.18
  444.0 4.4 copy-start.19
  446.5 207.8 %all-gather.9.cloned.1.call-start = ((), (), s32[]{:S(2)}) async-start(), calls=%async_computation.13 | async-start | bytes 1622016 | tf_op jit(solution)/shard_map/all_gather | solution.py:75
  447.1 2.5 copy-start.20
  447.2 2.5 copy-start.21
  447.2 2.5 copy-start.22
Sparse Core Ops, SparseCore 0:
  185.4 40.5 reduce-scatter.8
  228.9 35.5 reduce-scatter.6
  267.4 35.5 reduce-scatter.10
  305.2 35.4 reduce-scatter.12
  342.9 35.4 reduce-scatter.14
  380.6 35.4 reduce-scatter.16
  438.3 35.5 all-gather.14
  475.5 34.5 all-gather.16
  511.7 34.5 all-gather.10
  547.7 34.5 all-gather.12
  583.8 34.5 all-gather.6
  619.8 34.5 all-gather.8

commit v2 on v0

v2 whole, which is shorter than its diff:
```python
import functools

import jax
import jax.numpy as jnp
from jax import lax
from jax.experimental import pallas as pl
from jax.experimental.pallas import tpu as pltpu
from jax.sharding import PartitionSpec as P

BF, F32 = jnp.bfloat16, jnp.float32
MESH = pl.DeviceIdType.MESH
ANY = pl.BlockSpec(memory_space=pl.ANY)
ROWS = (((1,), (0,)), ((), ()))
BY_T = (((1,), (1,)), ((), ()))
T_BY = (((0,), (0,)), ((), ()))


def dot(a, b, dims):
    return lax.dot_general(a, b, dims, preferred_element_type=F32)


def rms_scale(wide):
    return lax.rsqrt(jnp.mean(wide * wide, -1, keepdims=True) + 1e-6)


def sigmoid(t):
    return 1.0 / (1.0 + jnp.exp(-t))


class Ring:
    def __init__(self, n, own, recv, send_sem, recv_sem):
        self.n, self.own, self.recv, self.send_sem, self.recv_sem = n, own, recv, send_sem, recv_sem
        self.rows, self.half = recv.shape[2], recv.shape[3]
        far, near = n // 2, n - 1 - n // 2
        self.streams = ((0, 1, far), (1, -1, far), (1, 1, near), (0, -1, near))
        self.me = lax.axis_index("dp")

    def mine(self, owner, half):
        owner = lax.rem(owner + self.n, self.n)
        rows = pl.ds(pl.multiple_of(owner * self.rows, self.rows), self.rows)
        return self.own.at[rows, pl.ds(half * self.half, self.half)]

    def copy(self, s, hop):
        half, way, hops = self.streams[s]
        src = self.mine(self.me + way * hops, half) if hop == 1 else self.recv.at[s, hop - 2]
        to = lax.rem(self.me + way + self.n, self.n)
        return pltpu.make_async_remote_copy(
            src_ref=src,
            dst_ref=self.recv.at[s, hop - 1],
            send_sem=self.send_sem.at[s, hop - 1],
            recv_sem=self.recv_sem.at[s, hop - 1],
            device_id={"dp": to},
            device_id_type=MESH,
        )

    def start(self):
        for s in range(4):
            self.copy(s, 1).start()

    def add(self, s, hop):
        half, way, hops = self.streams[s]
        self.copy(s, hop).wait_recv()
        if hop < hops:
            buf = self.recv.at[s, hop - 1]
            term = self.mine(self.me + way * (hops - hop), half)
            buf[...] = (buf[...].astype(F32) + term[...].astype(F32)).astype(BF)

    def send(self, s, hop):
        if hop < self.streams[s][2]:
            self.copy(s, hop + 1).start()

    def events(self):
        out = []
        for hop in range(1, self.streams[0][2] + 1):
            for pair in ((0, 1), (2, 3)):
                if hop <= self.streams[pair[0]][2]:
                    out.append(tuple((s, hop) for s in pair))
        return out

    def handle(self, pair):
        for s, hop in pair:
            self.add(s, hop)
        for s, hop in pair:
            self.send(s, hop)

    def finish(self, out):
        for half in (0, 1):
            total = self.mine(self.me, half)[...].astype(F32)
            for s, (its, _, hops) in enumerate(self.streams):
                if its == half:
                    total = total + self.recv[s, hops - 1].astype(F32)
            out[:, pl.ds(half * self.half, self.half)] = total.astype(BF)
        for s, (_, _, hops) in enumerate(self.streams):
            for hop in range(1, hops + 1):
                self.copy(s, hop).wait_send()


def ring_scratch(n, rows, cols):
    return [
        pltpu.VMEM((n * rows, cols), BF),
        pltpu.VMEM((4, n // 2, rows, cols // 2), BF),
        pltpu.SemaphoreType.DMA((4, n // 2)),
        pltpu.SemaphoreType.DMA((4, n // 2)),
        pltpu.SemaphoreType.DMA(()),
    ]


def greet(n, others):
    me = lax.axis_index("dp")
    barrier = pltpu.get_barrier_semaphore()
    for d in others:
        pl.semaphore_signal(barrier, inc=1, device_id={"dp": lax.rem(me + d + n, n)}, device_id_type=MESH)
    pl.semaphore_wait(barrier, len(others))


def with_ring(n, steps, due, refs, own_hbm, out):
    own, recv, send_sem, recv_sem, load_sem = refs
    i = pl.program_id(0)
    ring = Ring(n, own, recv, send_sem, recv_sem)
    load = pltpu.make_async_copy(own_hbm, own, load_sem)

    @pl.when(i == 0)
    def _():
        load.start()
        greet(n, (1, -1))
        load.wait()
        ring.start()

    events = ring.events()
    for step in range(1, steps):
        now = [e for e, d in zip(events, due, strict=True) if d == step]
        if now:

            @pl.when(i == step)
            def _(now=now):
                for e in now:
                    ring.handle(e)

    def close():
        @pl.when(i == steps - 1)
        def _():
            for e, d in zip(events, due, strict=True):
                if d >= steps:
                    ring.handle(e)
            ring.finish(out)

    return close


def load_all(copies):
    @pl.when(pl.program_id(0) == 0)
    def _():
        for c in copies:
            c.start()
        for c in copies:
            c.wait()


def top_kernel(x_ref, dy_ref, wg, wu, wd, gu0_ref, h1_ref, dgu1_ref, dwd_ref, wgu, wdn, acc, sem):
    i = pl.program_id(0)
    ff = wd.shape[1]
    load_all(
        [pltpu.make_async_copy(wg.at[k], wgu.at[k, :, pl.ds(0, ff)], sem.at[k, 0]) for k in (0, 1)]
        + [pltpu.make_async_copy(wu.at[k], wgu.at[k, :, pl.ds(ff, ff)], sem.at[k, 1]) for k in (0, 1)]
        + [pltpu.make_async_copy(wd.at[k], wdn.at[k], sem.at[k, 2]) for k in (0, 1)]
    )
    x = x_ref[...].astype(F32)
    gu = dot((x * rms_scale(x)).astype(BF), wgu[0], ROWS)
    gu0_ref[...] = gu
    gate, up = gu[:, :ff], gu[:, ff:]
    s = (gate * sigmoid(gate) * up).astype(BF)
    h = (x + dot(s, wdn[0], ROWS).astype(BF).astype(F32)).astype(BF)
    h1_ref[...] = h
    h = h.astype(F32)
    gu = dot((h * rms_scale(h)).astype(BF), wgu[1], ROWS)
    gate, up = gu[:, :ff], gu[:, ff:]
    sig = sigmoid(gate)
    silu = gate * sig
    dy = dy_ref[...]
    part = dot((silu * up).astype(BF), dy, T_BY)

    @pl.when(i == 0)
    def _():
        acc[...] = part

    @pl.when(i > 0)
    def _():
        acc[...] += part

    ds = dot(dy, wdn[1], BY_T).astype(BF).astype(F32)
    dgu1_ref[:, :ff] = (ds * up * (sig + silu * (1.0 - sig))).astype(BF)
    dgu1_ref[:, ff:] = (ds * silu).astype(BF)

    @pl.when(i == pl.num_programs(0) - 1)
    def _():
        dwd_ref[...] = acc[...].astype(BF)


def gu_kernel(n, due, h_ref, dgu_ref, own_hbm, dw_ref, sum_ref, acc, *ring):
    i = pl.program_id(0)
    close = with_ring(n, len(due[1]), due[0], ring, own_hbm, sum_ref)
    h = h_ref[...].astype(F32)
    part = dot((h * rms_scale(h)).astype(BF), dgu_ref[...], T_BY)

    @pl.when(i == 0)
    def _():
        acc[...] = part

    @pl.when(i > 0)
    def _():
        acc[...] += part

    @pl.when(i == pl.num_programs(0) - 1)
    def _():
        dw_ref[...] = acc[...].astype(BF)

    close()


def mid_kernel(n, due, h1_ref, dy_ref, dgu1_ref, gu0_ref, wg, wu, wd, own_hbm, dgu0_ref, dwd_ref, sum_ref, wgu, wdn, acc, sem, *ring):
    i = pl.program_id(0)
    ff = wd.shape[1]
    close = with_ring(n, len(due[1]), due[0], ring, own_hbm, sum_ref)
    load_all(
        [
            pltpu.make_async_copy(wg.at[1], wgu.at[:, pl.ds(0, ff)], sem.at[0]),
            pltpu.make_async_copy(wu.at[1], wgu.at[:, pl.ds(ff, ff)], sem.at[1]),
            pltpu.make_async_copy(wd.at[0], wdn, sem.at[2]),
        ]
    )
    da = dot(dgu1_ref[...], wgu[...], BY_T).astype(BF).astype(F32)
    h = h1_ref[...].astype(F32)
    scale = rms_scale(h)
    back = scale * (da - h * (scale * scale * jnp.mean(da * h, -1, keepdims=True)))
    dh = (dy_ref[...].astype(F32) + back.astype(BF).astype(F32)).astype(BF)
    ds = dot(dh, wdn[...], BY_T).astype(BF).astype(F32)
    gate, up = gu0_ref[:, :ff], gu0_ref[:, ff:]
    sig = sigmoid(gate)
    silu = gate * sig
    dgu0_ref[:, :ff] = (ds * up * (sig + silu * (1.0 - sig))).astype(BF)
    dgu0_ref[:, ff:] = (ds * silu).astype(BF)
    part = dot((silu * up).astype(BF), dh, T_BY)

    @pl.when(i == 0)
    def _():
        acc[...] = part

    @pl.when(i > 0)
    def _():
        acc[...] += part

    @pl.when(i == pl.num_programs(0) - 1)
    def _():
        dwd_ref[...] = acc[...].astype(BF)

    close()


def end_kernel(
    n, count, gu1, d1, d0, own_hbm, wg, wu, wd, mg, mu, md, vg, vu, vd,
    owg, owu, owd, omg, omu, omd, ovg, ovu, ovd,
    gbuf, dbuf, all_g, all_u, all_d, mb_g, mb_d, vb_g, vb_d, wb_g, wb_d, sq_send, sq_all,
    in_sem, out_sem, sq_s, sq_r, ag_s, ag_r, *ring_refs,
):
    me = lax.axis_index("dp")
    ff, d = md.shape[1] * n, md.shape[2]
    rg, rd = mg.shape[1], md.shape[1]
    own, recv, send_sem, recv_sem, load_sem = ring_refs
    ring = Ring(n, own, recv, send_sem, recv_sem)
    my_g = pl.ds(pl.multiple_of(me * rg, rg), rg)
    my_d = pl.ds(pl.multiple_of(me * rd, rd), rd)
    load = pltpu.make_async_copy(own_hbm, own, load_sem)
    load.start()
    loads = [
        pltpu.make_async_copy(gu1, gbuf.at[1], in_sem.at[0]),
        pltpu.make_async_copy(d1, dbuf.at[1], in_sem.at[1]),
        pltpu.make_async_copy(d0, dbuf.at[0], in_sem.at[2]),
        pltpu.make_async_copy(mg, mb_g.at[0], in_sem.at[3]),
        pltpu.make_async_copy(mu, mb_g.at[1], in_sem.at[4]),
        pltpu.make_async_copy(md, mb_d, in_sem.at[5]),
        pltpu.make_async_copy(vg, vb_g.at[0], in_sem.at[6]),
        pltpu.make_async_copy(vu, vb_g.at[1], in_sem.at[7]),
        pltpu.make_async_copy(vd, vb_d, in_sem.at[8]),
        pltpu.make_async_copy(wg.at[:, my_g], wb_g.at[0], in_sem.at[9]),
        pltpu.make_async_copy(wu.at[:, my_g], wb_g.at[1], in_sem.at[10]),
        pltpu.make_async_copy(wd.at[:, my_d], wb_d, in_sem.at[11]),
    ]
    for c in loads:
        c.start()
    greet(n, tuple(range(1, n)))
    load.wait()
    ring.start()
    for c in loads:
        c.wait()
    for e in ring.events():
        ring.handle(e)
    ring.finish(gbuf.at[0])

    def squares(t):
        t = t.astype(F32)
        t = t * t
        t = jnp.sum(t.reshape(t.shape[0] // 8, 8, t.shape[1]), 0)
        return sum(t[:, k : k + 128] for k in range(0, t.shape[1], 128))

    sq = squares(gbuf[0]) + squares(gbuf[1]) + squares(dbuf[0]) + squares(dbuf[1])
    sq_send[...] = sq
    to_all = [
        pltpu.make_async_remote_copy(
            src_ref=sq_send,
            dst_ref=sq_all.at[k - 1],
            send_sem=sq_s.at[k - 1],
            recv_sem=sq_r.at[k - 1],
            device_id={"dp": lax.rem(me + k, n)},
            device_id_type=MESH,
        )
        for k in range(1, n)
    ]
    for c in to_all:
        c.start()
    for c in to_all:
        c.wait_recv()
    total = jnp.sum(sq + jnp.sum(sq_all[...], 0), keepdims=True)
    factor = jnp.minimum(1.0, 0.5 * lax.rsqrt(total / count + 1e-30))

    far, near = n // 2, n - 1 - n // 2
    streams = ((0, 1, far), (1, -1, far), (1, 1, near), (0, -1, near))

    def gathered(layer, down, half, owner):
        owner = lax.rem(owner + n, n)
        if down:
            return all_d.at[layer, pl.ds(pl.multiple_of(owner * rd, rd), rd), pl.ds(half * (d // 2), d // 2)]
        return (all_g, all_u)[half].at[layer, pl.ds(pl.multiple_of(owner * rg, rg), rg)]

    def copy(layer, down, s, hop):
        half, way, _ = streams[s]
        part = gathered(layer, down, half, me - way * (hop - 1))
        unit = layer * 2 + down
        return pltpu.make_async_remote_copy(
            src_ref=part,
            dst_ref=part,
            send_sem=ag_s.at[unit, s, hop - 1],
            recv_sem=ag_r.at[unit, s, hop - 1],
            device_id={"dp": lax.rem(me + way + n, n)},
            device_id_type=MESH,
        )

    def arrival(layer, down, s, hop):
        half, way, _ = streams[s]
        part = gathered(layer, down, half, me - way * hop)
        unit = layer * 2 + down
        return pltpu.make_async_remote_copy(
            src_ref=part,
            dst_ref=part,
            send_sem=ag_s.at[unit, s, hop - 1],
            recv_sem=ag_r.at[unit, s, hop - 1],
            device_id={"dp": lax.rem(me + way + n, n)},
            device_id_type=MESH,
        )

    def adamw(w_ref, m_ref, v_ref, g, out):
        g = g.astype(F32) * factor
        m = 0.9 * m_ref[...] + 0.1 * g
        v = 0.95 * v_ref[...] + 0.05 * g * g
        w = w_ref[...].astype(F32)
        out[...] = (w - 0.02 * (m * lax.rsqrt(v + 1e-8) + 0.1 * w)).astype(BF)
        m_ref[...] = m
        v_ref[...] = v

    units = [(layer, down) for layer in (0, 1) for down in (0, 1)]
    for layer, down in units:
        if down:
            adamw(wb_d.at[layer], mb_d.at[layer], vb_d.at[layer], dbuf[layer], all_d.at[layer, my_d])
        else:
            for k, to in ((0, all_g), (1, all_u)):
                adamw(wb_g.at[k, layer], mb_g.at[k, layer], vb_g.at[k, layer], gbuf[layer, :, k * ff : (k + 1) * ff], to.at[layer, my_g])
        for s in range(4):
            copy(layer, down, s, 1).start()
    stores = [
        pltpu.make_async_copy(a, b, out_sem.at[k])
        for k, (a, b) in enumerate(
            ((mb_g.at[0], omg), (mb_g.at[1], omu), (mb_d, omd), (vb_g.at[0], ovg), (vb_g.at[1], ovu), (vb_d, ovd))
        )
    ]
    for c in stores:
        c.start()
    for hop in range(1, far + 1):
        for layer, down in units:
            for s in range(4):
                if hop <= streams[s][2]:
                    arrival(layer, down, s, hop).wait_recv()
                    if hop < streams[s][2]:
                        copy(layer, down, s, hop + 1).start()
    last = [pltpu.make_async_copy(a, b, out_sem.at[6 + k]) for k, (a, b) in enumerate(((all_g, owg), (all_u, owu), (all_d, owd)))]
    for c in last:
        c.start()
    for c in to_all:
        c.wait_send()
    for layer, down in units:
        for s in range(4):
            for hop in range(1, streams[s][2] + 1):
                copy(layer, down, s, hop).wait_send()
    for c in stores + last:
        c.wait()


def params(cid=None):
    if cid is None:
        return pltpu.CompilerParams(vmem_limit_bytes=62 << 20, dimension_semantics=("arbitrary",))
    return pltpu.CompilerParams(vmem_limit_bytes=62 << 20, collective_id=cid, has_side_effects=True)


def solution(mesh):
    n = mesh.shape["dp"]

    def step(x, dy, wg, wu, wd, mg, mu, md, vg, vu, vd):
        x, dy = x[0], dy[0]
        tokens, d = x.shape
        ff = wd.shape[1]
        rg, rd = d // n, ff // n
        tile = 256
        steps = tokens // tile
        rows = lambda c: pl.BlockSpec((tile, c), lambda i: (i, 0))
        whole = lambda *s: pl.BlockSpec(s, lambda i: (0,) * len(s))
        array = jax.ShapeDtypeStruct
        sem = pltpu.SemaphoreType.DMA
        mm = 2 * tokens * d * ff

        gu0, h1, dgu1, dwd1 = pl.pallas_call(
            top_kernel,
            grid=(steps,),
            in_specs=[rows(d), rows(d), ANY, ANY, ANY],
            out_specs=[rows(2 * ff), rows(d), rows(2 * ff), whole(ff, d)],
            out_shape=[array((tokens, 2 * ff), F32), array((tokens, d), BF), array((tokens, 2 * ff), BF), array((ff, d), BF)],
            scratch_shapes=[pltpu.VMEM((2, d, 2 * ff), BF), pltpu.VMEM((2, ff, d), BF), pltpu.VMEM((ff, d), F32), sem((2, 3))],
            compiler_params=params(),
            cost_estimate=pl.CostEstimate(flops=7 * mm, bytes_accessed=90 << 20, transcendentals=0),
            name="top",
        )(x, dy, wg, wu, wd)

        def due(msg_us, step_us):
            at = [2.5 + (p + 1) * msg_us for p in range(n - 1)]
            return [int(t / step_us) + 1 for t in at], [0] * steps

        def gu_grad(h, dgu, own, cid, name):
            return pl.pallas_call(
                functools.partial(gu_kernel, n, due(1.95, 1.0)),
                grid=(steps,),
                in_specs=[rows(d), rows(2 * ff), ANY],
                out_specs=[whole(d, 2 * ff), whole(rd, d)],
                out_shape=[array((d, 2 * ff), BF), array((rd, d), BF)],
                scratch_shapes=[pltpu.VMEM((d, 2 * ff), F32)] + ring_scratch(n, rd, d),
                compiler_params=params(cid),
                cost_estimate=pl.CostEstimate(flops=2 * mm, bytes_accessed=30 << 20, transcendentals=0),
                name=name,
            )(h, dgu, own)

        dwgu1, sum_d1 = gu_grad(h1, dgu1, dwd1, 0, "gu1")
        dgu0, dwd0, sum_gu1 = pl.pallas_call(
            functools.partial(mid_kernel, n, due(3.87, 2.0)),
            grid=(steps,),
            in_specs=[rows(d), rows(d), rows(2 * ff), rows(2 * ff), ANY, ANY, ANY, ANY],
            out_specs=[rows(2 * ff), whole(ff, d), whole(rg, 2 * ff)],
            out_shape=[array((tokens, 2 * ff), BF), array((ff, d), BF), array((rg, 2 * ff), BF)],
            scratch_shapes=[pltpu.VMEM((d, 2 * ff), BF), pltpu.VMEM((ff, d), BF), pltpu.VMEM((ff, d), F32), sem((3,))]
            + ring_scratch(n, rg, 2 * ff),
            compiler_params=params(1),
            cost_estimate=pl.CostEstimate(flops=4 * mm, bytes_accessed=100 << 20, transcendentals=0),
            name="mid",
        )(h1, dy, dgu1, gu0, wg, wu, wd, dwgu1)
        dwgu0, sum_d0 = gu_grad(x, dgu0, dwd0, 2, "gu0")

        vm = pltpu.VMEM
        outs = pl.pallas_call(
            functools.partial(end_kernel, n, float(wg.size + wu.size + wd.size)),
            in_specs=[ANY] * 13,
            out_specs=[ANY] * 9,
            out_shape=[array(t.shape, BF) for t in (wg, wu, wd)] + [array(t.shape, F32) for t in (mg, mu, md, vg, vu, vd)],
            scratch_shapes=[
                vm((2, rg, 2 * ff), BF), vm((2, rd, d), BF),
                vm(wg.shape, BF), vm(wu.shape, BF), vm(wd.shape, BF),
                vm((2, *mg.shape), F32), vm(md.shape, F32), vm((2, *vg.shape), F32), vm(vd.shape, F32),
                vm((2, *mg.shape), BF), vm(md.shape, BF),
                vm((8, 128), F32), vm((n - 1, 8, 128), F32),
                sem((12,)), sem((9,)), sem((n - 1,)), sem((n - 1,)), sem((4, 4, n // 2)), sem((4, 4, n // 2)),
            ] + ring_scratch(n, rg, 2 * ff),
            compiler_params=params(3),
            name="end",
        )(sum_gu1, sum_d1, sum_d0, dwgu0, wg, wu, wd, mg, mu, md, vg, vu, vd)
        return tuple(outs)

    seq, whole, rows = P(("rep", "dp"), None, None), P(None, None, None), P(None, "dp", None)
    return jax.shard_map(
        step,
        mesh=mesh,
        in_specs=(seq, seq) + (whole,) * 3 + (rows,) * 6,
        out_specs=(P("rep", None, None),) * 3 + (P("rep", "dp", None),) * 6,
        check_vma=False,
    )
```

time: 755 us -> 336 us (0.45); the launches traced: 744 us -> 336 us
  Pallas kernels: 0 us -> 322 us
  matrix products: 285 us -> 0 us
  waiting for transfers between devices: 159 us -> 0 us
  starting transfers between devices: 86.9 us -> 0 us
  other arithmetic: 76.3 us -> 0 us
  local copies, waits for them, and re-layouts: 79.3 us -> 13.4 us
  loops' own time: 24.7 us -> 0 us
  between operations: 17.8 us -> 0.7 us
  blocking collectives: 15.3 us -> 0 us
    pallas_call x0 -> x5, Pallas kernels: none -> 322 us  [the longest x1 125 us: step(): pl.pallas_call(functools.partial(end_kernel, n, float(wg.size + wu.size +...]
    dot_general x33 -> x0, matrix products: 285 us -> none  [the longest x11 108 us: layer(): gate = jnp.dot(a, w['w_gate'], preferred_element_type=jnp.float32)]
    reshape x3 -> x0, waiting for transfers between devices: 115 us -> none  [step(): t.reshape(-1, *t.shape[2:])]
    dot_general x54 -> x0, starting transfers between devices: 86.8 us -> none  [the longest x18 31.2 us: matmul(): jnp.dot(a, w, preferred_element_type=jnp.float32).astype(jnp.bfloat16)]
    unnamed x59 -> x25, local copies, waits for them, and re-layouts: 68.7 us -> 13.4 us
    dot_general x54 -> x0, waiting for transfers between devices: 43.3 us -> none  [the longest x18 20.6 us: matmul(): jnp.dot(a, w, preferred_element_type=jnp.float32).astype(jnp.bfloat16)]
    dot_general x48 -> x0, other arithmetic: 26.8 us -> none  [the longest x8 10.1 us: layer(): gate = jnp.dot(a, w['w_gate'], preferred_element_type=jnp.float32)]
    convert_element_type x3 -> x0, other arithmetic: 25.9 us -> none  [the longest x1 19.7 us: layer(): (jax.nn.silu(gate) * up).astype(jnp.bfloat16)]
  transfers between devices with their start and end apart: 57 -> 0, of which waited for: 18 -> 0; matrix products, arithmetic and copies ran while one was open for 33% -> 0% of each run, Pallas kernels for 0% -> 0%
where the time goes in v2:
time: 336 us
  Pallas kernels  322 us (96%)
  local copies, waits for them, and re-layouts  13.4 us (4%)
    pallas_call x1, Pallas kernels, step(): pl.pallas_call(functools.partial(end_kernel, n, float(wg.size + wu.size +...  125 us
    pallas_call x2, Pallas kernels, gu_grad(): pl.pallas_call(functools.partial(gu_kernel, n, due(1.95, 1.0)), grid=(ste...  71.2 us
    pallas_call x1, Pallas kernels, step(): pl.pallas_call(top_kernel, grid=(steps,), in_specs=[rows(d), rows(d), ANY...  71.1 us
    pallas_call x1, Pallas kernels, step(): pl.pallas_call(functools.partial(mid_kernel, n, due(3.87, 2.0)), grid=(st...  54.3 us
    unnamed x25, local copies, waits for them, and re-layouts  13.4 us

profile of v2, /device:TPU:22, one launch (start us, length us, event | category | flops | bytes accessed | tf_op | source)
XLA Modules:
  0.0 335.6 jit_solution(13018505400257728956)
XLA Ops:
  0.6 71.1 %top.1 = (f32[4096,2816]{1,0:T(8,128)}, bf16[4096,512]{1,0:T(8,128)(2,1)}, bf16[4096,2816]{1,0:T(8,128)(2,1)}, bf16[1408,512]{1,0:T(8,128)(2,1)}) custom-call(bf16[4096,512]{1,0:T(8,128)(2,1)} %bitcast.4, bf16[4096,512]{1,0:T(8,128)(2,1)} %bitcast.2, bf16[2,512,1408]{2,1,0:T(8,128)(2,1)} %wg.5, bf16[2,512,1408]{2,1,0:T(8,128)(2,1)} %wu.5, ...), custom_call_target="tpu_custom_call" | custom-call | flops 41339060224 | bytes 94371840 | tf_op jit(solution)/shard_map/top/pallas_call | solution.py:428
  71.8 38.4 %gu1.1 = (bf16[512,2816]{1,0:T(8,128)(2,1)}, bf16[176,512]{1,0:T(8,128)(2,1)}) custom-call(bf16[4096,512]{1,0:T(8,128)(2,1)} %get-tuple-element.20.h_ref.h1_ref, bf16[4096,2816]{1,0:T(8,128)(2,1)} %get-tuple-element.21.dgu_ref.dgu1_ref, bf16[1408,512]{1,0:T(8,128)(2,1)} %get-tuple-element.23.own_hbm), custom_call_target="tpu_custom_call" | custom-call | flops 11811160064 | bytes 31457280 | tf_op jit(solution)/shard_map/gu1/pallas_call | solution.py:445
  110.2 54.3 %mid.1 = (bf16[4096,2816]{1,0:T(8,128)(2,1)}, bf16[1408,512]{1,0:T(8,128)(2,1)}, bf16[64,2816]{1,0:T(8,128)(2,1)}) custom-call(bf16[4096,512]{1,0:T(8,128)(2,1)} %get-tuple-element.20.h_ref.h1_ref, bf16[4096,512]{1,0:T(8,128)(2,1)} %bitcast.3, bf16[4096,2816]{1,0:T(8,128)(2,1)} %get-tuple-element.21.dgu_ref.dgu1_ref, ...), custom_call_target="tpu_custom_call" | custom-call | flops 23622320128 | bytes 104857600 | tf_op jit(solution)/shard_map/mid/pallas_call | solution.py:458
  164.5 32.7 %gu0.1 = (bf16[512,2816]{1,0:T(8,128)(2,1)}, bf16[176,512]{1,0:T(8,128)(2,1)}) custom-call(bf16[4096,512]{1,0:T(8,128)(2,1)} %bitcast.5, bf16[4096,2816]{1,0:T(8,128)(2,1)} %get-tuple-element.27.dgu_ref, bf16[1408,512]{1,0:T(8,128)(2,1)} %get-tuple-element.28.own_hbm), custom_call_target="tpu_custom_call" | custom-call | flops 11811160064 | bytes 31457280 | tf_op jit(solution)/shard_map/gu0/pallas_call | solution.py:445
  197.3 124.9 %end.1 = (bf16[2,512,1408]{2,1,0:T(8,128)(2,1)}, bf16[2,512,1408]{2,1,0:T(8,128)(2,1)}, bf16[2,1408,512]{2,1,0:T(8,128)(2,1)}, f32[2,64,1408]{2,1,0:T(8,128)}, f...) custom-call(bf16[64,2816]{1,0:T(8,128)(2,1)} %get-tuple-element.25.g, ...), custom_call_target="tpu_custom_call" | custom-call | tf_op jit(solution)/shard_map/end/pallas_call | solution.py:473
  322.2 0.0 copy-start.1
  322.2 3.8 %copy.29 = bf16[2,512,1408]{2,1,0:T(8,128)(2,1)} copy(bf16[2,512,1408]{2,1,0:T(8,128)(2,1)} %get-tuple-element.40) | data formatting | bytes 5767168
  325.9 0.0 copy-done.1
  326.0 0.0 copy-start
  326.0 1.6 copy.30
  327.5 1.3 copy-done
  328.8 0.0 copy-start.7
  328.8 0.0 copy-start.6
  328.8 1.6 copy.31
  330.4 0.0 copy-done.7
  330.4 0.0 copy-start.5
  330.4 0.0 copy-start.4
  330.4 0.0 copy-start.3
  330.4 0.9 copy.32
  331.3 0.0 copy-done.6
  331.3 0.0 copy-start.2
  331.3 0.9 copy.33
  332.1 0.0 copy-done.5
  332.1 0.9 copy.34
  333.0 0.0 copy-done.4
  333.0 0.9 copy.35
  333.9 0.0 copy-done.3
  333.9 0.9 copy.36
  334.7 0.0 copy-done.2
  334.7 0.9 copy.37
Async XLA Ops:
  322.2 3.8 %copy-start.1 = (bf16[2,512,1408]{2,1,0:T(8,128)(2,1)S(1)}, bf16[2,512,1408]{2,1,0:T(8,128)(2,1)}, u32[]{:S(2)}) copy-start(bf16[2,512,1408]{2,1,0:T(8,128)(2,1)} %get-tuple-element.41) | copy-start | bytes 8650756
  326.0 2.9 copy-start
  328.8 1.6 copy-start.7
  328.8 2.5 copy-start.6
  330.4 1.7 copy-start.5
  330.4 2.6 copy-start.4
  330.4 3.4 %copy-start.3 = (f32[2,64,1408]{2,1,0:T(8,128)S(1)}, f32[2,64,1408]{2,1,0:T(8,128)}, u32[]{:S(2)}) copy-start(f32[2,64,1408]{2,1,0:T(8,128)} %get-tuple-element.47) | copy-start | bytes 2162692
  331.3 3.4 %copy-start.2 = (f32[2,176,512]{2,1,0:T(8,128)S(1)}, f32[2,176,512]{2,1,0:T(8,128)}, u32[]{:S(2)}) copy-start(f32[2,176,512]{2,1,0:T(8,128)} %get-tuple-element.48) | copy-start | bytes 2162692

commit v3 on v0

v3 whole, which is shorter than its diff:
```python
import functools

import jax
import jax.numpy as jnp
from jax import lax
from jax.experimental import pallas as pl
from jax.experimental.pallas import tpu as pltpu
from jax.sharding import PartitionSpec as P

BF, F32 = jnp.bfloat16, jnp.float32
MESH = pl.DeviceIdType.MESH
ANY = pl.BlockSpec(memory_space=pl.ANY)
ROWS = (((1,), (0,)), ((), ()))
BY_T = (((1,), (1,)), ((), ()))
T_BY = (((0,), (0,)), ((), ()))


def dot(a, b, dims):
    return lax.dot_general(a, b, dims, preferred_element_type=F32)


def rms_scale(wide):
    return lax.rsqrt(jnp.mean(wide * wide, -1, keepdims=True) + 1e-6)


def sigmoid(t):
    return 1.0 / (1.0 + jnp.exp(-t))


class Ring:
    def __init__(self, n, own, recv, send_sem, recv_sem):
        self.n, self.own, self.recv, self.send_sem, self.recv_sem = n, own, recv, send_sem, recv_sem
        self.rows, self.half = recv.shape[2], recv.shape[3]
        far, near = n // 2, n - 1 - n // 2
        self.streams = ((0, 1, far), (1, -1, far), (1, 1, near), (0, -1, near))
        self.me = lax.axis_index("dp")

    def mine(self, owner, half):
        owner = lax.rem(owner + self.n, self.n)
        rows = pl.ds(pl.multiple_of(owner * self.rows, self.rows), self.rows)
        return self.own.at[rows, pl.ds(half * self.half, self.half)]

    def copy(self, s, hop):
        half, way, hops = self.streams[s]
        src = self.mine(self.me + way * hops, half) if hop == 1 else self.recv.at[s, hop - 2]
        to = lax.rem(self.me + way + self.n, self.n)
        return pltpu.make_async_remote_copy(
            src_ref=src,
            dst_ref=self.recv.at[s, hop - 1],
            send_sem=self.send_sem.at[s, hop - 1],
            recv_sem=self.recv_sem.at[s, hop - 1],
            device_id={"dp": to},
            device_id_type=MESH,
        )

    def start(self):
        for s in range(4):
            self.copy(s, 1).start()

    def add(self, s, hop):
        half, way, hops = self.streams[s]
        self.copy(s, hop).wait_recv()
        if hop < hops:
            buf = self.recv.at[s, hop - 1]
            term = self.mine(self.me + way * (hops - hop), half)
            buf[...] = (buf[...].astype(F32) + term[...].astype(F32)).astype(BF)

    def send(self, s, hop):
        if hop < self.streams[s][2]:
            self.copy(s, hop + 1).start()

    def handle(self, pair):
        for s, hop in pair:
            self.add(s, hop)
        for s, hop in pair:
            self.send(s, hop)

    def finish(self, out):
        for half in (0, 1):
            total = self.mine(self.me, half)[...].astype(F32)
            for s, (its, _, hops) in enumerate(self.streams):
                if its == half:
                    total = total + self.recv[s, hops - 1].astype(F32)
            out[:, pl.ds(half * self.half, self.half)] = total.astype(BF)
        for s, (_, _, hops) in enumerate(self.streams):
            for hop in range(1, hops + 1):
                self.copy(s, hop).wait_send()


def greet(n, others):
    me = lax.axis_index("dp")
    barrier = pltpu.get_barrier_semaphore()
    for d in others:
        pl.semaphore_signal(barrier, inc=1, device_id={"dp": lax.rem(me + d + n, n)}, device_id_type=MESH)
    pl.semaphore_wait(barrier, len(others))


def plan(hops, rings, steps, step_us):
    latency, free, waiting, out = 2.5, 0.0, [], []
    far, near = hops

    def send(ring, group, hop, now):
        nonlocal free
        free = max(free, now) + rings[ring][1]
        waiting.append((free + latency, ring, group, hop))

    step, now = 0, 0.0
    while step < steps or waiting:
        if step < steps:
            now = step * step_us
        else:
            now = max(steps * step_us, min(w[0] for w in waiting))
        for w in sorted(w for w in waiting if w[0] <= now):
            waiting.remove(w)
            _, ring, group, hop = w
            out.append((min(step, steps), ring, tuple((s, hop) for s in ((0, 1), (2, 3))[group])))
            if hop < (far, near)[group]:
                send(ring, group, hop + 1, now)
        for ring, (start, _) in enumerate(rings):
            if start == step:
                send(ring, 0, 1, now)
                send(ring, 1, 1, now)
        step += 1
    return out


def run_plan(todo, rings, steps):
    i = pl.program_id(0)
    for step in range(1, steps):
        now = [(r, pair) for at, r, pair in todo if at == step]
        if now:

            @pl.when(i == step)
            def _(now=now):
                for r, pair in now:
                    rings[r].handle(pair)


def rest_of_plan(todo, rings, steps):
    for at, r, pair in todo:
        if at >= steps:
            rings[r].handle(pair)


def with_ring(n, steps, todo, refs, own_hbm, out):
    own, load_sem, recv, send_sem, recv_sem = refs
    i = pl.program_id(0)
    ring = Ring(n, own, recv, send_sem, recv_sem)
    load = pltpu.make_async_copy(own_hbm, own, load_sem)

    @pl.when(i == 0)
    def _():
        load.start()
        greet(n, (1, -1))
        load.wait()
        ring.start()

    run_plan(todo, [ring], steps)

    def close():
        @pl.when(i == steps - 1)
        def _():
            rest_of_plan(todo, [ring], steps)
            ring.finish(out)

    return close


def load_all(copies):
    @pl.when(pl.program_id(0) == 0)
    def _():
        for c in copies:
            c.start()
        for c in copies:
            c.wait()


LANES = 128


def gate_up_copies(wg, wu, wgu, sem, blocks):
    out = []
    for k in range(blocks):
        for j, w in enumerate((wg, wu)):
            to = wgu.at[:, pl.ds(LANES * (2 * k + j), LANES)]
            out.append(pltpu.make_async_copy(w.at[:, pl.ds(LANES * k, LANES)], to, sem.at[2 * k + j]))
    return out


def chunks(blocks):
    return [(k, min(2, blocks - k)) for k in range(0, blocks, 2)]


def halves(ref):
    rows = ref.shape[0] // 2
    return [pl.ds(0, rows), pl.ds(rows, rows)]


def gated(gate, up, ds):
    sig = sigmoid(gate)
    silu = gate * sig
    ds = ds.astype(BF).astype(F32)
    return (silu * up).astype(BF), (ds * up * (sig + silu * (1.0 - sig))).astype(BF), (ds * silu).astype(BF)


def top_kernel(x_ref, dy_ref, wg, wu, wd, gu0_ref, h1_ref, a0_ref, a1_ref, dgu1_ref, dwd_ref, wgu, wdn, s_ref, acc, sem, dsem):
    i = pl.program_id(0)
    blocks = wd.shape[1] // LANES
    load_all(
        [c for k in (0, 1) for c in gate_up_copies(wg.at[k], wu.at[k], wgu.at[k], sem.at[k], blocks)]
        + [pltpu.make_async_copy(wd.at[k], wdn.at[k], dsem.at[k]) for k in (0, 1)]
    )

    @pl.when(i == 0)
    def _():
        acc[...] = jnp.zeros_like(acc)

    rows = halves(x_ref)
    for r in rows:
        x = x_ref[r, :].astype(F32)
        a0_ref[r, :] = (x * rms_scale(x)).astype(BF)
    for k, c in chunks(blocks):
        at = pl.ds(2 * LANES * k, 2 * LANES * c)
        for r in rows:
            gu = dot(a0_ref[r, :], wgu[0, :, at], ROWS)
            gu0_ref[r, at] = gu
            for b in range(c):
                gate, up = (gu[:, (2 * b + j) * LANES : (2 * b + j + 1) * LANES] for j in (0, 1))
                s_ref[r, pl.ds((k + b) * LANES, LANES)] = (gate * sigmoid(gate) * up).astype(BF)
    for r in rows:
        h = x_ref[r, :].astype(F32) + dot(s_ref[r, :], wdn[0], ROWS).astype(BF).astype(F32)
        h = h.astype(BF)
        h1_ref[r, :] = h
        h = h.astype(F32)
        a1_ref[r, :] = (h * rms_scale(h)).astype(BF)
    for k, c in chunks(blocks):
        at = pl.ds(2 * LANES * k, 2 * LANES * c)
        for r in rows:
            gu = dot(a1_ref[r, :], wgu[1, :, at], ROWS)
            ds = dot(dy_ref[r, :], wdn[1, pl.ds(LANES * k, LANES * c), :], BY_T)
            for b in range(c):
                gate, up = (gu[:, (2 * b + j) * LANES : (2 * b + j + 1) * LANES] for j in (0, 1))
                s, dgate, dup = gated(gate, up, ds[:, b * LANES : (b + 1) * LANES])
                s_ref[r, pl.ds((k + b) * LANES, LANES)] = s
                dgu1_ref[r, pl.ds(2 * (k + b) * LANES, LANES)] = dgate
                dgu1_ref[r, pl.ds((2 * (k + b) + 1) * LANES, LANES)] = dup
    acc[...] += dot(s_ref[...], dy_ref[...], T_BY)

    @pl.when(i == pl.num_programs(0) - 1)
    def _():
        dwd_ref[...] = acc[...].astype(BF)


def gu_kernel(n, steps, todo, a_ref, dgu_ref, own_hbm, dw_ref, sum_ref, *ring):
    close = with_ring(n, steps, todo, ring, own_hbm, sum_ref)
    dw_ref[...] = dot(a_ref[...], dgu_ref[...], T_BY).astype(BF)
    close()


def mid_kernel(
    n, steps, todo, h1_ref, dy_ref, dgu1_ref, gu0_ref, wg, wu, wd, own_hbm, dgu0_ref, dwd_ref, sum_ref,
    wgu, wdn, s_ref, dh_ref, acc, sem, dsem, *ring,
):
    i = pl.program_id(0)
    blocks = wd.shape[1] // LANES
    close = with_ring(n, steps, todo, ring, own_hbm, sum_ref)
    load_all(gate_up_copies(wg.at[1], wu.at[1], wgu, sem, blocks) + [pltpu.make_async_copy(wd.at[0], wdn, dsem)])

    @pl.when(i == 0)
    def _():
        acc[...] = jnp.zeros_like(acc)

    rows = halves(h1_ref)
    for r in rows:
        da = dot(dgu1_ref[r, :], wgu[...], BY_T).astype(BF).astype(F32)
        h = h1_ref[r, :].astype(F32)
        scale = rms_scale(h)
        back = scale * (da - h * (scale * scale * jnp.mean(da * h, -1, keepdims=True)))
        dh_ref[r, :] = (dy_ref[r, :].astype(F32) + back.astype(BF).astype(F32)).astype(BF)
    for k, c in chunks(blocks):
        for r in rows:
            ds = dot(dh_ref[r, :], wdn[pl.ds(LANES * k, LANES * c), :], BY_T)
            for b in range(c):
                at = [pl.ds((2 * (k + b) + j) * LANES, LANES) for j in (0, 1)]
                s, dgate, dup = gated(gu0_ref[r, at[0]], gu0_ref[r, at[1]], ds[:, b * LANES : (b + 1) * LANES])
                s_ref[r, pl.ds((k + b) * LANES, LANES)] = s
                dgu0_ref[r, at[0]] = dgate
                dgu0_ref[r, at[1]] = dup
    acc[...] += dot(s_ref[...], dh_ref[...], T_BY)

    @pl.when(i == steps - 1)
    def _():
        dwd_ref[...] = acc[...].astype(BF)

    close()


def end_kernel(
    n, steps, todo, groups, count,
    a_ref, dgu_ref, d0_hbm, gu1, d1, wg, wu, wd, mg, mu, md, vg, vu, vd,
    out_g, out_u, out_d, mb_g, mb_u, mb_d, vb_g, vb_u, vb_d,
    all_g, all_u, all_d, own_gu, own_d, gbuf, dbuf, wb_g, wb_d, sq_send, sq_all, in_sem, sq_s, sq_r, ag_s, ag_r, put_sem, *ring_refs,
):
    i = pl.program_id(0)
    me = lax.axis_index("dp")
    d = md.shape[2]
    rg, rd = mg.shape[1], md.shape[1]
    my_g = pl.ds(pl.multiple_of(me * rg, rg), rg)
    my_d = pl.ds(pl.multiple_of(me * rd, rd), rd)
    width = dgu_ref.shape[1]
    rings = [Ring(n, own_d, *ring_refs[:3])]
    for k, (first, wide) in enumerate(groups):
        rings.append(Ring(n, own_gu.at[:, pl.ds(first * width, wide * width)], *ring_refs[3 * k + 3 : 3 * k + 6]))
    load = pltpu.make_async_copy(d0_hbm, own_d, in_sem.at[0])
    loads = [
        pltpu.make_async_copy(gu1, gbuf.at[1], in_sem.at[1]),
        pltpu.make_async_copy(d1, dbuf.at[1], in_sem.at[2]),
        pltpu.make_async_copy(mg, mb_g, in_sem.at[3]),
        pltpu.make_async_copy(mu, mb_u, in_sem.at[4]),
        pltpu.make_async_copy(md, mb_d, in_sem.at[5]),
        pltpu.make_async_copy(vg, vb_g, in_sem.at[6]),
        pltpu.make_async_copy(vu, vb_u, in_sem.at[7]),
        pltpu.make_async_copy(vd, vb_d, in_sem.at[8]),
        pltpu.make_async_copy(wg.at[:, my_g], wb_g.at[0], in_sem.at[9]),
        pltpu.make_async_copy(wu.at[:, my_g], wb_g.at[1], in_sem.at[10]),
        pltpu.make_async_copy(wd.at[:, my_d], wb_d, in_sem.at[11]),
    ]

    @pl.when(i == 0)
    def _():
        load.start()
        greet(n, tuple(range(1, n)))
        load.wait()
        rings[0].start()
        for c in loads:
            c.start()

    run_plan(todo, rings, steps)
    for k, (first, wide) in enumerate(groups):
        if first + wide < steps:

            @pl.when(i == first + wide)
            def _(k=k):
                rings[k + 1].start()

    own_gu[:, pl.ds(pl.multiple_of(i * width, width), width)] = dot(a_ref[...], dgu_ref[...], T_BY).astype(BF)

    @pl.when(i == steps - 1)
    def _():
        for c in loads:
            c.wait()
        for k, (first, wide) in enumerate(groups):
            if first + wide >= steps:
                rings[k + 1].start()
        rest_of_plan(todo, rings, steps)
        rings[0].finish(dbuf.at[0])
        for k, (first, wide) in enumerate(groups):
            rings[k + 1].finish(gbuf.at[0, :, pl.ds(first * width, wide * width)])

        def squares(t):
            t = t.astype(F32)
            t = t * t
            t = jnp.sum(t.reshape(t.shape[0] // 8, 8, t.shape[1]), 0)
            return sum(t[:, k : k + LANES] for k in range(0, t.shape[1], LANES))

        sq = squares(gbuf[0]) + squares(gbuf[1]) + squares(dbuf[0]) + squares(dbuf[1])
        sq_send[...] = sq
        to_all = [
            pltpu.make_async_remote_copy(
                src_ref=sq_send,
                dst_ref=sq_all.at[k - 1],
                send_sem=sq_s.at[k - 1],
                recv_sem=sq_r.at[k - 1],
                device_id={"dp": lax.rem(me + k, n)},
                device_id_type=MESH,
            )
            for k in range(1, n)
        ]
        for c in to_all:
            c.start()
        for c in to_all:
            c.wait_recv()
        total = jnp.sum(sq + jnp.sum(sq_all[...], 0), keepdims=True)
        factor = jnp.minimum(1.0, 0.5 * lax.rsqrt(total / count + 1e-30))

        streams = rings[0].streams

        def gathered(layer, down, half, owner, to=(all_g, all_u, all_d)):
            owner = lax.rem(owner + n, n)
            if down:
                return to[2].at[layer, pl.ds(pl.multiple_of(owner * rd, rd), rd), pl.ds(half * (d // 2), d // 2)]
            return to[half].at[layer, pl.ds(pl.multiple_of(owner * rg, rg), rg)]

        def put(layer, down, s, hop):
            half, way, _ = streams[s]
            where = layer, down, half, me - way * hop
            sem = put_sem.at[layer * 2 + down, s, hop]
            return pltpu.make_async_copy(gathered(*where), gathered(*where, (out_g, out_u, out_d)), sem)

        def copy(layer, down, s, hop, owner):
            part = gathered(layer, down, streams[s][0], owner)
            return pltpu.make_async_remote_copy(
                src_ref=part,
                dst_ref=part,
                send_sem=ag_s.at[layer * 2 + down, s, hop - 1],
                recv_sem=ag_r.at[layer * 2 + down, s, hop - 1],
                device_id={"dp": lax.rem(me + streams[s][1] + n, n)},
                device_id_type=MESH,
            )

        def sending(layer, down, s, hop):
            return copy(layer, down, s, hop, me - streams[s][1] * (hop - 1))

        def arrival(layer, down, s, hop):
            return copy(layer, down, s, hop, me - streams[s][1] * hop)

        def adamw(w_ref, m_ref, v_ref, g, out):
            g = g.astype(F32) * factor
            m = 0.9 * m_ref[...] + 0.1 * g
            v = 0.95 * v_ref[...] + 0.05 * g * g
            w = w_ref[...].astype(F32)
            out[...] = (w - 0.02 * (m * lax.rsqrt(v + 1e-8) + 0.1 * w)).astype(BF)
            m_ref[...] = m
            v_ref[...] = v

        units = [(layer, down) for layer in (0, 1) for down in (0, 1)]
        for layer, down in units:
            if down:
                adamw(wb_d.at[layer], mb_d.at[layer], vb_d.at[layer], dbuf[layer], all_d.at[layer, my_d])
            else:
                for j, (m, v, to) in enumerate(((mb_g, vb_g, all_g), (mb_u, vb_u, all_u))):
                    g = [gbuf[layer, :, k : k + LANES] for k in range(j * LANES, gbuf.shape[2], 2 * LANES)]
                    adamw(wb_g.at[j, layer], m.at[layer], v.at[layer], jnp.concatenate(g, 1), to.at[layer, my_g])
            for s in range(4):
                sending(layer, down, s, 1).start()
            for s in (0, 1):
                put(layer, down, s, 0).start()
        for hop in range(1, streams[0][2] + 1):
            for layer, down in units:
                for s in range(4):
                    if hop <= streams[s][2]:
                        arrival(layer, down, s, hop).wait_recv()
                        if hop < streams[s][2]:
                            sending(layer, down, s, hop + 1).start()
                        put(layer, down, s, hop).start()
        for c in to_all:
            c.wait_send()
        for layer, down in units:
            for s in range(4):
                for hop in range(1, streams[s][2] + 1):
                    sending(layer, down, s, hop).wait_send()
                for hop in range(0 if s < 2 else 1, streams[s][2] + 1):
                    put(layer, down, s, hop).wait()


def store_kernel(*refs):
    k = len(refs) // 2
    copies = [pltpu.make_async_copy(a, b, refs[-1].at[j]) for j, (a, b) in enumerate(zip(refs[:k], refs[k : 2 * k]))]
    for c in copies:
        c.start()
    for c in copies:
        c.wait()


def params(cid=None, mib=62):
    if cid is None:
        return pltpu.CompilerParams(vmem_limit_bytes=mib << 20)
    return pltpu.CompilerParams(vmem_limit_bytes=mib << 20, collective_id=cid, has_side_effects=True)


def solution(mesh):
    n = mesh.shape["dp"]
    hops = n // 2, n - 1 - n // 2

    def step(x, dy, wg, wu, wd, mg, mu, md, vg, vu, vd):
        x, dy = x[0], dy[0]
        tokens, d = x.shape
        ff = wd.shape[1]
        rg, rd = d // n, ff // n
        tile = 512
        steps = tokens // tile
        blocks = ff // LANES
        rows = lambda c: pl.BlockSpec((tile, c), lambda i: (i, 0))
        whole = lambda *s: pl.BlockSpec(s, lambda i: (0,) * len(s))
        once = lambda *s: pl.BlockSpec(s, lambda i: (0,) * len(s), pipeline_mode=pl.Buffered(1))
        columns = lambda r: pl.BlockSpec((r, 2 * LANES), lambda i: (0, i))
        array = jax.ShapeDtypeStruct
        sem, vm = pltpu.SemaphoreType.DMA, pltpu.VMEM
        mm = 2 * tokens * d * ff

        def us(row_count, cols):
            return row_count * cols * 2 / 46.6e3

        def ring(row_count, cols):
            return [vm((4, hops[0], row_count, cols // 2), BF), sem((4, hops[0])), sem((4, hops[0]))]

        gu0, h1, a0, a1, dgu1, dwd1 = pl.pallas_call(
            top_kernel,
            grid=(steps,),
            in_specs=[rows(d), rows(d), ANY, ANY, ANY],
            out_specs=[rows(2 * ff), rows(d), rows(d), rows(d), rows(2 * ff), whole(ff, d)],
            out_shape=[array((tokens, 2 * ff), F32)]
            + [array((tokens, d), BF)] * 3
            + [array((tokens, 2 * ff), BF), array((ff, d), BF)],
            scratch_shapes=[
                vm((2, d, 2 * ff), BF), vm((2, ff, d), BF), vm((tile, ff), BF), vm((ff, d), F32), sem((2, 2 * blocks)), sem((2,)),
            ],
            compiler_params=params(),
            cost_estimate=pl.CostEstimate(flops=7 * mm, bytes_accessed=90 << 20, transcendentals=0),
            name="top",
        )(x, dy, wg, wu, wd)

        dwgu1, sum_d1 = pl.pallas_call(
            functools.partial(gu_kernel, n, blocks, plan(hops, [(0, us(rd, d // 2))], blocks, 1.7)),
            grid=(blocks,),
            in_specs=[once(tokens, d), columns(tokens), ANY],
            out_specs=[columns(d), whole(rd, d)],
            out_shape=[array((d, 2 * ff), BF), array((rd, d), BF)],
            scratch_shapes=[vm((ff, d), BF), sem(())] + ring(rd, d),
            compiler_params=params(0),
            cost_estimate=pl.CostEstimate(flops=2 * mm, bytes_accessed=30 << 20, transcendentals=0),
            name="gu1",
        )(a1, dgu1, dwd1)

        dgu0, dwd0, sum_gu1 = pl.pallas_call(
            functools.partial(mid_kernel, n, steps, plan(hops, [(0, us(rg, ff))], steps, 6.0)),
            grid=(steps,),
            in_specs=[rows(d), rows(d), rows(2 * ff), rows(2 * ff), ANY, ANY, ANY, ANY],
            out_specs=[rows(2 * ff), whole(ff, d), whole(rg, 2 * ff)],
            out_shape=[array((tokens, 2 * ff), BF), array((ff, d), BF), array((rg, 2 * ff), BF)],
            scratch_shapes=[
                vm((d, 2 * ff), BF), vm((ff, d), BF), vm((tile, ff), BF), vm((tile, d), BF), vm((ff, d), F32),
                sem((2 * blocks,)), sem(()), vm((d, 2 * ff), BF), sem(()),
            ] + ring(rg, 2 * ff),
            compiler_params=params(1),
            cost_estimate=pl.CostEstimate(flops=4 * mm, bytes_accessed=100 << 20, transcendentals=0),
            name="mid",
        )(h1, dy, dgu1, gu0, wg, wu, wd, dwgu1)

        groups, first = [], 0
        for k in range(3):
            wide = -(-(blocks - first) // (3 - k))
            groups.append((first, wide))
            first += wide
        todo = plan(hops, [(0, us(rd, d // 2))] + [(f + w, us(rg, w * LANES)) for f, w in groups], blocks, 1.7)
        outs = pl.pallas_call(
            functools.partial(end_kernel, n, blocks, todo, groups, float(wg.size + wu.size + wd.size)),
            grid=(blocks,),
            in_specs=[once(tokens, d), columns(tokens)] + [ANY] * 12,
            out_specs=[pl.BlockSpec(memory_space=pltpu.VMEM)] * 9,
            out_shape=[vm(t.shape, BF) for t in (wg, wu, wd)] + [vm(t.shape, F32) for t in (mg, mu, md, vg, vu, vd)],
            scratch_shapes=[
                vm(wg.shape, BF), vm(wu.shape, BF), vm(wd.shape, BF),
                vm((d, 2 * ff), BF), vm((ff, d), BF), vm((2, rg, 2 * ff), BF), vm((2, rd, d), BF),
                vm((2, *mg.shape), BF), vm(md.shape, BF), vm((8, LANES), F32), vm((n - 1, 8, LANES), F32),
                sem((12,)), sem((n - 1,)), sem((n - 1,)), sem((4, 4, hops[0])), sem((4, 4, hops[0])), sem((4, 4, hops[0] + 1)),
            ] + ring(rd, d) + [r for _, w in groups for r in ring(rg, w * 2 * LANES)],
            compiler_params=params(2, 40),
            cost_estimate=pl.CostEstimate(flops=2 * mm, bytes_accessed=30 << 20, transcendentals=0),
            name="end",
        )(a0, dgu0, dwd0, sum_gu1, sum_d1, wg, wu, wd, mg, mu, md, vg, vu, vd)
        return tuple(
            pl.pallas_call(
                store_kernel,
                in_specs=[pl.BlockSpec(memory_space=pltpu.VMEM)] * 9,
                out_specs=[ANY] * 9,
                out_shape=[array(t.shape, t.dtype) for t in outs],
                scratch_shapes=[sem((9,))],
                compiler_params=params(None, 2),
                name="store",
            )(*outs)
        )

    seq, whole, rows = P(("rep", "dp"), None, None), P(None, None, None), P(None, "dp", None)
    return jax.shard_map(
        step,
        mesh=mesh,
        in_specs=(seq, seq) + (whole,) * 3 + (rows,) * 6,
        out_specs=(P("rep", None, None),) * 3 + (P("rep", "dp", None),) * 6,
        check_vma=False,
    )
```

time: 755 us -> 286 us (0.38); the launches traced: 744 us -> 285 us
  matrix products: 285 us -> 0 us
  Pallas kernels: 0 us -> 284 us
  waiting for transfers between devices: 159 us -> 0 us
  starting transfers between devices: 86.9 us -> 0 us
  local copies, waits for them, and re-layouts: 79.3 us -> 0.99 us
  other arithmetic: 76.3 us -> 0 us
  loops' own time: 24.7 us -> 0 us
  between operations: 17.8 us -> 0.89 us
  blocking collectives: 15.3 us -> 0 us
    dot_general x33 -> x0, matrix products: 285 us -> none  [the longest x11 108 us: layer(): gate = jnp.dot(a, w['w_gate'], preferred_element_type=jnp.float32)]
    pallas_call x0 -> x5, Pallas kernels: none -> 284 us  [the longest x1 138 us: step(): pl.pallas_call(functools.partial(end_kernel, n, blocks, todo, groups, flo...]
    reshape x3 -> x0, waiting for transfers between devices: 115 us -> none  [step(): t.reshape(-1, *t.shape[2:])]
    dot_general x54 -> x0, starting transfers between devices: 86.8 us -> none  [the longest x18 31.2 us: matmul(): jnp.dot(a, w, preferred_element_type=jnp.float32).astype(jnp.bfloat16)]
    unnamed x59 -> x6, local copies, waits for them, and re-layouts: 68.7 us -> 0.99 us
    dot_general x54 -> x0, waiting for transfers between devices: 43.3 us -> none  [the longest x18 20.6 us: matmul(): jnp.dot(a, w, preferred_element_type=jnp.float32).astype(jnp.bfloat16)]
    dot_general x48 -> x0, other arithmetic: 26.8 us -> none  [the longest x8 10.1 us: layer(): gate = jnp.dot(a, w['w_gate'], preferred_element_type=jnp.float32)]
    convert_element_type x3 -> x0, other arithmetic: 25.9 us -> none  [the longest x1 19.7 us: layer(): (jax.nn.silu(gate) * up).astype(jnp.bfloat16)]
  transfers between devices with their start and end apart: 57 -> 0, of which waited for: 18 -> 0; matrix products, arithmetic and copies ran while one was open for 33% -> 0% of each run, Pallas kernels for 0% -> 0%
where the time goes in v3:
time: 286 us; the launch traced here: 285 us
  Pallas kernels  284 us (99%)
    pallas_call x1, Pallas kernels, step(): pl.pallas_call(functools.partial(end_kernel, n, blocks, todo, groups, flo...  138 us
    pallas_call x1, Pallas kernels, step(): pl.pallas_call(top_kernel, grid=(steps,), in_specs=[rows(d), rows(d), ANY...  58.7 us
    pallas_call x1, Pallas kernels, step(): pl.pallas_call(functools.partial(mid_kernel, n, steps, plan(hops, [(0, us...  51.3 us
    pallas_call x1, Pallas kernels, step(): pl.pallas_call(functools.partial(gu_kernel, n, blocks, plan(hops, [(0, us...  30.4 us

profile of v3, /device:TPU:22, one launch (start us, length us, event | category | flops | bytes accessed | tf_op | source)
XLA Modules:
  0.0 285.4 jit_solution(12742383330347416820)
XLA Ops:
  0.6 58.7 %top.1 = (f32[4096,2816]{1,0:T(8,128)}, bf16[4096,512]{1,0:T(8,128)(2,1)}, bf16[4096,512]{1,0:T(8,128)(2,1)}, bf16[4096,512]{1,0:T(8,128)(2,1)}, bf16[4096,2816]{1,0:T(8,128)(2,1)}, /*index=5*/bf16[1408,512]{1,0:T(8,128)(2,1)}) custom-call(bf16[4096,512]{1,0:T(8,128)(2,1)} %bitcast.4, bf16[4096,512]{1,0:T(8,128)(2,1)} %bitcast.2, bf16[2,512,1408]{2,1,0:T(8,128)(2,1)} %wg.5, ...), custom_call_target="tpu_custom_call" | custom-call | flops 41339060224 | bytes 94371840 | tf_op jit(solution)/shard_map/top/pallas_call | solution.py:497
  59.3 30.4 %gu1.1 = (bf16[512,2816]{1,0:T(8,128)(2,1)}, bf16[176,512]{1,0:T(8,128)(2,1)}) custom-call(bf16[4096,512]{1,0:T(8,128)(2,1)} %get-tuple-element.33.a_ref, bf16[4096,2816]{1,0:T(8,128)(2,1)} %get-tuple-element.31.dgu_ref.dgu1_ref, bf16[1408,512]{1,0:T(8,128)(2,1)} %get-tuple-element.34.own_hbm), custom_call_target="tpu_custom_call" | custom-call | flops 11811160064 | bytes 31457280 | tf_op jit(solution)/shard_map/gu1/pallas_call | solution.py:513
  89.7 0.0 copy-start
  89.7 0.0 copy-start.2
  89.7 51.3 %mid.1 = (bf16[4096,2816]{1,0:T(8,128)(2,1)}, bf16[1408,512]{1,0:T(8,128)(2,1)}, bf16[64,2816]{1,0:T(8,128)(2,1)}) custom-call(bf16[4096,512]{1,0:T(8,128)(2,1)} %get-tuple-element.30.h1_ref, bf16[4096,512]{1,0:T(8,128)(2,1)} %bitcast.3, bf16[4096,2816]{1,0:T(8,128)(2,1)} %get-tuple-element.31.dgu_ref.dgu1_ref, f32[4096,2816]{1,0:T(8,128)} %get-tuple-element.32.gu0_ref, ...), custom_call_target="tpu_custom_call" | custom-call | flops 23622320128 | bytes 104857600 | tf_op jit(solution)/shard_map/mid/pallas_call | solution.py:525
  141.0 0.0 copy-done
  141.0 0.0 copy-done.2
  141.0 0.0 copy-start.1
  141.0 1.0 copy-done.1
  142.0 138.4 %end.1 = (bf16[2,512,1408]{2,1,0:T(8,128)(2,1)S(1)}, bf16[2,512,1408]{2,1,0:T(8,128)(2,1)S(1)}, bf16[2,1408,512]{2,1,0:T(8,128)(2,1)S(1)}, f32[2,64,1408]{2,1,0:...) custom-call(bf16[4096,512]{1,0:T(8,128)(2,1)} %get-tuple-element.29., ...), custom_call_target="tpu_custom_call" | custom-call | flops 11811160064 | bytes 31457280 | tf_op jit(solution)/shard_map/end/pallas_call | solution.py:546
  280.4 4.8 %store.1 = (bf16[2,512,1408]{2,1,0:T(8,128)(2,1)}, bf16[2,512,1408]{2,1,0:T(8,128)(2,1)}, bf16[2,1408,512]{2,1,0:T(8,128)(2,1)}, f32[2,64,1408]{2,1,0:T(8,128)},...) custom-call(bf16[2,512,1408]{2,1,0:T(8,128)(2,1)S(1)} %get-tuple-ele, ...), custom_call_target="tpu_custom_call" | custom-call | tf_op jit(solution)/shard_map/store/pallas_call | solution.py:563
Async XLA Ops:
  89.7 51.3 %copy-start = (f32[2,64,1408]{2,1,0:T(8,128)S(1)}, f32[2,64,1408]{2,1,0:T(8,128)}, u32[]{:S(2)}) copy-start(f32[2,64,1408]{2,1,0:T(8,128)} %mg.1) | copy-start | bytes 2162692
  89.7 51.3 %copy-start.2 = (bf16[176,512]{1,0:T(8,128)(2,1)S(1)}, bf16[176,512]{1,0:T(8,128)(2,1)}, u32[]{:S(2)}) copy-start(bf16[176,512]{1,0:T(8,128)(2,1)} %get-tuple-element.39.d1) | copy-start | bytes 540676
  141.0 1.0 copy-start.1

commit v4 on v3

--- a/solution.py
+++ b/solution.py
@@ -200,15 +200,15 @@
     sig = sigmoid(gate)
     silu = gate * sig
     ds = ds.astype(BF).astype(F32)
-    return (silu * up).astype(BF), (ds * up * (sig + silu * (1.0 - sig))).astype(BF), (ds * silu).astype(BF)
-
-
-def top_kernel(x_ref, dy_ref, wg, wu, wd, gu0_ref, h1_ref, a0_ref, a1_ref, dgu1_ref, dwd_ref, wgu, wdn, s_ref, acc, sem, dsem):
+    return (ds * up * (sig + silu * (1.0 - sig))).astype(BF), (ds * silu).astype(BF)
+
+
+def top_kernel(x_ref, dy_ref, wg, wu, wd, gu0_ref, gu1_ref, s0_ref, h1_ref, a0_ref, a1_ref, dwd_ref, wgu, wdn, s_ref, acc, sem, dsem):
     i = pl.program_id(0)
     blocks = wd.shape[1] // LANES
     load_all(
         [c for k in (0, 1) for c in gate_up_copies(wg.at[k], wu.at[k], wgu.at[k], sem.at[k], blocks)]
-        + [pltpu.make_async_copy(wd.at[k], wdn.at[k], dsem.at[k]) for k in (0, 1)]
+        + [pltpu.make_async_copy(wd.at[0], wdn, dsem)]
     )
 
     @pl.when(i == 0)
@@ -216,77 +216,96 @@
         acc[...] = jnp.zeros_like(acc)
 
     rows = halves(x_ref)
+
+    def gate_up(layer, a_ref, gu_ref, to):
+        for k, c in chunks(blocks):
+            at = pl.ds(2 * LANES * k, 2 * LANES * c)
+            for r in rows:
+                gu = dot(a_ref[r, :], wgu[layer, :, at], ROWS)
+                gu_ref[r, at] = gu
+                for b in range(c):
+                    gate, up = (gu[:, (2 * b + j) * LANES : (2 * b + j + 1) * LANES] for j in (0, 1))
+                    to[r, pl.ds((k + b) * LANES, LANES)] = (gate * sigmoid(gate) * up).astype(BF)
+
     for r in rows:
         x = x_ref[r, :].astype(F32)
         a0_ref[r, :] = (x * rms_scale(x)).astype(BF)
-    for k, c in chunks(blocks):
-        at = pl.ds(2 * LANES * k, 2 * LANES * c)
-        for r in rows:
-            gu = dot(a0_ref[r, :], wgu[0, :, at], ROWS)
-            gu0_ref[r, at] = gu
-            for b in range(c):
-                gate, up = (gu[:, (2 * b + j) * LANES : (2 * b + j + 1) * LANES] for j in (0, 1))
-                s_ref[r, pl.ds((k + b) * LANES, LANES)] = (gate * sigmoid(gate) * up).astype(BF)
+    gate_up(0, a0_ref, gu0_ref, s0_ref)
     for r in rows:
-        h = x_ref[r, :].astype(F32) + dot(s_ref[r, :], wdn[0], ROWS).astype(BF).astype(F32)
+        h = x_ref[r, :].astype(F32) + dot(s0_ref[r, :], wdn[...], ROWS).astype(BF).astype(F32)
         h = h.astype(BF)
         h1_ref[r, :] = h
         h = h.astype(F32)
         a1_ref[r, :] = (h * rms_scale(h)).astype(BF)
-    for k, c in chunks(blocks):
-        at = pl.ds(2 * LANES * k, 2 * LANES * c)
-        for r in rows:
-            gu = dot(a1_ref[r, :], wgu[1, :, at], ROWS)
-            ds = dot(dy_ref[r, :], wdn[1, pl.ds(LANES * k, LANES * c), :], BY_T)
+    gate_up(1, a1_ref, gu1_ref, s_ref)
+    acc[...] += dot(s_ref[...], dy_ref[...], T_BY)
+
+    @pl.when(i == pl.num_programs(0) - 1)
+    def _():
+        dwd_ref[...] = acc[...].astype(BF)
+
+
+def back_of_chunk(dh_ref, a_ref, gu_ref, wd_ref, dgu_ref, blocks, keep):
+    i = pl.program_id(0)
+    tokens = gu_ref.shape[0]
+    part = tokens // 4
+
+    def run(c, half):
+        for k in range(4):
+            r = pl.ds(k * part, part)
+            everywhere = pl.ds(half * tokens + k * part, part)
+            ds = dot(dh_ref[everywhere, :], wd_ref[0, pl.ds(0, c * LANES), :], BY_T)
             for b in range(c):
-                gate, up = (gu[:, (2 * b + j) * LANES : (2 * b + j + 1) * LANES] for j in (0, 1))
-                s, dgate, dup = gated(gate, up, ds[:, b * LANES : (b + 1) * LANES])
-                s_ref[r, pl.ds((k + b) * LANES, LANES)] = s
-                dgu1_ref[r, pl.ds(2 * (k + b) * LANES, LANES)] = dgate
-                dgu1_ref[r, pl.ds((2 * (k + b) + 1) * LANES, LANES)] = dup
-    acc[...] += dot(s_ref[...], dy_ref[...], T_BY)
-
-    @pl.when(i == pl.num_programs(0) - 1)
-    def _():
-        dwd_ref[...] = acc[...].astype(BF)
-
-
-def gu_kernel(n, steps, todo, a_ref, dgu_ref, own_hbm, dw_ref, sum_ref, *ring):
+                at = [pl.ds((2 * b + j) * LANES, LANES) for j in (0, 1)]
+                dgate, dup = gated(gu_ref[r, at[0]], gu_ref[r, at[1]], ds[:, b * LANES : (b + 1) * LANES])
+                dgu_ref[everywhere, at[0]] = dgate
+                dgu_ref[everywhere, at[1]] = dup
+        if half == 1:
+            wide = 2 * c * LANES
+            keep(i // 2, wide, dot(a_ref[...], dgu_ref[:, pl.ds(0, wide)], T_BY).astype(BF))
+
+    whole_chunks = blocks // 2
+    for half in (0, 1):
+
+        @pl.when((i < 2 * whole_chunks) & (lax.rem(i, 2) == half))
+        def _(half=half):
+            run(2, half)
+
+        if blocks % 2:
+
+            @pl.when(i == 2 * whole_chunks + half)
+            def _(half=half):
+                run(1, half)
+
+
+def back_kernel(n, steps, todo, blocks, dh_ref, a_ref, gu_ref, wd_ref, own_hbm, dgu_ref, dw_ref, sum_ref, *ring):
     close = with_ring(n, steps, todo, ring, own_hbm, sum_ref)
-    dw_ref[...] = dot(a_ref[...], dgu_ref[...], T_BY).astype(BF)
+
+    def keep(chunk, wide, dw):
+        dw_ref[:, pl.ds(0, wide)] = dw
+
+    back_of_chunk(dh_ref, a_ref, gu_ref, wd_ref, dgu_ref, blocks, keep)
     close()
 
 
 def mid_kernel(
-    n, steps, todo, h1_ref, dy_ref, dgu1_ref, gu0_ref, wg, wu, wd, own_hbm, dgu0_ref, dwd_ref, sum_ref,
-    wgu, wdn, s_ref, dh_ref, acc, sem, dsem, *ring,
+    n, steps, todo, h1_ref, dy_ref, dgu1_ref, s0_ref, wg, wu, own_hbm, dh_ref, dwd_ref, sum_ref, wgu, acc, sem, *ring,
 ):
     i = pl.program_id(0)
-    blocks = wd.shape[1] // LANES
     close = with_ring(n, steps, todo, ring, own_hbm, sum_ref)
-    load_all(gate_up_copies(wg.at[1], wu.at[1], wgu, sem, blocks) + [pltpu.make_async_copy(wd.at[0], wdn, dsem)])
+    load_all(gate_up_copies(wg.at[1], wu.at[1], wgu, sem, wg.shape[2] // LANES))
 
     @pl.when(i == 0)
     def _():
         acc[...] = jnp.zeros_like(acc)
 
-    rows = halves(h1_ref)
-    for r in rows:
+    for r in halves(h1_ref):
         da = dot(dgu1_ref[r, :], wgu[...], BY_T).astype(BF).astype(F32)
         h = h1_ref[r, :].astype(F32)
         scale = rms_scale(h)
         back = scale * (da - h * (scale * scale * jnp.mean(da * h, -1, keepdims=True)))
         dh_ref[r, :] = (dy_ref[r, :].astype(F32) + back.astype(BF).astype(F32)).astype(BF)
-    for k, c in chunks(blocks):
-        for r in rows:
-            ds = dot(dh_ref[r, :], wdn[pl.ds(LANES * k, LANES * c), :], BY_T)
-            for b in range(c):
-                at = [pl.ds((2 * (k + b) + j) * LANES, LANES) for j in (0, 1)]
-                s, dgate, dup = gated(gu0_ref[r, at[0]], gu0_ref[r, at[1]], ds[:, b * LANES : (b + 1) * LANES])
-                s_ref[r, pl.ds((k + b) * LANES, LANES)] = s
-                dgu0_ref[r, at[0]] = dgate
-                dgu0_ref[r, at[1]] = dup
-    acc[...] += dot(s_ref[...], dh_ref[...], T_BY)
+    acc[...] += dot(s0_ref[...], dh_ref[...], T_BY)
 
     @pl.when(i == steps - 1)
     def _():
@@ -297,9 +316,9 @@
 
 def end_kernel(
     n, steps, todo, groups, count,
-    a_ref, dgu_ref, d0_hbm, gu1, d1, wg, wu, wd, mg, mu, md, vg, vu, vd,
+    dh_ref, a_ref, gu_ref, wd_ref, d0_hbm, gu1, d1, wg, wu, wd, mg, mu, md, vg, vu, vd,
     out_g, out_u, out_d, mb_g, mb_u, mb_d, vb_g, vb_u, vb_d,
-    all_g, all_u, all_d, own_gu, own_d, gbuf, dbuf, wb_g, wb_d, sq_send, sq_all, in_sem, sq_s, sq_r, ag_s, ag_r, put_sem, *ring_refs,
+    dgu_ref, all_g, all_u, all_d, own_gu, own_d, gbuf, dbuf, wb_g, wb_d, sq_send, sq_all, in_sem, sq_s, sq_r, ag_s, ag_r, put_sem, *ring_refs,
 ):
     i = pl.program_id(0)
     me = lax.axis_index("dp")
@@ -307,10 +326,11 @@
     rg, rd = mg.shape[1], md.shape[1]
     my_g = pl.ds(pl.multiple_of(me * rg, rg), rg)
     my_d = pl.ds(pl.multiple_of(me * rd, rd), rd)
-    width = dgu_ref.shape[1]
+    width = gu_ref.shape[1]
+    blocks = wg.shape[2] // LANES
     rings = [Ring(n, own_d, *ring_refs[:3])]
-    for k, (first, wide) in enumerate(groups):
-        rings.append(Ring(n, own_gu.at[:, pl.ds(first * width, wide * width)], *ring_refs[3 * k + 3 : 3 * k + 6]))
+    for k, ((first, wide), _) in enumerate(groups):
+        rings.append(Ring(n, own_gu.at[:, pl.ds(first * 2 * LANES, wide * 2 * LANES)], *ring_refs[3 * k + 3 : 3 * k + 6]))
     load = pltpu.make_async_copy(d0_hbm, own_d, in_sem.at[0])
     loads = [
         pltpu.make_async_copy(gu1, gbuf.at[1], in_sem.at[1]),
@@ -336,26 +356,29 @@
             c.start()
 
     run_plan(todo, rings, steps)
-    for k, (first, wide) in enumerate(groups):
-        if first + wide < steps:
-
-            @pl.when(i == first + wide)
+    for k, (_, at) in enumerate(groups):
+        if at < steps:
+
+            @pl.when(i == at)
             def _(k=k):
                 rings[k + 1].start()
 
-    own_gu[:, pl.ds(pl.multiple_of(i * width, width), width)] = dot(a_ref[...], dgu_ref[...], T_BY).astype(BF)
+    def keep(chunk, wide, dw):
+        own_gu[:, pl.ds(pl.multiple_of(chunk * width, width), wide)] = dw
+
+    back_of_chunk(dh_ref, a_ref, gu_ref, wd_ref, dgu_ref, blocks, keep)
 
     @pl.when(i == steps - 1)
     def _():
         for c in loads:
             c.wait()
-        for k, (first, wide) in enumerate(groups):
-            if first + wide >= steps:
+        for k, (_, at) in enumerate(groups):
+            if at >= steps:
                 rings[k + 1].start()
         rest_of_plan(todo, rings, steps)
         rings[0].finish(dbuf.at[0])
-        for k, (first, wide) in enumerate(groups):
-            rings[k + 1].finish(gbuf.at[0, :, pl.ds(first * width, wide * width)])
+        for k, ((first, wide), _) in enumerate(groups):
+            rings[k + 1].finish(gbuf.at[0, :, pl.ds(first * 2 * LANES, wide * 2 * LANES)])
 
         def squares(t):
             t = t.astype(F32)
@@ -483,7 +506,6 @@
         rows = lambda c: pl.BlockSpec((tile, c), lambda i: (i, 0))
         whole = lambda *s: pl.BlockSpec(s, lambda i: (0,) * len(s))
         once = lambda *s: pl.BlockSpec(s, lambda i: (0,) * len(s), pipeline_mode=pl.Buffered(1))
-        columns = lambda r: pl.BlockSpec((r, 2 * LANES), lambda i: (0, i))
         array = jax.ShapeDtypeStruct
         sem, vm = pltpu.SemaphoreType.DMA, pltpu.VMEM
         mm = 2 * tokens * d * ff
@@ -494,71 +516,75 @@
         def ring(row_count, cols):
             return [vm((4, hops[0], row_count, cols // 2), BF), sem((4, hops[0])), sem((4, hops[0]))]
 
-        gu0, h1, a0, a1, dgu1, dwd1 = pl.pallas_call(
+        gu0, gu1, s0, h1, a0, a1, dwd1 = pl.pallas_call(
             top_kernel,
             grid=(steps,),
             in_specs=[rows(d), rows(d), ANY, ANY, ANY],
-            out_specs=[rows(2 * ff), rows(d), rows(d), rows(d), rows(2 * ff), whole(ff, d)],
-            out_shape=[array((tokens, 2 * ff), F32)]
+            out_specs=[rows(2 * ff), rows(2 * ff), rows(ff), rows(d), rows(d), rows(d), whole(ff, d)],
+            out_shape=[array((tokens, 2 * ff), F32)] * 2
+            + [array((tokens, ff), BF)]
             + [array((tokens, d), BF)] * 3
-            + [array((tokens, 2 * ff), BF), array((ff, d), BF)],
+            + [array((ff, d), BF)],
             scratch_shapes=[
-                vm((2, d, 2 * ff), BF), vm((2, ff, d), BF), vm((tile, ff), BF), vm((ff, d), F32), sem((2, 2 * blocks)), sem((2,)),
+                vm((2, d, 2 * ff), BF), vm((ff, d), BF), vm((tile, ff), BF), vm((ff, d), F32), sem((2, 2 * blocks)), sem(()),
             ],
             compiler_params=params(),
-            cost_estimate=pl.CostEstimate(flops=7 * mm, bytes_accessed=90 << 20, transcendentals=0),
+            cost_estimate=pl.CostEstimate(flops=6 * mm, bytes_accessed=130 << 20, transcendentals=0),
             name="top",
         )(x, dy, wg, wu, wd)
 
-        dwgu1, sum_d1 = pl.pallas_call(
-            functools.partial(gu_kernel, n, blocks, plan(hops, [(0, us(rd, d // 2))], blocks, 1.7)),
-            grid=(blocks,),
-            in_specs=[once(tokens, d), columns(tokens), ANY],
-            out_specs=[columns(d), whole(rd, d)],
-            out_shape=[array((d, 2 * ff), BF), array((rd, d), BF)],
+        pieces = 2 * -(-blocks // 2)
+        of_chunk = lambda layer: [
+            once(tokens, d),
+            once(tokens, d),
+            pl.BlockSpec((tokens // 2, 4 * LANES), lambda i: (lax.rem(i, 2), i // 2)),
+            pl.BlockSpec((1, 2 * LANES, d), lambda i: (layer, i // 2, 0)),
+        ]
+        columns = lambda r: pl.BlockSpec((r, 4 * LANES), lambda i: (0, i // 2))
+        dgu1, dwgu1, sum_d1 = pl.pallas_call(
+            functools.partial(back_kernel, n, pieces, plan(hops, [(0, us(rd, d // 2))], pieces, 2.2), blocks),
+            grid=(pieces,),
+            in_specs=of_chunk(1) + [ANY],
+            out_specs=[columns(tokens), columns(d), whole(rd, d)],
+            out_shape=[array((tokens, 2 * ff), BF), array((d, 2 * ff), BF), array((rd, d), BF)],
             scratch_shapes=[vm((ff, d), BF), sem(())] + ring(rd, d),
             compiler_params=params(0),
-            cost_estimate=pl.CostEstimate(flops=2 * mm, bytes_accessed=30 << 20, transcendentals=0),
-            name="gu1",
-        )(a1, dgu1, dwd1)
-
-        dgu0, dwd0, sum_gu1 = pl.pallas_call(
-            functools.partial(mid_kernel, n, steps, plan(hops, [(0, us(rg, ff))], steps, 6.0)),
+            cost_estimate=pl.CostEstimate(flops=3 * mm, bytes_accessed=80 << 20, transcendentals=0),
+            name="back1",
+        )(dy, a1, gu1, wd, dwd1)
+
+        dh1, dwd0, sum_gu1 = pl.pallas_call(
+            functools.partial(mid_kernel, n, steps, plan(hops, [(0, us(rg, ff))], steps, 3.5)),
             grid=(steps,),
-            in_specs=[rows(d), rows(d), rows(2 * ff), rows(2 * ff), ANY, ANY, ANY, ANY],
-            out_specs=[rows(2 * ff), whole(ff, d), whole(rg, 2 * ff)],
-            out_shape=[array((tokens, 2 * ff), BF), array((ff, d), BF), array((rg, 2 * ff), BF)],
-            scratch_shapes=[
-                vm((d, 2 * ff), BF), vm((ff, d), BF), vm((tile, ff), BF), vm((tile, d), BF), vm((ff, d), F32),
-                sem((2 * blocks,)), sem(()), vm((d, 2 * ff), BF), sem(()),
-            ] + ring(rg, 2 * ff),
+            in_specs=[rows(d), rows(d), rows(2 * ff), rows(ff), ANY, ANY, ANY],
+            out_specs=[rows(d), whole(ff, d), whole(rg, 2 * ff)],
+            out_shape=[array((tokens, d), BF), array((ff, d), BF), array((rg, 2 * ff), BF)],
+            scratch_shapes=[vm((d, 2 * ff), BF), vm((ff, d), F32), sem((2 * blocks,)), vm((d, 2 * ff), BF), sem(())]
+            + ring(rg, 2 * ff),
             compiler_params=params(1),
-            cost_estimate=pl.CostEstimate(flops=4 * mm, bytes_accessed=100 << 20, transcendentals=0),
+            cost_estimate=pl.CostEstimate(flops=3 * mm, bytes_accessed=50 << 20, transcendentals=0),
             name="mid",
-        )(h1, dy, dgu1, gu0, wg, wu, wd, dwgu1)
-
-        groups, first = [], 0
-        for k in range(3):
-            wide = -(-(blocks - first) // (3 - k))
-            groups.append((first, wide))
-            first += wide
-        todo = plan(hops, [(0, us(rd, d // 2))] + [(f + w, us(rg, w * LANES)) for f, w in groups], blocks, 1.7)
+        )(h1, dy, dgu1, s0, wg, wu, dwgu1)
+
+        groups = [(k, min(4, blocks - k)) for k in range(0, blocks, 4)]
+        ready = [min(2 * -(-(f + w) // 2), pieces) for f, w in groups]
+        todo = plan(hops, [(0, us(rd, d // 2))] + [(at, us(rg, w * LANES)) for at, (_, w) in zip(ready, groups)], pieces, 2.2)
         outs = pl.pallas_call(
-            functools.partial(end_kernel, n, blocks, todo, groups, float(wg.size + wu.size + wd.size)),
-            grid=(blocks,),
-            in_specs=[once(tokens, d), columns(tokens)] + [ANY] * 12,
+            functools.partial(end_kernel, n, pieces, todo, list(zip(groups, ready)), float(wg.size + wu.size + wd.size)),
+            grid=(pieces,),
+            in_specs=of_chunk(0) + [ANY] * 12,
             out_specs=[pl.BlockSpec(memory_space=pltpu.VMEM)] * 9,
             out_shape=[vm(t.shape, BF) for t in (wg, wu, wd)] + [vm(t.shape, F32) for t in (mg, mu, md, vg, vu, vd)],
             scratch_shapes=[
-                vm(wg.shape, BF), vm(wu.shape, BF), vm(wd.shape, BF),
+                vm((tokens, 4 * LANES), BF), vm(wg.shape, BF), vm(wu.shape, BF), vm(wd.shape, BF),
                 vm((d, 2 * ff), BF), vm((ff, d), BF), vm((2, rg, 2 * ff), BF), vm((2, rd, d), BF),
                 vm((2, *mg.shape), BF), vm(md.shape, BF), vm((8, LANES), F32), vm((n - 1, 8, LANES), F32),
                 sem((12,)), sem((n - 1,)), sem((n - 1,)), sem((4, 4, hops[0])), sem((4, 4, hops[0])), sem((4, 4, hops[0] + 1)),
             ] + ring(rd, d) + [r for _, w in groups for r in ring(rg, w * 2 * LANES)],
-            compiler_params=params(2, 40),
+            compiler_params=params(2, 48),
             cost_estimate=pl.CostEstimate(flops=2 * mm, bytes_accessed=30 << 20, transcendentals=0),
             name="end",
-        )(a0, dgu0, dwd0, sum_gu1, sum_d1, wg, wu, wd, mg, mu, md, vg, vu, vd)
+        )(dh1, a0, gu0, wd, dwd0, sum_gu1, sum_d1, wg, wu, wd, mg, mu, md, vg, vu, vd)
         return tuple(
             pl.pallas_call(
                 store_kernel,

time: 286 us -> 297 us (1.038)
  Pallas kernels: 284 us -> 295 us
    pallas_call x2, Pallas kernels: 169 us -> 201 us  [the longest x1 148 us: step(): pl.pallas_call(functools.partial(end_kernel, n, pieces, todo, list(zip(gr...]
    pallas_call x1, Pallas kernels: 51.3 us -> 36.9 us  [step(): pl.pallas_call(functools.partial(mid_kernel, n, steps, plan(hops, [(0, us...]
    pallas_call x1, Pallas kernels: 58.7 us -> 52.2 us  [step(): pl.pallas_call(top_kernel, grid=(steps,), in_specs=[rows(d), rows(d), ANY...]
where the time goes in v4:
time: 297 us; the launch traced here: 296 us
  Pallas kernels  295 us (99%)
    pallas_call x1, Pallas kernels, step(): pl.pallas_call(functools.partial(end_kernel, n, pieces, todo, list(zip(gr...  148 us
    pallas_call x1, Pallas kernels, step(): pl.pallas_call(functools.partial(back_kernel, n, pieces, plan(hops, [(0,...  53 us
    pallas_call x1, Pallas kernels, step(): pl.pallas_call(top_kernel, grid=(steps,), in_specs=[rows(d), rows(d), ANY...  52.2 us
    pallas_call x1, Pallas kernels, step(): pl.pallas_call(functools.partial(mid_kernel, n, steps, plan(hops, [(0, us...  36.9 us

profile of v4, /device:TPU:22, one launch (start us, length us, event | category | flops | bytes accessed | tf_op | source)
XLA Modules:
  0.0 296.2 jit_solution(3283993685531957347)
XLA Ops:
  0.6 52.2 %top.1 = (f32[4096,2816]{1,0:T(8,128)}, f32[4096,2816]{1,0:T(8,128)}, bf16[4096,1408]{1,0:T(8,128)(2,1)}, bf16[4096,512]{1,0:T(8,128)(2,1)}, bf16[4096,512]{1,0:...) custom-call(bf16[4096,512]{1,0:T(8,128)(2,1)} %bitcast.2, bf16[4096,512]{1,0:T(8,128)(2,1)} %bitcast.3, ...), custom_call_target="tpu_custom_call" | custom-call | flops 35433480192 | bytes 136314880 | tf_op jit(solution)/shard_map/top/pallas_call | solution.py:519
  52.9 53.0 %back1.1 = (bf16[4096,2816]{1,0:T(8,128)(2,1)}, bf16[512,2816]{1,0:T(8,128)(2,1)}, bf16[176,512]{1,0:T(8,128)(2,1)}) custom-call(bf16[4096,512]{1,0:T(8,128)(2,1)} %bitcast.4, bf16[4096,512]{1,0:T(8,128)(2,1)} %get-tuple-element.32.a_ref, f32[4096,2816]{1,0:T(8,128)} %get-tuple-element.33.gu_ref, bf16[2,1408,512]{2,1,0:T(8,128)(2,1)} %wd.3, ...), custom_call_target="tpu_custom_call" | custom-call | flops 17716740096 | bytes 83886080 | tf_op jit(solution)/shard_map/back1/pallas_call | solution.py:544
  105.8 36.9 %mid.1 = (bf16[4096,512]{1,0:T(8,128)(2,1)}, bf16[1408,512]{1,0:T(8,128)(2,1)}, bf16[64,2816]{1,0:T(8,128)(2,1)}) custom-call(bf16[4096,512]{1,0:T(8,128)(2,1)} %get-tuple-element.31.h1_ref, bf16[4096,512]{1,0:T(8,128)(2,1)} %bitcast.5, bf16[4096,2816]{1,0:T(8,128)(2,1)} %get-tuple-element.35.dgu1_ref, bf16[4096,1408]{1,0:T(8,128)(2,1)} %get-tuple-element.36.s0_ref, ...), custom_call_target="tpu_custom_call" | custom-call | flops 17716740096 | bytes 52428800 | tf_op jit(solution)/shard_map/mid/pallas_call | solution.py:556
  142.8 148.4 %end.1 = (bf16[2,512,1408]{2,1,0:T(8,128)(2,1)S(1)}, bf16[2,512,1408]{2,1,0:T(8,128)(2,1)S(1)}, bf16[2,1408,512]{2,1,0:T(8,128)(2,1)S(1)}, f32[2,64,1408]{2,1,0:...) custom-call(bf16[4096,512]{1,0:T(8,128)(2,1)} %get-tuple-element.38., ...), custom_call_target="tpu_custom_call" | custom-call | flops 11811160064 | bytes 31457280 | tf_op jit(solution)/shard_map/end/pallas_call | solution.py:572
  291.2 4.8 %store.1 = (bf16[2,512,1408]{2,1,0:T(8,128)(2,1)}, bf16[2,512,1408]{2,1,0:T(8,128)(2,1)}, bf16[2,1408,512]{2,1,0:T(8,128)(2,1)}, f32[2,64,1408]{2,1,0:T(8,128)},...) custom-call(bf16[2,512,1408]{2,1,0:T(8,128)(2,1)S(1)} %get-tuple-ele, ...), custom_call_target="tpu_custom_call" | custom-call | tf_op jit(solution)/shard_map/store/pallas_call | solution.py:589

commit v5 on v4

--- a/solution.py
+++ b/solution.py
@@ -200,15 +200,15 @@
     sig = sigmoid(gate)
     silu = gate * sig
     ds = ds.astype(BF).astype(F32)
-    return (ds * up * (sig + silu * (1.0 - sig))).astype(BF), (ds * silu).astype(BF)
-
-
-def top_kernel(x_ref, dy_ref, wg, wu, wd, gu0_ref, gu1_ref, s0_ref, h1_ref, a0_ref, a1_ref, dwd_ref, wgu, wdn, s_ref, acc, sem, dsem):
+    return (silu * up).astype(BF), (ds * up * (sig + silu * (1.0 - sig))).astype(BF), (ds * silu).astype(BF)
+
+
+def top_kernel(x_ref, dy_ref, wg, wu, wd, gu0_ref, s0_ref, h1_ref, a0_ref, a1_ref, dgu1_ref, dwd_ref, wgu, wdn, s_ref, acc, sem, dsem):
     i = pl.program_id(0)
     blocks = wd.shape[1] // LANES
     load_all(
         [c for k in (0, 1) for c in gate_up_copies(wg.at[k], wu.at[k], wgu.at[k], sem.at[k], blocks)]
-        + [pltpu.make_async_copy(wd.at[0], wdn, dsem)]
+        + [pltpu.make_async_copy(wd.at[k], wdn.at[k], dsem.at[k]) for k in (0, 1)]
     )
 
     @pl.when(i == 0)
@@ -216,28 +216,34 @@
         acc[...] = jnp.zeros_like(acc)
 
     rows = halves(x_ref)
-
-    def gate_up(layer, a_ref, gu_ref, to):
-        for k, c in chunks(blocks):
-            at = pl.ds(2 * LANES * k, 2 * LANES * c)
-            for r in rows:
-                gu = dot(a_ref[r, :], wgu[layer, :, at], ROWS)
-                gu_ref[r, at] = gu
-                for b in range(c):
-                    gate, up = (gu[:, (2 * b + j) * LANES : (2 * b + j + 1) * LANES] for j in (0, 1))
-                    to[r, pl.ds((k + b) * LANES, LANES)] = (gate * sigmoid(gate) * up).astype(BF)
-
     for r in rows:
         x = x_ref[r, :].astype(F32)
         a0_ref[r, :] = (x * rms_scale(x)).astype(BF)
-    gate_up(0, a0_ref, gu0_ref, s0_ref)
+    for k, c in chunks(blocks):
+        at = pl.ds(2 * LANES * k, 2 * LANES * c)
+        for r in rows:
+            gu = dot(a0_ref[r, :], wgu[0, :, at], ROWS)
+            gu0_ref[r, at] = gu
+            for b in range(c):
+                gate, up = (gu[:, (2 * b + j) * LANES : (2 * b + j + 1) * LANES] for j in (0, 1))
+                s0_ref[r, pl.ds((k + b) * LANES, LANES)] = (gate * sigmoid(gate) * up).astype(BF)
     for r in rows:
-        h = x_ref[r, :].astype(F32) + dot(s0_ref[r, :], wdn[...], ROWS).astype(BF).astype(F32)
+        h = x_ref[r, :].astype(F32) + dot(s0_ref[r, :], wdn[0], ROWS).astype(BF).astype(F32)
         h = h.astype(BF)
         h1_ref[r, :] = h
         h = h.astype(F32)
         a1_ref[r, :] = (h * rms_scale(h)).astype(BF)
-    gate_up(1, a1_ref, gu1_ref, s_ref)
+    for k, c in chunks(blocks):
+        at = pl.ds(2 * LANES * k, 2 * LANES * c)
+        for r in rows:
+            gu = dot(a1_ref[r, :], wgu[1, :, at], ROWS)
+            ds = dot(dy_ref[r, :], wdn[1, pl.ds(LANES * k, LANES * c), :], BY_T)
+            for b in range(c):
+                gate, up = (gu[:, (2 * b + j) * LANES : (2 * b + j + 1) * LANES] for j in (0, 1))
+                s, dgate, dup = gated(gate, up, ds[:, b * LANES : (b + 1) * LANES])
+                s_ref[r, pl.ds((k + b) * LANES, LANES)] = s
+                dgu1_ref[r, pl.ds(2 * (k + b) * LANES, LANES)] = dgate
+                dgu1_ref[r, pl.ds((2 * (k + b) + 1) * LANES, LANES)] = dup
     acc[...] += dot(s_ref[...], dy_ref[...], T_BY)
 
     @pl.when(i == pl.num_programs(0) - 1)
@@ -245,24 +251,38 @@
         dwd_ref[...] = acc[...].astype(BF)
 
 
-def back_of_chunk(dh_ref, a_ref, gu_ref, wd_ref, dgu_ref, blocks, keep):
+def back_of_chunk(dh_ref, a_ref, gu_ref, wd_ref, dgu_ref, acc, blocks, keep):
     i = pl.program_id(0)
     tokens = gu_ref.shape[0]
     part = tokens // 4
 
     def run(c, half):
-        for k in range(4):
-            r = pl.ds(k * part, part)
-            everywhere = pl.ds(half * tokens + k * part, part)
+        wide = pl.ds(0, 2 * c * LANES)
+
+        def hidden(k):
+            r, everywhere = pl.ds(k * part, part), pl.ds(half * tokens + k * part, part)
             ds = dot(dh_ref[everywhere, :], wd_ref[0, pl.ds(0, c * LANES), :], BY_T)
             for b in range(c):
                 at = [pl.ds((2 * b + j) * LANES, LANES) for j in (0, 1)]
-                dgate, dup = gated(gu_ref[r, at[0]], gu_ref[r, at[1]], ds[:, b * LANES : (b + 1) * LANES])
-                dgu_ref[everywhere, at[0]] = dgate
-                dgu_ref[everywhere, at[1]] = dup
+                _, dgate, dup = gated(gu_ref[r, at[0]], gu_ref[r, at[1]], ds[:, b * LANES : (b + 1) * LANES])
+                dgu_ref[r, at[0]] = dgate
+                dgu_ref[r, at[1]] = dup
+
+        def weights(k):
+            r, everywhere = pl.ds(k * part, part), pl.ds(half * tokens + k * part, part)
+            term = dot(a_ref[everywhere, :], dgu_ref[r, wide], T_BY)
+            if half == 0 and k == 0:
+                acc[:, wide] = term
+            else:
+                acc[:, wide] += term
+
+        for k in range(4):
+            hidden(k)
+            if k > 0:
+                weights(k - 1)
+        weights(3)
         if half == 1:
-            wide = 2 * c * LANES
-            keep(i // 2, wide, dot(a_ref[...], dgu_ref[:, pl.ds(0, wide)], T_BY).astype(BF))
+            keep(i // 2, 2 * c * LANES, acc[:, wide].astype(BF))
 
     whole_chunks = blocks // 2
     for half in (0, 1):
@@ -278,20 +298,45 @@
                 run(1, half)
 
 
-def back_kernel(n, steps, todo, blocks, dh_ref, a_ref, gu_ref, wd_ref, own_hbm, dgu_ref, dw_ref, sum_ref, *ring):
-    close = with_ring(n, steps, todo, ring, own_hbm, sum_ref)
-
-    def keep(chunk, wide, dw):
-        dw_ref[:, pl.ds(0, wide)] = dw
-
-    back_of_chunk(dh_ref, a_ref, gu_ref, wd_ref, dgu_ref, blocks, keep)
-    close()
+def gu_kernel(n, steps, todo, early, a_ref, dgu_ref, own_hbm, dw_ref, sum_ref, early_ref, own, load_sem, own_gu, *ring_refs):
+    i = pl.program_id(0)
+    width = dgu_ref.shape[1]
+    rings = [Ring(n, own, *ring_refs[:3]), Ring(n, own_gu, *ring_refs[3:])]
+    load = pltpu.make_async_copy(own_hbm, own, load_sem)
+
+    @pl.when(i == 0)
+    def _():
+        load.start()
+        greet(n, (1, -1))
+        load.wait()
+        rings[0].start()
+
+    run_plan(todo, rings, steps)
+
+    @pl.when(i == early)
+    def _():
+        rings[1].start()
+
+    dw = dot(a_ref[...], dgu_ref[...], T_BY).astype(BF)
+    dw_ref[...] = dw
+
+    @pl.when(i < early)
+    def _():
+        own_gu[:, pl.ds(pl.multiple_of(i * width, width), width)] = dw_ref[...]
+
+    @pl.when(i == steps - 1)
+    def _():
+        rest_of_plan(todo, rings, steps)
+        rings[0].finish(sum_ref)
+        rings[1].finish(early_ref)
 
 
 def mid_kernel(
     n, steps, todo, h1_ref, dy_ref, dgu1_ref, s0_ref, wg, wu, own_hbm, dh_ref, dwd_ref, sum_ref, wgu, acc, sem, *ring,
 ):
     i = pl.program_id(0)
+    own_cols = ring[0].shape[1]
+    own_hbm = own_hbm.at[:, pl.ds(wgu.shape[1] - own_cols, own_cols)]
     close = with_ring(n, steps, todo, ring, own_hbm, sum_ref)
     load_all(gate_up_copies(wg.at[1], wu.at[1], wgu, sem, wg.shape[2] // LANES))
 
@@ -316,9 +361,9 @@
 
 def end_kernel(
     n, steps, todo, groups, count,
-    dh_ref, a_ref, gu_ref, wd_ref, d0_hbm, gu1, d1, wg, wu, wd, mg, mu, md, vg, vu, vd,
+    dh_ref, a_ref, gu_ref, wd_ref, d0_hbm, gu1_early, gu1, d1, wg, wu, wd, mg, mu, md, vg, vu, vd,
     out_g, out_u, out_d, mb_g, mb_u, mb_d, vb_g, vb_u, vb_d,
-    dgu_ref, all_g, all_u, all_d, own_gu, own_d, gbuf, dbuf, wb_g, wb_d, sq_send, sq_all, in_sem, sq_s, sq_r, ag_s, ag_r, put_sem, *ring_refs,
+    dgu_ref, acc, all_g, all_u, all_d, own_gu, own_d, gbuf, dbuf, wb_g, wb_d, sq_send, sq_all, in_sem, sq_s, sq_r, ag_s, ag_r, put_sem, *ring_refs,
 ):
     i = pl.program_id(0)
     me = lax.axis_index("dp")
@@ -327,13 +372,15 @@
     my_g = pl.ds(pl.multiple_of(me * rg, rg), rg)
     my_d = pl.ds(pl.multiple_of(me * rd, rd), rd)
     width = gu_ref.shape[1]
+    early = gu1_early.shape[1]
     blocks = wg.shape[2] // LANES
     rings = [Ring(n, own_d, *ring_refs[:3])]
     for k, ((first, wide), _) in enumerate(groups):
         rings.append(Ring(n, own_gu.at[:, pl.ds(first * 2 * LANES, wide * 2 * LANES)], *ring_refs[3 * k + 3 : 3 * k + 6]))
     load = pltpu.make_async_copy(d0_hbm, own_d, in_sem.at[0])
     loads = [
-        pltpu.make_async_copy(gu1, gbuf.at[1], in_sem.at[1]),
+        pltpu.make_async_copy(gu1_early, gbuf.at[1, :, pl.ds(0, early)], in_sem.at[12]),
+        pltpu.make_async_copy(gu1, gbuf.at[1, :, pl.ds(early, gbuf.shape[2] - early)], in_sem.at[1]),
         pltpu.make_async_copy(d1, dbuf.at[1], in_sem.at[2]),
         pltpu.make_async_copy(mg, mb_g, in_sem.at[3]),
         pltpu.make_async_copy(mu, mb_u, in_sem.at[4]),
@@ -366,7 +413,7 @@
     def keep(chunk, wide, dw):
         own_gu[:, pl.ds(pl.multiple_of(chunk * width, width), wide)] = dw
 
-    back_of_chunk(dh_ref, a_ref, gu_ref, wd_ref, dgu_ref, blocks, keep)
+    back_of_chunk(dh_ref, a_ref, gu_ref, wd_ref, dgu_ref, acc, blocks, keep)
 
     @pl.when(i == steps - 1)
     def _():
@@ -516,20 +563,19 @@
         def ring(row_count, cols):
             return [vm((4, hops[0], row_count, cols // 2), BF), sem((4, hops[0])), sem((4, hops[0]))]
 
-        gu0, gu1, s0, h1, a0, a1, dwd1 = pl.pallas_call(
+        gu0, s0, h1, a0, a1, dgu1, dwd1 = pl.pallas_call(
             top_kernel,
             grid=(steps,),
             in_specs=[rows(d), rows(d), ANY, ANY, ANY],
-            out_specs=[rows(2 * ff), rows(2 * ff), rows(ff), rows(d), rows(d), rows(d), whole(ff, d)],
-            out_shape=[array((tokens, 2 * ff), F32)] * 2
-            + [array((tokens, ff), BF)]
+            out_specs=[rows(2 * ff), rows(ff), rows(d), rows(d), rows(d), rows(2 * ff), whole(ff, d)],
+            out_shape=[array((tokens, 2 * ff), F32), array((tokens, ff), BF)]
             + [array((tokens, d), BF)] * 3
-            + [array((ff, d), BF)],
+            + [array((tokens, 2 * ff), BF), array((ff, d), BF)],
             scratch_shapes=[
-                vm((2, d, 2 * ff), BF), vm((ff, d), BF), vm((tile, ff), BF), vm((ff, d), F32), sem((2, 2 * blocks)), sem(()),
+                vm((2, d, 2 * ff), BF), vm((2, ff, d), BF), vm((tile, ff), BF), vm((ff, d), F32), sem((2, 2 * blocks)), sem((2,)),
             ],
             compiler_params=params(),
-            cost_estimate=pl.CostEstimate(flops=6 * mm, bytes_accessed=130 << 20, transcendentals=0),
+            cost_estimate=pl.CostEstimate(flops=7 * mm, bytes_accessed=100 << 20, transcendentals=0),
             name="top",
         )(x, dy, wg, wu, wd)
 
@@ -540,27 +586,30 @@
             pl.BlockSpec((tokens // 2, 4 * LANES), lambda i: (lax.rem(i, 2), i // 2)),
             pl.BlockSpec((1, 2 * LANES, d), lambda i: (layer, i // 2, 0)),
         ]
-        columns = lambda r: pl.BlockSpec((r, 4 * LANES), lambda i: (0, i // 2))
-        dgu1, dwgu1, sum_d1 = pl.pallas_call(
-            functools.partial(back_kernel, n, pieces, plan(hops, [(0, us(rd, d // 2))], pieces, 2.2), blocks),
-            grid=(pieces,),
-            in_specs=of_chunk(1) + [ANY],
-            out_specs=[columns(tokens), columns(d), whole(rd, d)],
-            out_shape=[array((tokens, 2 * ff), BF), array((d, 2 * ff), BF), array((rd, d), BF)],
-            scratch_shapes=[vm((ff, d), BF), sem(())] + ring(rd, d),
+        columns = lambda r: pl.BlockSpec((r, 2 * LANES), lambda i: (0, i))
+        early = 3
+        todo = plan(hops, [(0, us(rd, d // 2)), (early, us(rg, early * LANES))], blocks, 1.7)
+        dwgu1, sum_d1, sum_early = pl.pallas_call(
+            functools.partial(gu_kernel, n, blocks, todo, early),
+            grid=(blocks,),
+            in_specs=[once(tokens, d), columns(tokens), ANY],
+            out_specs=[columns(d), whole(rd, d), whole(rg, 2 * LANES * early)],
+            out_shape=[array((d, 2 * ff), BF), array((rd, d), BF), array((rg, 2 * LANES * early), BF)],
+            scratch_shapes=[vm((ff, d), BF), sem(()), vm((d, 2 * LANES * early), BF)] + ring(rd, d) + ring(rg, 2 * LANES * early),
             compiler_params=params(0),
-            cost_estimate=pl.CostEstimate(flops=3 * mm, bytes_accessed=80 << 20, transcendentals=0),
-            name="back1",
-        )(dy, a1, gu1, wd, dwd1)
+            cost_estimate=pl.CostEstimate(flops=2 * mm, bytes_accessed=30 << 20, transcendentals=0),
+            name="gu1",
+        )(a1, dgu1, dwd1)
 
         dh1, dwd0, sum_gu1 = pl.pallas_call(
-            functools.partial(mid_kernel, n, steps, plan(hops, [(0, us(rg, ff))], steps, 3.5)),
+            functools.partial(mid_kernel, n, steps, plan(hops, [(0, us(rg, ff - early * LANES))], steps, 3.5)),
             grid=(steps,),
             in_specs=[rows(d), rows(d), rows(2 * ff), rows(ff), ANY, ANY, ANY],
-            out_specs=[rows(d), whole(ff, d), whole(rg, 2 * ff)],
-            out_shape=[array((tokens, d), BF), array((ff, d), BF), array((rg, 2 * ff), BF)],
-            scratch_shapes=[vm((d, 2 * ff), BF), vm((ff, d), F32), sem((2 * blocks,)), vm((d, 2 * ff), BF), sem(())]
-            + ring(rg, 2 * ff),
+            out_specs=[rows(d), whole(ff, d), whole(rg, 2 * ff - 2 * LANES * early)],
+            out_shape=[array((tokens, d), BF), array((ff, d), BF), array((rg, 2 * ff - 2 * LANES * early), BF)],
+            scratch_shapes=[vm((d, 2 * ff), BF), vm((ff, d), F32), sem((2 * blocks,))]
+            + [vm((d, 2 * ff - 2 * LANES * early), BF), sem(())]
+            + ring(rg, 2 * ff - 2 * LANES * early),
             compiler_params=params(1),
             cost_estimate=pl.CostEstimate(flops=3 * mm, bytes_accessed=50 << 20, transcendentals=0),
             name="mid",
@@ -568,23 +617,23 @@
 
         groups = [(k, min(4, blocks - k)) for k in range(0, blocks, 4)]
         ready = [min(2 * -(-(f + w) // 2), pieces) for f, w in groups]
-        todo = plan(hops, [(0, us(rd, d // 2))] + [(at, us(rg, w * LANES)) for at, (_, w) in zip(ready, groups)], pieces, 2.2)
+        todo = plan(hops, [(0, us(rd, d // 2))] + [(at, us(rg, w * LANES)) for at, (_, w) in zip(ready, groups)], pieces, 2.8)
         outs = pl.pallas_call(
             functools.partial(end_kernel, n, pieces, todo, list(zip(groups, ready)), float(wg.size + wu.size + wd.size)),
             grid=(pieces,),
-            in_specs=of_chunk(0) + [ANY] * 12,
+            in_specs=of_chunk(0) + [ANY] * 13,
             out_specs=[pl.BlockSpec(memory_space=pltpu.VMEM)] * 9,
             out_shape=[vm(t.shape, BF) for t in (wg, wu, wd)] + [vm(t.shape, F32) for t in (mg, mu, md, vg, vu, vd)],
             scratch_shapes=[
-                vm((tokens, 4 * LANES), BF), vm(wg.shape, BF), vm(wu.shape, BF), vm(wd.shape, BF),
+                vm((tokens // 2, 4 * LANES), BF), vm((d, 4 * LANES), F32), vm(wg.shape, BF), vm(wu.shape, BF), vm(wd.shape, BF),
                 vm((d, 2 * ff), BF), vm((ff, d), BF), vm((2, rg, 2 * ff), BF), vm((2, rd, d), BF),
                 vm((2, *mg.shape), BF), vm(md.shape, BF), vm((8, LANES), F32), vm((n - 1, 8, LANES), F32),
-                sem((12,)), sem((n - 1,)), sem((n - 1,)), sem((4, 4, hops[0])), sem((4, 4, hops[0])), sem((4, 4, hops[0] + 1)),
+                sem((13,)), sem((n - 1,)), sem((n - 1,)), sem((4, 4, hops[0])), sem((4, 4, hops[0])), sem((4, 4, hops[0] + 1)),
             ] + ring(rd, d) + [r for _, w in groups for r in ring(rg, w * 2 * LANES)],
             compiler_params=params(2, 48),
             cost_estimate=pl.CostEstimate(flops=2 * mm, bytes_accessed=30 << 20, transcendentals=0),
             name="end",
-        )(dh1, a0, gu0, wd, dwd0, sum_gu1, sum_d1, wg, wu, wd, mg, mu, md, vg, vu, vd)
+        )(dh1, a0, gu0, wd, dwd0, sum_early, sum_gu1, sum_d1, wg, wu, wd, mg, mu, md, vg, vu, vd)
         return tuple(
             pl.pallas_call(
                 store_kernel,

time: 297 us -> 278 us (0.936)
  Pallas kernels: 295 us -> 277 us
    pallas_call x1, Pallas kernels: 53 us -> 37.5 us  [step(): pl.pallas_call(functools.partial(gu_kernel, n, blocks, todo, early), grid...]
    pallas_call x1, Pallas kernels: 52.2 us -> 59.2 us  [step(): pl.pallas_call(top_kernel, grid=(steps,), in_specs=[rows(d), rows(d), ANY...]
    pallas_call x1, Pallas kernels: 36.9 us -> 31.5 us  [step(): pl.pallas_call(functools.partial(mid_kernel, n, steps, plan(hops, [(0, us...]
    pallas_call x1, Pallas kernels: 148 us -> 144 us  [step(): pl.pallas_call(functools.partial(end_kernel, n, pieces, todo, list(zip(gr...]
where the time goes in v5:
time: 278 us
  Pallas kernels  277 us (100%)
    pallas_call x1, Pallas kernels, step(): pl.pallas_call(functools.partial(end_kernel, n, pieces, todo, list(zip(gr...  144 us
    pallas_call x1, Pallas kernels, step(): pl.pallas_call(top_kernel, grid=(steps,), in_specs=[rows(d), rows(d), ANY...  59.2 us
    pallas_call x1, Pallas kernels, step(): pl.pallas_call(functools.partial(gu_kernel, n, blocks, todo, early), grid...  37.5 us
    pallas_call x1, Pallas kernels, step(): pl.pallas_call(functools.partial(mid_kernel, n, steps, plan(hops, [(0, us...  31.5 us

profile of v5, /device:TPU:22, one launch (start us, length us, event | category | flops | bytes accessed | tf_op | source)
XLA Modules:
  0.0 278.0 jit_solution(5328916710118410742)
XLA Ops:
  0.6 59.2 %top.1 = (f32[4096,2816]{1,0:T(8,128)}, bf16[4096,1408]{1,0:T(8,128)(2,1)}, bf16[4096,512]{1,0:T(8,128)(2,1)}, bf16[4096,512]{1,0:T(8,128)(2,1)}, bf16[4096,512]...) custom-call(bf16[4096,512]{1,0:T(8,128)(2,1)} %bitcast.2, bf16[4096,512]{1,0:T(8,128)(2,1)} %bitcast.3, ...), custom_call_target="tpu_custom_call" | custom-call | flops 41339060224 | bytes 104857600 | tf_op jit(solution)/shard_map/top/pallas_call | solution.py:566
  59.8 37.5 %gu1.1 = (bf16[512,2816]{1,0:T(8,128)(2,1)}, bf16[176,512]{1,0:T(8,128)(2,1)}, bf16[64,768]{1,0:T(8,128)(2,1)}) custom-call(bf16[4096,512]{1,0:T(8,128)(2,1)} %get-tuple-element.34.a_ref, bf16[4096,2816]{1,0:T(8,128)(2,1)} %get-tuple-element.32.dgu_ref.dgu1_ref, bf16[1408,512]{1,0:T(8,128)(2,1)} %get-tuple-element.35.own_hbm), custom_call_target="tpu_custom_call" | custom-call | flops 11811160064 | bytes 31457280 | tf_op jit(solution)/shard_map/gu1/pallas_call | solution.py:592
  97.4 31.5 %mid.1 = (bf16[4096,512]{1,0:T(8,128)(2,1)}, bf16[1408,512]{1,0:T(8,128)(2,1)}, bf16[64,2048]{1,0:T(8,128)(2,1)}) custom-call(bf16[4096,512]{1,0:T(8,128)(2,1)} %get-tuple-element.31.h1_ref, bf16[4096,512]{1,0:T(8,128)(2,1)} %bitcast.4, bf16[4096,2816]{1,0:T(8,128)(2,1)} %get-tuple-element.32.dgu_ref.dgu1_ref, bf16[4096,1408]{1,0:T(8,128)(2,1)} %get-tuple-element.33.s0_ref, ...), custom_call_target="tpu_custom_call" | custom-call | flops 17716740096 | bytes 52428800 | tf_op jit(solution)/shard_map/mid/pallas_call | solution.py:604
  128.9 144.1 %end.1 = (bf16[2,512,1408]{2,1,0:T(8,128)(2,1)S(1)}, bf16[2,512,1408]{2,1,0:T(8,128)(2,1)S(1)}, bf16[2,1408,512]{2,1,0:T(8,128)(2,1)S(1)}, f32[2,64,1408]{2,1,0:...) custom-call(bf16[4096,512]{1,0:T(8,128)(2,1)} %get-tuple-element.37., ...), custom_call_target="tpu_custom_call" | custom-call | flops 11811160064 | bytes 31457280 | tf_op jit(solution)/shard_map/end/pallas_call | solution.py:621
  273.0 4.8 %store.1 = (bf16[2,512,1408]{2,1,0:T(8,128)(2,1)}, bf16[2,512,1408]{2,1,0:T(8,128)(2,1)}, bf16[2,1408,512]{2,1,0:T(8,128)(2,1)}, f32[2,64,1408]{2,1,0:T(8,128)},...) custom-call(bf16[2,512,1408]{2,1,0:T(8,128)(2,1)S(1)} %get-tuple-ele, ...), custom_call_target="tpu_custom_call" | custom-call | tf_op jit(solution)/shard_map/store/pallas_call | solution.py:638

commit v6 on v5

--- a/solution.py
+++ b/solution.py
@@ -142,10 +142,9 @@
             rings[r].handle(pair)
 
 
-def with_ring(n, steps, todo, refs, own_hbm, out):
-    own, load_sem, recv, send_sem, recv_sem = refs
+def with_rings(n, steps, todo, own, load_sem, columns, refs, own_hbm, out):
     i = pl.program_id(0)
-    ring = Ring(n, own, recv, send_sem, recv_sem)
+    rings = [Ring(n, own.at[:, pl.ds(*c)], *refs[3 * k : 3 * k + 3]) for k, c in enumerate(columns)]
     load = pltpu.make_async_copy(own_hbm, own, load_sem)
 
     @pl.when(i == 0)
@@ -153,15 +152,17 @@
         load.start()
         greet(n, (1, -1))
         load.wait()
-        ring.start()
-
-    run_plan(todo, [ring], steps)
+        for ring in rings:
+            ring.start()
+
+    run_plan(todo, rings, steps)
 
     def close():
         @pl.when(i == steps - 1)
         def _():
-            rest_of_plan(todo, [ring], steps)
-            ring.finish(out)
+            rest_of_plan(todo, rings, steps)
+            for ring, c in zip(rings, columns):
+                ring.finish(out.at[:, pl.ds(*c)])
 
     return close
 
@@ -298,46 +299,18 @@
                 run(1, half)
 
 
-def gu_kernel(n, steps, todo, early, a_ref, dgu_ref, own_hbm, dw_ref, sum_ref, early_ref, own, load_sem, own_gu, *ring_refs):
-    i = pl.program_id(0)
-    width = dgu_ref.shape[1]
-    rings = [Ring(n, own, *ring_refs[:3]), Ring(n, own_gu, *ring_refs[3:])]
-    load = pltpu.make_async_copy(own_hbm, own, load_sem)
-
-    @pl.when(i == 0)
-    def _():
-        load.start()
-        greet(n, (1, -1))
-        load.wait()
-        rings[0].start()
-
-    run_plan(todo, rings, steps)
-
-    @pl.when(i == early)
-    def _():
-        rings[1].start()
-
-    dw = dot(a_ref[...], dgu_ref[...], T_BY).astype(BF)
-    dw_ref[...] = dw
-
-    @pl.when(i < early)
-    def _():
-        own_gu[:, pl.ds(pl.multiple_of(i * width, width), width)] = dw_ref[...]
-
-    @pl.when(i == steps - 1)
-    def _():
-        rest_of_plan(todo, rings, steps)
-        rings[0].finish(sum_ref)
-        rings[1].finish(early_ref)
+def gu_kernel(n, steps, todo, a_ref, dgu_ref, own_hbm, dw_ref, sum_ref, own, load_sem, *ring):
+    close = with_rings(n, steps, todo, own, load_sem, ((0, own.shape[1]),), ring, own_hbm, sum_ref)
+    dw_ref[...] = dot(a_ref[...], dgu_ref[...], T_BY).astype(BF)
+    close()
 
 
 def mid_kernel(
-    n, steps, todo, h1_ref, dy_ref, dgu1_ref, s0_ref, wg, wu, own_hbm, dh_ref, dwd_ref, sum_ref, wgu, acc, sem, *ring,
+    n, steps, todo, columns, h1_ref, dy_ref, dgu1_ref, s0_ref, wg, wu, own_hbm, dh_ref, dwd_ref, sum_ref,
+    wgu, acc, sem, own, load_sem, *ring,
 ):
     i = pl.program_id(0)
-    own_cols = ring[0].shape[1]
-    own_hbm = own_hbm.at[:, pl.ds(wgu.shape[1] - own_cols, own_cols)]
-    close = with_ring(n, steps, todo, ring, own_hbm, sum_ref)
+    close = with_rings(n, steps, todo, own, load_sem, columns, ring, own_hbm, sum_ref)
     load_all(gate_up_copies(wg.at[1], wu.at[1], wgu, sem, wg.shape[2] // LANES))
 
     @pl.when(i == 0)
@@ -361,9 +334,9 @@
 
 def end_kernel(
     n, steps, todo, groups, count,
-    dh_ref, a_ref, gu_ref, wd_ref, d0_hbm, gu1_early, gu1, d1, wg, wu, wd, mg, mu, md, vg, vu, vd,
+    dh_ref, a_ref, gu_ref, wd_ref, d0_hbm, gu1, d1, wg, wu, wd, mg, mu, md, vg, vu, vd,
     out_g, out_u, out_d, mb_g, mb_u, mb_d, vb_g, vb_u, vb_d,
-    dgu_ref, acc, all_g, all_u, all_d, own_gu, own_d, gbuf, dbuf, wb_g, wb_d, sq_send, sq_all, in_sem, sq_s, sq_r, ag_s, ag_r, put_sem, *ring_refs,
+    dgu_ref, acc, all_g, all_u, all_d, own_gu, own_d, gbuf, dbuf, wb_g, wb_d, sq_send, sq_all, in_sem, sq_s, sq_r, ag_s, ag_r, put_sem, direct, direct_s, direct_r, *ring_refs,
 ):
     i = pl.program_id(0)
     me = lax.axis_index("dp")
@@ -372,15 +345,14 @@
     my_g = pl.ds(pl.multiple_of(me * rg, rg), rg)
     my_d = pl.ds(pl.multiple_of(me * rd, rd), rd)
     width = gu_ref.shape[1]
-    early = gu1_early.shape[1]
     blocks = wg.shape[2] // LANES
+    last = pl.ds(2 * LANES * (blocks - 1), 2 * LANES)
     rings = [Ring(n, own_d, *ring_refs[:3])]
     for k, ((first, wide), _) in enumerate(groups):
         rings.append(Ring(n, own_gu.at[:, pl.ds(first * 2 * LANES, wide * 2 * LANES)], *ring_refs[3 * k + 3 : 3 * k + 6]))
     load = pltpu.make_async_copy(d0_hbm, own_d, in_sem.at[0])
     loads = [
-        pltpu.make_async_copy(gu1_early, gbuf.at[1, :, pl.ds(0, early)], in_sem.at[12]),
-        pltpu.make_async_copy(gu1, gbuf.at[1, :, pl.ds(early, gbuf.shape[2] - early)], in_sem.at[1]),
+        pltpu.make_async_copy(gu1, gbuf.at[1], in_sem.at[1]),
         pltpu.make_async_copy(d1, dbuf.at[1], in_sem.at[2]),
         pltpu.make_async_copy(mg, mb_g, in_sem.at[3]),
         pltpu.make_async_copy(mu, mb_u, in_sem.at[4]),
@@ -417,12 +389,28 @@
 
     @pl.when(i == steps - 1)
     def _():
+        straight = []
+        for k in range(1, n):
+            to = lax.rem(me + k, n)
+            straight.append(
+                pltpu.make_async_remote_copy(
+                    src_ref=own_gu.at[pl.ds(pl.multiple_of(to * rg, rg), rg), last],
+                    dst_ref=direct.at[k - 1],
+                    send_sem=direct_s.at[k - 1],
+                    recv_sem=direct_r.at[k - 1],
+                    device_id={"dp": to},
+                    device_id_type=MESH,
+                )
+            )
         for c in loads:
             c.wait()
-        for k, (_, at) in enumerate(groups):
-            if at >= steps:
-                rings[k + 1].start()
+        for c in straight:
+            c.start()
         rest_of_plan(todo, rings, steps)
+        for c in straight:
+            c.wait_recv()
+        own_terms = own_gu[my_g, last].astype(F32)
+        gbuf[0, :, last] = (own_terms + jnp.sum(direct[...].astype(F32), 0)).astype(BF)
         rings[0].finish(dbuf.at[0])
         for k, ((first, wide), _) in enumerate(groups):
             rings[k + 1].finish(gbuf.at[0, :, pl.ds(first * 2 * LANES, wide * 2 * LANES)])
@@ -513,7 +501,7 @@
                         if hop < streams[s][2]:
                             sending(layer, down, s, hop + 1).start()
                         put(layer, down, s, hop).start()
-        for c in to_all:
+        for c in to_all + straight:
             c.wait_send()
         for layer, down in units:
             for s in range(4):
@@ -587,53 +575,55 @@
             pl.BlockSpec((1, 2 * LANES, d), lambda i: (layer, i // 2, 0)),
         ]
         columns = lambda r: pl.BlockSpec((r, 2 * LANES), lambda i: (0, i))
-        early = 3
-        todo = plan(hops, [(0, us(rd, d // 2)), (early, us(rg, early * LANES))], blocks, 1.7)
-        dwgu1, sum_d1, sum_early = pl.pallas_call(
-            functools.partial(gu_kernel, n, blocks, todo, early),
+        dwgu1, sum_d1 = pl.pallas_call(
+            functools.partial(gu_kernel, n, blocks, plan(hops, [(0, us(rd, d // 2))], blocks, 1.8)),
             grid=(blocks,),
             in_specs=[once(tokens, d), columns(tokens), ANY],
-            out_specs=[columns(d), whole(rd, d), whole(rg, 2 * LANES * early)],
-            out_shape=[array((d, 2 * ff), BF), array((rd, d), BF), array((rg, 2 * LANES * early), BF)],
-            scratch_shapes=[vm((ff, d), BF), sem(()), vm((d, 2 * LANES * early), BF)] + ring(rd, d) + ring(rg, 2 * LANES * early),
+            out_specs=[columns(d), whole(rd, d)],
+            out_shape=[array((d, 2 * ff), BF), array((rd, d), BF)],
+            scratch_shapes=[vm((ff, d), BF), sem(())] + ring(rd, d),
             compiler_params=params(0),
             cost_estimate=pl.CostEstimate(flops=2 * mm, bytes_accessed=30 << 20, transcendentals=0),
             name="gu1",
         )(a1, dgu1, dwd1)
 
+        cut = blocks // 2 * 2 * LANES
+        parts = ((0, cut), (cut, 2 * ff - cut))
+        todo = plan(hops, [(0, us(rg, w // 2)) for _, w in parts], steps, 3.6)
         dh1, dwd0, sum_gu1 = pl.pallas_call(
-            functools.partial(mid_kernel, n, steps, plan(hops, [(0, us(rg, ff - early * LANES))], steps, 3.5)),
+            functools.partial(mid_kernel, n, steps, todo, parts),
             grid=(steps,),
             in_specs=[rows(d), rows(d), rows(2 * ff), rows(ff), ANY, ANY, ANY],
-            out_specs=[rows(d), whole(ff, d), whole(rg, 2 * ff - 2 * LANES * early)],
-            out_shape=[array((tokens, d), BF), array((ff, d), BF), array((rg, 2 * ff - 2 * LANES * early), BF)],
+            out_specs=[rows(d), whole(ff, d), whole(rg, 2 * ff)],
+            out_shape=[array((tokens, d), BF), array((ff, d), BF), array((rg, 2 * ff), BF)],
             scratch_shapes=[vm((d, 2 * ff), BF), vm((ff, d), F32), sem((2 * blocks,))]
-            + [vm((d, 2 * ff - 2 * LANES * early), BF), sem(())]
-            + ring(rg, 2 * ff - 2 * LANES * early),
+            + [vm((d, 2 * ff), BF), sem(())]
+            + [r for _, w in parts for r in ring(rg, w)],
             compiler_params=params(1),
             cost_estimate=pl.CostEstimate(flops=3 * mm, bytes_accessed=50 << 20, transcendentals=0),
             name="mid",
         )(h1, dy, dgu1, s0, wg, wu, dwgu1)
 
-        groups = [(k, min(4, blocks - k)) for k in range(0, blocks, 4)]
+        groups = [(k, min(4, blocks - 1 - k)) for k in range(0, blocks - 1, 4)]
         ready = [min(2 * -(-(f + w) // 2), pieces) for f, w in groups]
         todo = plan(hops, [(0, us(rd, d // 2))] + [(at, us(rg, w * LANES)) for at, (_, w) in zip(ready, groups)], pieces, 2.8)
         outs = pl.pallas_call(
             functools.partial(end_kernel, n, pieces, todo, list(zip(groups, ready)), float(wg.size + wu.size + wd.size)),
             grid=(pieces,),
-            in_specs=of_chunk(0) + [ANY] * 13,
+            in_specs=of_chunk(0) + [ANY] * 12,
             out_specs=[pl.BlockSpec(memory_space=pltpu.VMEM)] * 9,
             out_shape=[vm(t.shape, BF) for t in (wg, wu, wd)] + [vm(t.shape, F32) for t in (mg, mu, md, vg, vu, vd)],
             scratch_shapes=[
                 vm((tokens // 2, 4 * LANES), BF), vm((d, 4 * LANES), F32), vm(wg.shape, BF), vm(wu.shape, BF), vm(wd.shape, BF),
                 vm((d, 2 * ff), BF), vm((ff, d), BF), vm((2, rg, 2 * ff), BF), vm((2, rd, d), BF),
                 vm((2, *mg.shape), BF), vm(md.shape, BF), vm((8, LANES), F32), vm((n - 1, 8, LANES), F32),
-                sem((13,)), sem((n - 1,)), sem((n - 1,)), sem((4, 4, hops[0])), sem((4, 4, hops[0])), sem((4, 4, hops[0] + 1)),
+                sem((12,)), sem((n - 1,)), sem((n - 1,)), sem((4, 4, hops[0])), sem((4, 4, hops[0])), sem((4, 4, hops[0] + 1)),
+                vm((n - 1, rg, 2 * LANES), BF), sem((n - 1,)), sem((n - 1,)),
             ] + ring(rd, d) + [r for _, w in groups for r in ring(rg, w * 2 * LANES)],
             compiler_params=params(2, 48),
             cost_estimate=pl.CostEstimate(flops=2 * mm, bytes_accessed=30 << 20, transcendentals=0),
             name="end",
-        )(dh1, a0, gu0, wd, dwd0, sum_early, sum_gu1, sum_d1, wg, wu, wd, mg, mu, md, vg, vu, vd)
+        )(dh1, a0, gu0, wd, dwd0, sum_gu1, sum_d1, wg, wu, wd, mg, mu, md, vg, vu, vd)
         return tuple(
             pl.pallas_call(
                 store_kernel,

time: 278 us -> 279 us (level)
    pallas_call x1, Pallas kernels: 144 us -> 147 us  [step(): pl.pallas_call(functools.partial(end_kernel, n, pieces, todo, list(zip(gr...]
where the time goes in v6:
time: 279 us
  Pallas kernels  278 us (100%)
    pallas_call x1, Pallas kernels, step(): pl.pallas_call(functools.partial(end_kernel, n, pieces, todo, list(zip(gr...  147 us
    pallas_call x1, Pallas kernels, step(): pl.pallas_call(top_kernel, grid=(steps,), in_specs=[rows(d), rows(d), ANY...  59.2 us
    pallas_call x1, Pallas kernels, step(): pl.pallas_call(functools.partial(mid_kernel, n, steps, todo, parts), grid...  36.6 us
    pallas_call x1, Pallas kernels, step(): pl.pallas_call(functools.partial(gu_kernel, n, blocks, plan(hops, [(0, us...  30.4 us

profile of v6, /device:TPU:22, one launch (start us, length us, event | category | flops | bytes accessed | tf_op | source)
XLA Modules:
  0.0 278.8 jit_solution(12199670142494974114)
XLA Ops:
  0.6 59.2 %top.1 = (f32[4096,2816]{1,0:T(8,128)}, bf16[4096,1408]{1,0:T(8,128)(2,1)}, bf16[4096,512]{1,0:T(8,128)(2,1)}, bf16[4096,512]{1,0:T(8,128)(2,1)}, bf16[4096,512]...) custom-call(bf16[4096,512]{1,0:T(8,128)(2,1)} %bitcast.2, bf16[4096,512]{1,0:T(8,128)(2,1)} %bitcast.3, ...), custom_call_target="tpu_custom_call" | custom-call | flops 41339060224 | bytes 104857600 | tf_op jit(solution)/shard_map/top/pallas_call | solution.py:554
  59.8 30.4 %gu1.1 = (bf16[512,2816]{1,0:T(8,128)(2,1)}, bf16[176,512]{1,0:T(8,128)(2,1)}) custom-call(bf16[4096,512]{1,0:T(8,128)(2,1)} %get-tuple-element.33.a_ref, bf16[4096,2816]{1,0:T(8,128)(2,1)} %get-tuple-element.31.dgu_ref.dgu1_ref, bf16[1408,512]{1,0:T(8,128)(2,1)} %get-tuple-element.34.own_hbm), custom_call_target="tpu_custom_call" | custom-call | flops 11811160064 | bytes 31457280 | tf_op jit(solution)/shard_map/gu1/pallas_call | solution.py:578
  90.2 36.6 %mid.1 = (bf16[4096,512]{1,0:T(8,128)(2,1)}, bf16[1408,512]{1,0:T(8,128)(2,1)}, bf16[64,2816]{1,0:T(8,128)(2,1)}) custom-call(bf16[4096,512]{1,0:T(8,128)(2,1)} %get-tuple-element.30.h1_ref, bf16[4096,512]{1,0:T(8,128)(2,1)} %bitcast.4, bf16[4096,2816]{1,0:T(8,128)(2,1)} %get-tuple-element.31.dgu_ref.dgu1_ref, bf16[4096,1408]{1,0:T(8,128)(2,1)} %get-tuple-element.32.s0_ref, ...), custom_call_target="tpu_custom_call" | custom-call | flops 17716740096 | bytes 52428800 | tf_op jit(solution)/shard_map/mid/pallas_call | solution.py:593
  126.8 147.0 %end.1 = (bf16[2,512,1408]{2,1,0:T(8,128)(2,1)S(1)}, bf16[2,512,1408]{2,1,0:T(8,128)(2,1)S(1)}, bf16[2,1408,512]{2,1,0:T(8,128)(2,1)S(1)}, f32[2,64,1408]{2,1,0:...) custom-call(bf16[4096,512]{1,0:T(8,128)(2,1)} %get-tuple-element.36., ...), custom_call_target="tpu_custom_call" | custom-call | flops 11811160064 | bytes 31457280 | tf_op jit(solution)/shard_map/end/pallas_call | solution.py:610
  273.8 4.8 %store.1 = (bf16[2,512,1408]{2,1,0:T(8,128)(2,1)}, bf16[2,512,1408]{2,1,0:T(8,128)(2,1)}, bf16[2,1408,512]{2,1,0:T(8,128)(2,1)}, f32[2,64,1408]{2,1,0:T(8,128)},...) custom-call(bf16[2,512,1408]{2,1,0:T(8,128)(2,1)S(1)} %get-tuple-ele, ...), custom_call_target="tpu_custom_call" | custom-call | tf_op jit(solution)/shard_map/store/pallas_call | solution.py:628

commit v7 on v6

--- a/solution.py
+++ b/solution.py
@@ -96,7 +96,7 @@
 
 
 def plan(hops, rings, steps, step_us):
-    latency, free, waiting, out = 2.5, 0.0, [], []
+    latency, free, waiting, out = 3.0, 0.0, [], []
     far, near = hops
 
     def send(ring, group, hop, now):
@@ -124,11 +124,11 @@
     return out
 
 
-def run_plan(todo, rings, steps):
+def ticks(todo, rings, steps, per_step, k, only=lambda step: True):
     i = pl.program_id(0)
-    for step in range(1, steps):
-        now = [(r, pair) for at, r, pair in todo if at == step]
-        if now:
+    for step in range(steps):
+        now = [(r, pair) for at, r, pair in todo if at == step * per_step + k]
+        if now and only(step):
 
             @pl.when(i == step)
             def _(now=now):
@@ -142,7 +142,7 @@
             rings[r].handle(pair)
 
 
-def with_rings(n, steps, todo, own, load_sem, columns, refs, own_hbm, out):
+def with_rings(n, steps, per_step, todo, own, load_sem, columns, refs, own_hbm, out):
     i = pl.program_id(0)
     rings = [Ring(n, own.at[:, pl.ds(*c)], *refs[3 * k : 3 * k + 3]) for k, c in enumerate(columns)]
     load = pltpu.make_async_copy(own_hbm, own, load_sem)
@@ -155,16 +155,16 @@
         for ring in rings:
             ring.start()
 
-    run_plan(todo, rings, steps)
+    ticks(todo, rings, steps, per_step, 0)
 
     def close():
         @pl.when(i == steps - 1)
         def _():
-            rest_of_plan(todo, rings, steps)
+            rest_of_plan(todo, rings, steps * per_step)
             for ring, c in zip(rings, columns):
                 ring.finish(out.at[:, pl.ds(*c)])
 
-    return close
+    return lambda k: ticks(todo, rings, steps, per_step, k), close
 
 
 def load_all(copies):
@@ -252,10 +252,11 @@
         dwd_ref[...] = acc[...].astype(BF)
 
 
-def back_of_chunk(dh_ref, a_ref, gu_ref, wd_ref, dgu_ref, acc, blocks, keep):
+def back_of_chunk(dh_ref, a_ref, gu_ref, wd_ref, dgu_ref, acc, blocks, keep, tick):
     i = pl.program_id(0)
     tokens = gu_ref.shape[0]
     part = tokens // 4
+    whole_chunks = blocks // 2
 
     def run(c, half):
         wide = pl.ds(0, 2 * c * LANES)
@@ -278,6 +279,8 @@
                 acc[:, wide] += term
 
         for k in range(4):
+            if k > 0:
+                tick(k, lambda step: step % 2 == half and (step < 2 * whole_chunks) == (c == 2))
             hidden(k)
             if k > 0:
                 weights(k - 1)
@@ -285,7 +288,6 @@
         if half == 1:
             keep(i // 2, 2 * c * LANES, acc[:, wide].astype(BF))
 
-    whole_chunks = blocks // 2
     for half in (0, 1):
 
         @pl.when((i < 2 * whole_chunks) & (lax.rem(i, 2) == half))
@@ -300,7 +302,7 @@
 
 
 def gu_kernel(n, steps, todo, a_ref, dgu_ref, own_hbm, dw_ref, sum_ref, own, load_sem, *ring):
-    close = with_rings(n, steps, todo, own, load_sem, ((0, own.shape[1]),), ring, own_hbm, sum_ref)
+    _, close = with_rings(n, steps, 1, todo, own, load_sem, ((0, own.shape[1]),), ring, own_hbm, sum_ref)
     dw_ref[...] = dot(a_ref[...], dgu_ref[...], T_BY).astype(BF)
     close()
 
@@ -310,7 +312,7 @@
     wgu, acc, sem, own, load_sem, *ring,
 ):
     i = pl.program_id(0)
-    close = with_rings(n, steps, todo, own, load_sem, columns, ring, own_hbm, sum_ref)
+    tick, close = with_rings(n, steps, 2, todo, own, load_sem, columns, ring, own_hbm, sum_ref)
     load_all(gate_up_copies(wg.at[1], wu.at[1], wgu, sem, wg.shape[2] // LANES))
 
     @pl.when(i == 0)
@@ -323,6 +325,7 @@
         scale = rms_scale(h)
         back = scale * (da - h * (scale * scale * jnp.mean(da * h, -1, keepdims=True)))
         dh_ref[r, :] = (dy_ref[r, :].astype(F32) + back.astype(BF).astype(F32)).astype(BF)
+    tick(1)
     acc[...] += dot(s0_ref[...], dh_ref[...], T_BY)
 
     @pl.when(i == steps - 1)
@@ -374,7 +377,7 @@
         for c in loads:
             c.start()
 
-    run_plan(todo, rings, steps)
+    ticks(todo, rings, steps, 4, 0)
     for k, (_, at) in enumerate(groups):
         if at < steps:
 
@@ -385,7 +388,7 @@
     def keep(chunk, wide, dw):
         own_gu[:, pl.ds(pl.multiple_of(chunk * width, width), wide)] = dw
 
-    back_of_chunk(dh_ref, a_ref, gu_ref, wd_ref, dgu_ref, acc, blocks, keep)
+    back_of_chunk(dh_ref, a_ref, gu_ref, wd_ref, dgu_ref, acc, blocks, keep, lambda k, only: ticks(todo, rings, steps, 4, k, only))
 
     @pl.when(i == steps - 1)
     def _():
@@ -406,7 +409,7 @@
             c.wait()
         for c in straight:
             c.start()
-        rest_of_plan(todo, rings, steps)
+        rest_of_plan(todo, rings, 4 * steps)
         for c in straight:
             c.wait_recv()
         own_terms = own_gu[my_g, last].astype(F32)
@@ -589,7 +592,7 @@
 
         cut = blocks // 2 * 2 * LANES
         parts = ((0, cut), (cut, 2 * ff - cut))
-        todo = plan(hops, [(0, us(rg, w // 2)) for _, w in parts], steps, 3.6)
+        todo = plan(hops, [(0, us(rg, w // 2)) for _, w in parts], 2 * steps, 2.0)
         dh1, dwd0, sum_gu1 = pl.pallas_call(
             functools.partial(mid_kernel, n, steps, todo, parts),
             grid=(steps,),
@@ -606,7 +609,7 @@
 
         groups = [(k, min(4, blocks - 1 - k)) for k in range(0, blocks - 1, 4)]
         ready = [min(2 * -(-(f + w) // 2), pieces) for f, w in groups]
-        todo = plan(hops, [(0, us(rd, d // 2))] + [(at, us(rg, w * LANES)) for at, (_, w) in zip(ready, groups)], pieces, 2.8)
+        todo = plan(hops, [(0, us(rd, d // 2))] + [(4 * at, us(rg, w * LANES)) for at, (_, w) in zip(ready, groups)], 4 * pieces, 0.85)
         outs = pl.pallas_call(
             functools.partial(end_kernel, n, pieces, todo, list(zip(groups, ready)), float(wg.size + wu.size + wd.size)),
             grid=(pieces,),

time: 279 us -> 280 us (level)
  no operation moved by 1% of the time
where the time goes in v7:
time: 280 us; the launch traced here: 279 us
  Pallas kernels  278 us (99%)
    pallas_call x1, Pallas kernels, step(): pl.pallas_call(functools.partial(end_kernel, n, pieces, todo, list(zip(gr...  146 us
    pallas_call x1, Pallas kernels, step(): pl.pallas_call(top_kernel, grid=(steps,), in_specs=[rows(d), rows(d), ANY...  59.2 us
    pallas_call x1, Pallas kernels, step(): pl.pallas_call(functools.partial(mid_kernel, n, steps, todo, parts), grid...  37.6 us
    pallas_call x1, Pallas kernels, step(): pl.pallas_call(functools.partial(gu_kernel, n, blocks, plan(hops, [(0, us...  30.4 us

profile of v7, /device:TPU:22, one launch (start us, length us, event | category | flops | bytes accessed | tf_op | source)
XLA Modules:
  0.0 279.2 jit_solution(3738964360066750221)
XLA Ops:
  0.6 59.2 %top.1 = (f32[4096,2816]{1,0:T(8,128)}, bf16[4096,1408]{1,0:T(8,128)(2,1)}, bf16[4096,512]{1,0:T(8,128)(2,1)}, bf16[4096,512]{1,0:T(8,128)(2,1)}, bf16[4096,512]...) custom-call(bf16[4096,512]{1,0:T(8,128)(2,1)} %bitcast.2, bf16[4096,512]{1,0:T(8,128)(2,1)} %bitcast.3, ...), custom_call_target="tpu_custom_call" | custom-call | flops 41339060224 | bytes 104857600 | tf_op jit(solution)/shard_map/top/pallas_call | solution.py:557
  59.8 30.4 %gu1.1 = (bf16[512,2816]{1,0:T(8,128)(2,1)}, bf16[176,512]{1,0:T(8,128)(2,1)}) custom-call(bf16[4096,512]{1,0:T(8,128)(2,1)} %get-tuple-element.33.a_ref, bf16[4096,2816]{1,0:T(8,128)(2,1)} %get-tuple-element.31.dgu_ref.dgu1_ref, bf16[1408,512]{1,0:T(8,128)(2,1)} %get-tuple-element.34.own_hbm), custom_call_target="tpu_custom_call" | custom-call | flops 11811160064 | bytes 31457280 | tf_op jit(solution)/shard_map/gu1/pallas_call | solution.py:581
  90.2 37.6 %mid.1 = (bf16[4096,512]{1,0:T(8,128)(2,1)}, bf16[1408,512]{1,0:T(8,128)(2,1)}, bf16[64,2816]{1,0:T(8,128)(2,1)}) custom-call(bf16[4096,512]{1,0:T(8,128)(2,1)} %get-tuple-element.30.h1_ref, bf16[4096,512]{1,0:T(8,128)(2,1)} %bitcast.4, bf16[4096,2816]{1,0:T(8,128)(2,1)} %get-tuple-element.31.dgu_ref.dgu1_ref, bf16[4096,1408]{1,0:T(8,128)(2,1)} %get-tuple-element.32.s0_ref, ...), custom_call_target="tpu_custom_call" | custom-call | flops 17716740096 | bytes 52428800 | tf_op jit(solution)/shard_map/mid/pallas_call | solution.py:596
  127.8 146.4 %end.1 = (bf16[2,512,1408]{2,1,0:T(8,128)(2,1)S(1)}, bf16[2,512,1408]{2,1,0:T(8,128)(2,1)S(1)}, bf16[2,1408,512]{2,1,0:T(8,128)(2,1)S(1)}, f32[2,64,1408]{2,1,0:...) custom-call(bf16[4096,512]{1,0:T(8,128)(2,1)} %get-tuple-element.36., ...), custom_call_target="tpu_custom_call" | custom-call | flops 11811160064 | bytes 31457280 | tf_op jit(solution)/shard_map/end/pallas_call | solution.py:613
  274.2 4.8 %store.1 = (bf16[2,512,1408]{2,1,0:T(8,128)(2,1)}, bf16[2,512,1408]{2,1,0:T(8,128)(2,1)}, bf16[2,1408,512]{2,1,0:T(8,128)(2,1)}, f32[2,64,1408]{2,1,0:T(8,128)},...) custom-call(bf16[2,512,1408]{2,1,0:T(8,128)(2,1)S(1)} %get-tuple-ele, ...), custom_call_target="tpu_custom_call" | custom-call | tf_op jit(solution)/shard_map/store/pallas_call | solution.py:631
